TPU v7x, 512 devices: a whole 4x8x8 slice. The times are simulated.
512 devices in a mesh: lat: 16 (over y, core), lon: 32 (over z, x).
Axes of the slice: x: 4, y: 8, z: 8, core: 2. Of those that a mesh axis runs over, the one named last changes fastest.
Arguments:
- forcing: float32 [2560, 4096], P('lat', 'lon'), may hold values from -28 to 28
- search_direction: float32 [2560, 4096], P('lat', 'lon'), may hold values from -28 to 28
- ocean_depth: float32 [2560, 4096], P('lat', 'lon'), may hold values from 0.5 to 8
- land_mask: int32 [2560, 4096], P('lat', 'lon'), may hold values 0 or 1
- fold_map: int32 [4096], replicated, may hold values from 0 to 4095, as said below
Outputs:
- scaled_height: float32 [2560, 4096], P('lat', 'lon')
- residual: float32 [2560, 4096], P('lat', 'lon')
Inputs may be any that keep to these rules, and one draw needn't show every extreme that they name: `fold_map`: column j's partner across the fold is (c - j) mod 4096 for one c of 0 to 4095, so the map is its own inverse.
All inputs are finite; a program needn't handle non-finite values. No bound on the sum of `land_mask` on one device may be relied on, other than what follows from the above.
Results may differ from a plain program's by a relative error of at most 0.0003.
Values sent between devices are 32-bit elements; how exact they have to be, the bound alone decides.
No kernel may reach another device: no remote copies, remote signals or barrier semaphores. Data moves between devices by JAX's collectives and lax.ppermute only.
A program may use at most 64 MiB of HBM per device.

v0:
```python
import functools

import jax
import jax.numpy as jnp
from jax import lax
from jax.experimental import pallas as pl
from jax.experimental.pallas import tpu as pltpu
from jax.sharding import Mesh
from jax.sharding import PartitionSpec as P

STEPS = 8
REACH = 256
ROWS = 160
LANES = 128
EXT = ROWS + 32
EDGE = 9
BLK = 40
LON = ("lon_0", "lon_1")
VECTORS = 2 * STEPS + 1
F32 = jnp.float32


def lanes_of(rows):
    return lax.broadcasted_iota(jnp.int32, (rows, LANES), 1)


def shift_east(a, b, lane):
    ra, rb = pltpu.roll(a, 1, 1), pltpu.roll(b, 1, 1)
    first = lane == 0
    return jnp.where(first, rb, ra), jnp.where(first, ra, rb)


def shift_west(a, b, lane):
    ra, rb = pltpu.roll(a, LANES - 1, 1), pltpu.roll(b, LANES - 1, 1)
    last = lane == LANES - 1
    return jnp.where(last, rb, ra), jnp.where(last, ra, rb)


def pack_kernel(f_ref, p_ref, d_ref, m_ref, x_ref, east_ref, west_ref):
    for g in range(ROWS // 8):
        rows = pl.ds(8 * g, 8)
        flag = m_ref[rows, :].astype(F32)
        x_ref[0, rows, :] = d_ref[rows, :] * flag
        x_ref[1, rows, :] = f_ref[rows, :] * flag
        x_ref[2, rows, :] = p_ref[rows, :] * flag
    lane = lanes_of(8)
    for v in range(BLK // 8):
        east = jnp.zeros((8, LANES), F32)
        west = jnp.zeros((8, LANES), F32)
        for q in range(3):
            for blk in range(4):
                at = EDGE * (4 * q + blk)
                tile = x_ref[q, pl.ds(BLK * blk + 8 * v, 8), :]
                inside = (lane >= at) & (lane < at + EDGE)
                west = jnp.where(inside, pltpu.roll(tile, at, 1) if at else tile, west)
                east = jnp.where(inside, pltpu.roll(tile, (at + EDGE) % LANES, 1), east)
        east_ref[pl.ds(8 * v, 8), :] = east
        west_ref[pl.ds(8 * v, 8), :] = west
    for slot, (q, row) in enumerate(((0, ROWS - 8), (1, ROWS - 8), (2, ROWS - 8), (0, ROWS - 16))):
        tile = x_ref[q, pl.ds(row, 8), :]
        east_ref[pl.ds(BLK + 8 * slot, 8), :] = tile
        west_ref[pl.ds(BLK + 8 * slot, 8), :] = tile


def unpack_halo(from_west, from_east, q, blk, v, lane):
    at = EDGE * (4 * q + blk)
    right = from_east[pl.ds(8 * v, 8), :]
    left = from_west[pl.ds(8 * v, 8), :]
    right = pltpu.roll(right, LANES - at, 1) if at else right
    left = pltpu.roll(left, (2 * LANES - EDGE - at) % LANES, 1)
    return jnp.where(lane < EDGE, right, jnp.where(lane >= LANES - EDGE, left, 0.0))


def turn_kernel(r_ref, x_ref, fw_ref, fe_ref, north_ref, south_ref, fold_ref, next_ref, t1_ref, t2_ref):
    lane = lanes_of(8)
    top, low = ROWS // 8 - 1, 0
    for slot, (q, g) in enumerate(((0, top), (1, top), (2, top), (0, top - 1))):
        north_ref[pl.ds(8 * slot, 8), :] = x_ref[q, pl.ds(8 * g, 8), :]
        blk, v = 8 * g // BLK, (8 * g % BLK) // 8
        north_ref[pl.ds(32 + 8 * slot, 8), :] = unpack_halo(fw_ref, fe_ref, q, blk, v, lane)
    for slot, (q, g) in enumerate(((0, low), (1, low), (2, low), (0, low + 1))):
        south_ref[pl.ds(8 * slot, 8), :] = x_ref[q, pl.ds(8 * g, 8), :]
        blk, v = 8 * g // BLK, (8 * g % BLK) // 8
        south_ref[pl.ds(32 + 8 * slot, 8), :] = unpack_halo(fw_ref, fe_ref, q, blk, v, lane)
    reach = r_ref[0]
    along = reach - lane
    pick = along & (LANES - 1)
    place_a = along
    place_b = jnp.where(lane < EDGE, along - LANES, along + LANES)
    halo = (lane < EDGE) | (lane >= LANES - EDGE)
    for slot in range(4):
        rows = pl.ds(8 * slot, 8)
        own = jnp.take_along_axis(north_ref[rows, :], pick, axis=1, mode="promise_in_bounds")
        west = jnp.take_along_axis(fw_ref[pl.ds(BLK + 8 * slot, 8), :], pick, axis=1, mode="promise_in_bounds")
        east = jnp.take_along_axis(fe_ref[pl.ds(BLK + 8 * slot, 8), :], pick, axis=1, mode="promise_in_bounds")
        for part, place in ((0, place_a), (32, place_b)):
            near = jnp.where(place < 0, west, jnp.where(place < LANES, own, east))
            near = jnp.where(place < 2 * LANES, near, 0.0)
            far = jnp.where(place >= 2 * LANES, own, 0.0)
            if part:
                near = jnp.where(halo, near, 0.0)
                far = jnp.where(halo, far, 0.0)
            t1_ref[pl.ds(part + 8 * slot, 8), :] = near
            t2_ref[pl.ds(part + 8 * slot, 8), :] = far
    for g in range(8):
        for m in range(8):
            fold_ref[pl.ds(8 * g + m, 1), :] = t1_ref[pl.ds(8 * g + 7 - m, 1), :]
            next_ref[pl.ds(8 * g + m, 1), :] = t2_ref[pl.ds(8 * g + 7 - m, 1), :]


GROUPS = ROWS // 8 + 2


def basis_kernel(x_ref, fw_ref, fe_ref, fs_ref, fn_ref, ff_ref, basis_ref, sums_ref,
                 depth, side, inv, coef, acc):
    lane = lanes_of(8)
    zero = jnp.zeros((8, LANES), F32)
    targets = (
        lambda t: depth.at[t],
        lambda t: (basis_ref if t == 0 else side).at[STEPS + 1],
        lambda t: (basis_ref if t == 0 else side).at[0],
    )
    for q in range(3):
        own, rim = targets[q](0), targets[q](1)
        for g in range(ROWS // 8):
            own[pl.ds(16 + 8 * g, 8), :] = x_ref[q, pl.ds(8 * g, 8), :]
            blk, v = 8 * g // BLK, (8 * g % BLK) // 8
            rim[pl.ds(16 + 8 * g, 8), :] = unpack_halo(fw_ref, fe_ref, q, blk, v, lane)
        for t, ref in ((0, own), (1, rim)):
            at = 32 * t + 8 * q
            ref[pl.ds(8, 8), :] = fs_ref[pl.ds(at, 8), :]
            ref[pl.ds(EXT - 16, 8), :] = fn_ref[pl.ds(at, 8), :] + ff_ref[pl.ds(at, 8), :]
            if q == 0:
                at = 32 * t + 24
                ref[pl.ds(0, 8), :] = fs_ref[pl.ds(at, 8), :]
                ref[pl.ds(EXT - 8, 8), :] = fn_ref[pl.ds(at, 8), :] + ff_ref[pl.ds(at, 8), :]
            else:
                ref[pl.ds(0, 8), :] = zero
                ref[pl.ds(EXT - 8, 8), :] = zero
    for k in list(range(1, STEPS + 1)) + list(range(STEPS + 2, VECTORS)):
        for ref in (basis_ref, side):
            ref[k, pl.ds(0, 8), :] = zero
            ref[k, pl.ds(EXT - 8, 8), :] = zero
    for t in range(2):
        inv[t, pl.ds(0, 8), :] = zero
        inv[t, pl.ds(EXT - 8, 8), :] = zero

    def root_of(g, carry):
        at = 8 + 8 * g
        vert, mid, wet_mid, deep = [], [], [], []
        for t in range(2):
            down = depth[t, pl.ds(at - 1, 8), :]
            here = depth[t, pl.ds(at, 8), :]
            up = depth[t, pl.ds(at + 1, 8), :]
            wet = jnp.where(here > 0.0, 1.0, 0.0)
            wets = jnp.where(down > 0.0, 1.0, 0.0) + jnp.where(up > 0.0, 1.0, 0.0)
            vert.append((down + up, wets))
            mid.append((here + 0.5 * (down + up), wet + 0.5 * wets))
            deep.append(here)
            wet_mid.append(wet)
        sums = []
        for c in range(2):
            ea, eb = shift_east(mid[0][c], mid[1][c], lane)
            wa, wb = shift_west(mid[0][c], mid[1][c], lane)
            sums.append((vert[0][c] + (ea + wa), vert[1][c] + (eb + wb)))
        for t in range(2):
            links = 0.5 * (deep[t] * sums[1][t] + sums[0][t])
            diagonal = wet_mid[t] * (deep[t] / (REACH * REACH) + links) + (1.0 - wet_mid[t])
            inv[t, pl.ds(at, 8), :] = lax.rsqrt(diagonal) * wet_mid[t]
        return carry

    lax.fori_loop(0, GROUPS, root_of, 0, unroll=2)

    def coefs_of(g, carry):
        at = 8 + 8 * g
        d = [[depth[t, pl.ds(at + s, 8), :] for s in (-1, 0, 1)] for t in range(2)]
        r = [[inv[t, pl.ds(at + s, 8), :] for s in (-1, 0, 1)] for t in range(2)]
        de, re = shift_east(d[0][1], d[1][1], lane), shift_east(r[0][1], r[1][1], lane)
        dw, rw = shift_west(d[0][1], d[1][1], lane), shift_west(r[0][1], r[1][1], lane)
        for t in range(2):
            for base, (dc, rc) in enumerate(((d[t][1], r[t][1]), (de[t], re[t]), (dw[t], rw[t]))):
                for s in range(3):
                    if base == 0 and s == 1:
                        continue
                    whole = base == 0 or s == 1
                    c = (dc + d[t][s]) * (rc * r[t][s])
                    coef[t, 3 * base + s, pl.ds(at, 8), :] = c * (-1.0 if whole else -0.5)
        return carry

    lax.fori_loop(0, GROUPS, coefs_of, 0, unroll=2)

    def twice_applied(k, at, tiles, weights):
        parts = []
        for t in range(2):
            ref = basis_ref if t == 0 else side
            down, here, up = (ref[k, pl.ds(at + s, 8), :] for s in (-1, 0, 1))
            w = weights[t]
            straight = w[0] * down + w[2] * up
            toward_w = (w[3] * down + w[5] * up) + w[4] * here
            toward_e = (w[6] * down + w[8] * up) + w[7] * here
            parts.append((straight, toward_w, toward_e, here))
        wa, wb = shift_west(parts[0][1], parts[1][1], lane)
        ea, eb = shift_east(parts[0][2], parts[1][2], lane)
        return ((parts[0][0] + (wa + ea), parts[1][0] + (wb + eb))[:tiles], parts[0][3])

    def weights_at(at):
        return [[None if i == 1 else coef[t, i, pl.ds(at, 8), :] for i in range(9)] for t in range(2)]

    def step(k, first, last):
        total = [zero] * 6
        tiles = 1 if last else 2
        for g in range(1, GROUPS - 1) if last else range(GROUPS):
            at = 8 + 8 * g
            w = weights_at(at)
            now, new = [], []
            for base in ((0,) if last else (0, STEPS + 1)):
                out, here = twice_applied(base + k, at, tiles, w)
                now.append(here)
                for t in range(tiles):
                    ref = basis_ref if t == 0 else side
                    value = 0.5 * out[t] if first else out[t] - ref[base + k - 1, pl.ds(at, 8), :]
                    ref[base + k + 1, pl.ds(at, 8), :] = value
                    if t == 0:
                        new.append(value)
            if last:
                now.append(basis_ref[STEPS + 1 + k, pl.ds(at, 8), :])
            if 1 <= g <= ROWS // 8:
                p, r = now
                total[0] += p * p
                total[1] += p * new[0]
                total[2] += r * r
                total[3] += new[0] * new[0] if last else r * new[1]
                total[4] += p * r
                total[5] += new[0] * r
        for i in range(6):
            acc[k, i, :, :] = total[i]
        acc[k, 6, :, :] = zero
        acc[k, 7, :, :] = zero

    step(0, True, False)

    def middle(k, carry):
        step(k, False, False)
        return carry

    lax.fori_loop(1, STEPS - 1, middle, 0)
    step(STEPS - 1, False, True)

    flat = jnp.sum(acc[...].reshape(8 * STEPS, 8, LANES), axis=1)
    flat = jnp.concatenate([flat, jnp.zeros_like(flat)], axis=0)
    row = lax.dot_general(
        jnp.ones((8, LANES), F32), flat, (((1,), (1,)), ((), ())),
        precision=lax.Precision.HIGHEST, preferred_element_type=F32,
    )
    for g in range(sums_ref.shape[0] // 8):
        sums_ref[pl.ds(8 * g, 8), :] = row


def middle_kernel(in_ref, out_ref):
    out_ref[...] = jnp.broadcast_to(jnp.sum(in_ref[...], axis=0, keepdims=True), out_ref.shape)


def final_kernel(sum_ref, basis_ref, height_ref, residual_ref):
    held = jnp.broadcast_to(jnp.sum(sum_ref[...], axis=0, keepdims=True), (8, LANES))
    row = lax.broadcasted_iota(jnp.int32, (24, LANES), 0)
    col = lax.broadcasted_iota(jnp.int32, (24, LANES), 1)
    half = STEPS + 1
    i = jnp.where(row < half, row, row - half)
    j = jnp.where(col < half, col, col - half)
    row_p, col_p = row < half, col < half
    inside = (row < VECTORS) & (col < VECTORS)
    total, apart = i + j, jnp.abs(i - j)
    even = (total & 1) == 0
    slot = jnp.where(row_p & col_p, 0, jnp.where(row_p | col_p, 4, 2))
    slot = slot + jnp.where(even, 0, 1)

    def gathered(index):
        index = jnp.where(inside, index, 6)
        parts = [
            jnp.take_along_axis(held, index[8 * g : 8 * g + 8], axis=1, mode="promise_in_bounds")
            for g in range(3)
        ]
        return jnp.concatenate(parts, axis=0)

    high = jnp.where(total == 2 * STEPS, 8 * (STEPS - 1) + 3, 8 * (total >> 1) + slot)
    gram = gathered(high) + gathered(8 * (apart >> 1) + slot) - gathered(slot)

    lead_r = (row == 0) | (row == half)
    tail_r = (row == STEPS) | (row >= VECTORS - 1)
    same = (row_p == col_p) & inside & ~tail_r
    h_turned = jnp.where(same & (row == col), 1.0, 0.0)
    h_turned = h_turned + jnp.where(same & (col == row + 1), jnp.where(lead_r, 1.0, 0.5), 0.0)
    h_turned = h_turned + jnp.where(same & (col == row - 1) & ~lead_r, 0.5, 0.0)
    keep = jnp.where(tail_r, 0.0, 1.0)
    to_next = jnp.where(tail_r, 0.0, jnp.where(lead_r, 1.0, 0.5))
    to_last = jnp.where(tail_r | lead_r, 0.0, 0.5)

    def as_row(matrix, column):
        return jnp.sum(matrix * column, axis=0, keepdims=True)

    def dot(a, b):
        return jnp.sum(a * b, axis=1, keepdims=True)

    xc = jnp.zeros((24, LANES), F32)
    pc, rc = jnp.where(row == 0, 1.0, 0.0), jnp.where(row == half, 1.0, 0.0)
    pr, rr_row = jnp.where(col[:1] == 0, 1.0, 0.0), jnp.where(col[:1] == half, 1.0, 0.0)
    norm = dot(as_row(gram, rc), rr_row)
    for _ in range(STEPS):
        q_row = as_row(h_turned, pc)
        q_col = keep * pc + pltpu.roll(to_next * pc, 1, 0) + pltpu.roll(to_last * pc, 23, 0)
        t = norm / dot(as_row(gram, pc), q_row)
        xc = xc + t * pc
        rc = rc - t * q_col
        rr_row = rr_row - t * q_row
        new = dot(as_row(gram, rc), rr_row)
        ratio = new / norm
        pc = rc + ratio * pc
        norm = new
    xs = [jnp.broadcast_to(xc[k : k + 1, :], (8, LANES)) for k in range(VECTORS)]
    rs = [jnp.broadcast_to(rc[k : k + 1, :], (8, LANES)) for k in range(VECTORS)]
    for g in range(ROWS // 8):
        first = second = None
        for k in range(VECTORS):
            tile = basis_ref[k, pl.ds(16 + 8 * g, 8), :]
            first = xs[k] * tile if first is None else first + xs[k] * tile
            second = rs[k] * tile if second is None else second + rs[k] * tile
        height_ref[pl.ds(8 * g, 8), :] = first
        residual_ref[pl.ds(8 * g, 8), :] = second


def shape(*dims):
    return jax.ShapeDtypeStruct(dims, F32)


def per_device(forcing, search_direction, ocean_depth, land_mask, fold_map):
    lat_count, lon_count = lax.axis_size("lat"), lax.axis_size(LON)
    call = functools.partial(pl.pallas_call, compiler_params=pltpu.CompilerParams())
    fields, to_east, to_west = call(
        pack_kernel, name="pack",
        out_shape=(shape(3, ROWS, LANES), shape(BLK + 32, LANES), shape(BLK + 32, LANES)),
    )(forcing, search_direction, ocean_depth, land_mask)
    up = [(i, (i + 1) % lon_count) for i in range(lon_count)]
    from_west = lax.ppermute(to_east, LON, up)
    from_east = lax.ppermute(to_west, LON, [(b, a) for a, b in up])

    pivot = fold_map[0]
    offset = (pivot - 8) % (2 * LANES)
    reach = offset + 8
    pairing = ((pivot - reach) // (2 * LANES)) % (lon_count // 2)
    split = (reach + EDGE >= 2 * LANES).astype(jnp.int32)
    to_north, to_south, across, across_next = call(
        turn_kernel, name="turn",
        in_specs=[pl.BlockSpec(memory_space=pltpu.SMEM)] + [pl.BlockSpec(memory_space=pltpu.VMEM)] * 3,
        out_shape=(shape(64, LANES),) * 4,
        scratch_shapes=[pltpu.VMEM((64, LANES), F32)] * 2,
    )(reach.reshape(1), fields, from_west, from_east)

    from_south = lax.ppermute(to_north, "lat", [(i, i + 1) for i in range(lat_count - 1)])
    from_north = lax.ppermute(to_south, "lat", [(i + 1, i) for i in range(lat_count - 1)])
    top = (lat_count - 1) * lon_count

    def over_fold(value, pairing):
        pairs = [(top + i, top + (2 * pairing - i) % lon_count) for i in range(lon_count)]
        return lax.ppermute(value, ("lat",) + LON, pairs)

    def branch(index):
        if index % 2 == 0:
            return lambda near, far: over_fold(near, index // 2)
        return lambda near, far: over_fold(near, index // 2) + over_fold(far, index // 2 + 1)

    folded = lax.switch(2 * pairing + split, [branch(i) for i in range(lon_count)], across, across_next)

    basis, sums = call(
        basis_kernel, name="basis",
        out_shape=(shape(VECTORS, EXT, LANES), shape(lon_count, LANES)),
        scratch_shapes=[
            pltpu.VMEM((2, EXT, LANES), F32),
            pltpu.VMEM((VECTORS, EXT, LANES), F32),
            pltpu.VMEM((2, EXT, LANES), F32),
            pltpu.VMEM((2, 9, EXT, LANES), F32),
            pltpu.VMEM((STEPS, 8, 8, LANES), F32),
        ],
    )(fields, from_west, from_east, from_south, from_north, folded)
    sums = lax.all_to_all(sums, LON, split_axis=0, concat_axis=0, tiled=True)
    sums = call(middle_kernel, name="middle", out_shape=shape(lat_count, LANES))(sums)
    sums = lax.all_to_all(sums, "lat", split_axis=0, concat_axis=0, tiled=True)
    return call(
        final_kernel, name="final", out_shape=(shape(ROWS, LANES), shape(ROWS, LANES)),
    )(sums, basis)


def solution(mesh):
    lon = mesh.shape["lon"]
    split = Mesh(mesh.devices.reshape(mesh.shape["lat"], lon // 4, 4), ("lat", "lon_0", "lon_1"))
    return jax.shard_map(
        per_device,
        mesh=split,
        in_specs=(P("lat", LON), P("lat", LON), P("lat", LON), P("lat", LON), P()),
        out_specs=(P("lat", LON), P("lat", LON)),
        check_vma=False,
    )
```

profile of v0, /device:TPU:1, one launch (start us, length us, event | category | flops | bytes accessed | tf_op | source)
XLA Modules:
  0.0 78.2 jit_solution(5757035358562257481)
XLA Ops:
  0.6 1.8 %pack.1 = (f32[3,160,128]{2,1,0:T(8,128)}, f32[72,128]{1,0:T(8,128)}, f32[72,128]{1,0:T(8,128)}) custom-call(f32[160,128]{1,0:T(8,128)} %f_ref.1, f32[160,128]{1,0:T(8,128)} %p_ref.1, f32[160,128]{1,0:T(8,128)} %d_ref.1, s32[160,128]{1,0:T(8,128)} %m_ref.1), custom_call_target="tpu_custom_call" | custom-call | tf_op jit(solution)/shard_map/pack/pallas_call | solution.py:338
  2.5 3.9 %collective-permute-start.48 = (f32[72,128]{1,0:T(8,128)}, f32[72,128]{1,0:T(8,128)S(1)}, u32[]{:S(2)}, u32[]{:S(2)}) collective-permute-start(f32[72,128]{1,0:T(8,128)} %get-tuple-element.157), channel_id=1, source_target_pairs={{0,1},{1,2},{2,3},{3,4},{4,5},{5,6},{6,7},{7,8},{8,9},{9,10},{10,1... | collective-permute-start | bytes 110600 | tf_op jit(solution)/shard_map/ppermute | solution.py:343
  6.4 11.7 %collective-permute-start.49 = (f32[72,128]{1,0:T(8,128)}, f32[72,128]{1,0:T(8,128)S(1)}, u32[]{:S(2)}, u32[]{:S(2)}) collective-permute-start(f32[72,128]{1,0:T(8,128)} %get-tuple-element.158), channel_id=1, source_target_pairs={{1,0},{2,1},{3,2},{4,3},{5,4},{6,5},{7,6},{8,7},{9,8},{10,9},{11,1... | collective-permute-start | bytes 110600 | tf_op jit(solution)/shard_map/ppermute | solution.py:344
  18.1 1.2 %slice.3 = s32[1]{0:T(128)} slice(s32[4096]{0:T(1024)} %param.41), slice={[0:1]} | slice | bytes 8 | tf_op jit(solution)/shard_map/slice | solution.py:346
  19.8 0.0 collective-permute-done.48.fw_ref
  19.9 0.0 copy-start
  19.9 0.0 collective-permute-done.49.fe_ref
  19.9 0.0 copy-start.1
  19.9 0.6 copy-done
  20.5 0.0 copy-done.1
  20.5 1.7 %turn.1 = (f32[64,128]{1,0:T(8,128)}, f32[64,128]{1,0:T(8,128)}, f32[64,128]{1,0:T(8,128)S(1)}, f32[64,128]{1,0:T(8,128)S(1)}) custom-call(s32[1]{0:T(128)} %bitcast.1.r_ref, f32[3,160,128]{2,1,0:T(8,128)} %get-tuple-element.156.x_ref, f32[72,128]{1,0:T(8,128)} %copy-done, f32[72,128]{1,0:T(8,128)} %copy-done.1), custom_call_target="tpu_custom_call" | custom-call | tf_op jit(solution)/shard_map/turn/pallas_call | solution.py:351
  22.2 4.1 %collective-permute-start.50 = (f32[64,128]{1,0:T(8,128)}, f32[64,128]{1,0:T(8,128)S(1)}, u32[]{:S(2)}, u32[]{:S(2)}) collective-permute-start(f32[64,128]{1,0:T(8,128)} %get-tuple-element.159), channel_id=1, source_target_pairs={{0,32},{32,64},{64,96},{96,128},{128,160},{160,192},{192,224},{224... | collective-permute-start | bytes 98312 | tf_op jit(solution)/shard_map/ppermute | solution.py:358
  26.4 1.9 %collective-permute-start.51 = (f32[64,128]{1,0:T(8,128)}, f32[64,128]{1,0:T(8,128)S(1)}, u32[]{:S(2)}, u32[]{:S(2)}) collective-permute-start(f32[64,128]{1,0:T(8,128)} %get-tuple-element.160), channel_id=1, source_target_pairs={{32,0},{64,32},{96,64},{128,96},{160,128},{192,160},{224,192},{256... | collective-permute-start | bytes 98312 | tf_op jit(solution)/shard_map/ppermute | solution.py:359
  28.9 1.3 %conditional.1 = (f32[64,128]{1,0:T(8,128)}) conditional(s32[]{:T(128)} %clamp.3, f32[64,128]{1,0:T(8,128)S(1)} %get-tuple-element.161, (f32[64,128]{1,0:T(8,128)S(1)}, f32[64,128]{1,0:T(8,128)S(1)}) %tuple.103, f32[64,128]{1,0:T(8,128)S(1)} %get-tuple-element.161, (f32[64,128]{1,0:T(8,128)S(1)}, ...), branch_computations={%region_0.1_spmd, %region_1.2_spmd, %region_2.3_spmd, %region_3.4_... | conditional | flops 8192 | bytes 360536 | solution.py:371
  29.0 1.3 %collective-permute-start.39 = (f32[64,128]{1,0:T(8,128)S(1)}, f32[64,128]{1,0:T(8,128)}, u32[]{:S(2)}, u32[]{:S(2)}) collective-permute-start(f32[64,128]{1,0:T(8,128)S(1)} %param.26), channel_id=1, source_target_pairs={{480,506},{481,505},{482,504},{483,503},{484,502},{485,501},{486,5... | collective-permute-start | bytes 98312 | tf_op jit(solution)/shard_map/cond/branch_26_fun/ppermute | solution.py:364
  30.2 0.0 collective-permute-done.39
  30.2 0.0 collective-permute-done.50.fs_ref
  30.2 0.0 copy-start.2
  30.2 1.6 %collective-permute-done.51.fn_ref = f32[64,128]{1,0:T(8,128)S(1)} collective-permute-done((f32[64,128]{1,0:T(8,128)}, f32[64,128]{1,0:T(8,128)S(1)}, u32[]{:S(2)}, u32[]{:S(2)}) %collective-permute-start.51) | collective-permute-done | bytes 32800 | tf_op jit(solution)/shard_map/ppermute | solution.py:359
  31.8 0.0 copy-done.2
  31.8 0.0 copy-start.3
  31.8 0.6 copy-done.3
  32.4 7.5 %basis.1 = (f32[17,192,128]{2,1,0:T(8,128)}, f32[32,128]{1,0:T(8,128)}) custom-call(f32[3,160,128]{2,1,0:T(8,128)} %get-tuple-element.156.x_ref, f32[72,128]{1,0:T(8,128)} %copy-done, f32[72,128]{1,0:T(8,128)} %copy-done.1, f32[64,128]{1,0:T(8,128)} %copy-done.2, f32[64,128]{1,0:T(8,128)} %copy-done.3, f32[64,128]{1,0:T(8,128)} %get-tuple-element.165.ff_ref), custom_call_target="tpu_custom_call" | custom-call | tf_op jit(solution)/shard_map/basis/pallas_call | solution.py:373
  39.9 16.1 %all_to_all.22 = f32[32,1,128]{2,1,0:T(1,128)} all-to-all(f32[32,1,128]{2,1,0:T(1,128)} %bitcast.13), channel_id=1, replica_groups=mesh['lat'=16,'lon_0'=8,'lon_1'=4] {'lon_0','lon_1'}, dimensions={0} | all-to-all | bytes 32768 | tf_op jit(solution)/shard_map/all_to_all | solution.py:384
  56.0 1.3 %middle.1 = f32[16,128]{1,0:T(8,128)} custom-call(f32[32,128]{1,0:T(8,128)} %bitcast.10), custom_call_target="tpu_custom_call" | custom-call | tf_op jit(solution)/shard_map/middle/pallas_call | solution.py:385
  57.3 17.1 %all_to_all.23 = f32[16,1,128]{2,1,0:T(1,128)} all-to-all(f32[16,1,128]{2,1,0:T(1,128)} %bitcast.12), channel_id=1, replica_groups=mesh['lat'=16,'lon_0'=8,'lon_1'=4] {'lat'}, dimensions={0} | all-to-all | bytes 16384 | tf_op jit(solution)/shard_map/all_to_all | solution.py:386
  74.4 3.8 %final.1 = (f32[160,128]{1,0:T(8,128)}, f32[160,128]{1,0:T(8,128)}) custom-call(f32[16,128]{1,0:T(8,128)} %bitcast.11, f32[17,192,128]{2,1,0:T(8,128)} %get-tuple-element.164.basis_ref), custom_call_target="tpu_custom_call" | custom-call | tf_op jit(solution)/shard_map/final/pallas_call | solution.py:387
Async XLA Ops:
  2.5 17.4 %collective-permute-start.48 = (f32[72,128]{1,0:T(8,128)}, f32[72,128]{1,0:T(8,128)S(1)}, u32[]{:S(2)}, u32[]{:S(2)}) collective-permute-start(f32[72,128]{1,0:T(8,128)} %get-tuple-element.157), channel_id=1, source_target_pairs={{0,1},{1,2},{2,3},{3,4},{4,5},{5,6},{6,7},{7,8},{8,9},{9,10},{10,1... | collective-permute-start | bytes 110600 | tf_op jit(solution)/shard_map/ppermute | solution.py:343
  6.4 13.5 %collective-permute-start.49 = (f32[72,128]{1,0:T(8,128)}, f32[72,128]{1,0:T(8,128)S(1)}, u32[]{:S(2)}, u32[]{:S(2)}) collective-permute-start(f32[72,128]{1,0:T(8,128)} %get-tuple-element.158), channel_id=1, source_target_pairs={{1,0},{2,1},{3,2},{4,3},{5,4},{6,5},{7,6},{8,7},{9,8},{10,9},{11,1... | collective-permute-start | bytes 110600 | tf_op jit(solution)/shard_map/ppermute | solution.py:344
  19.9 0.6 copy-start
  19.9 0.6 copy-start.1
  22.2 8.0 %collective-permute-start.50 = (f32[64,128]{1,0:T(8,128)}, f32[64,128]{1,0:T(8,128)S(1)}, u32[]{:S(2)}, u32[]{:S(2)}) collective-permute-start(f32[64,128]{1,0:T(8,128)} %get-tuple-element.159), channel_id=1, source_target_pairs={{0,32},{32,64},{64,96},{96,128},{128,160},{160,192},{192,224},{224... | collective-permute-start | bytes 98312 | tf_op jit(solution)/shard_map/ppermute | solution.py:358
  26.4 5.4 %collective-permute-start.51 = (f32[64,128]{1,0:T(8,128)}, f32[64,128]{1,0:T(8,128)S(1)}, u32[]{:S(2)}, u32[]{:S(2)}) collective-permute-start(f32[64,128]{1,0:T(8,128)} %get-tuple-element.160), channel_id=1, source_target_pairs={{32,0},{64,32},{96,64},{128,96},{160,128},{192,160},{224,192},{256... | collective-permute-start | bytes 98312 | tf_op jit(solution)/shard_map/ppermute | solution.py:359
  29.0 1.3 %collective-permute-start.39 = (f32[64,128]{1,0:T(8,128)S(1)}, f32[64,128]{1,0:T(8,128)}, u32[]{:S(2)}, u32[]{:S(2)}) collective-permute-start(f32[64,128]{1,0:T(8,128)S(1)} %param.26), channel_id=1, source_target_pairs={{480,506},{481,505},{482,504},{483,503},{484,502},{485,501},{486,5... | collective-permute-start | bytes 98312 | tf_op jit(solution)/shard_map/cond/branch_26_fun/ppermute | solution.py:364
  30.2 1.6 %copy-start.2 = (f32[64,128]{1,0:T(8,128)}, f32[64,128]{1,0:T(8,128)S(1)}, u32[]{:S(2)}) copy-start(f32[64,128]{1,0:T(8,128)S(1)} %collective-permute-done.50.fs_ref) | copy-start | bytes 98308
  31.8 0.6 copy-start.3
where the time goes:
time: 79.4 us; the launch traced here: 78.2 us
  blocking collectives  33.2 us (42%)
  starting transfers between devices  22.9 us (29%)
  Pallas kernels  16.2 us (20%)
  local copies, waits for them, and re-layouts  2.42 us (3%)
  between operations  1.88 us (2%)
  waiting for transfers between devices  1.6 us (2%)
    all_to_all x1, blocking collectives, per_device(): sums = lax.all_to_all(sums, 'lat', split_axis=0, concat_axis=0, tiled=True)  17.1 us
    all_to_all x1, blocking collectives, per_device(): sums = lax.all_to_all(sums, LON, split_axis=0, concat_axis=0, tiled=True)  16.1 us
    ppermute x1, starting transfers between devices, per_device(): from_east = lax.ppermute(to_west, LON, [(b, a) for a, b in up])  11.7 us
    pallas_call x1, Pallas kernels, per_device(): call(basis_kernel, name='basis', out_shape=(shape(VECTORS, EXT, LANES), s...  7.52 us
    ppermute x1, starting transfers between devices, per_device(): lax.ppermute(to_north, 'lat', [(i, i + 1) for i in range(lat_count - 1)])  4.15 us
    ppermute x1, starting transfers between devices, per_device(): from_west = lax.ppermute(to_east, LON, up)  3.92 us
    pallas_call x1, Pallas kernels, per_device(): call(final_kernel, name='final', out_shape=(shape(ROWS, LANES), shape(ROW...  3.76 us
    ppermute x1, starting transfers between devices, per_device(): lax.ppermute(to_south, 'lat', [(i + 1, i) for i in range(lat_count - 1)])  1.92 us
  transfers between devices with their start and end apart: 5, of which 1 were waited for; matrix products, arithmetic and copies ran while one was open for 2% of the time, Pallas kernels for 0%

commit v1 on v0

--- a/solution.py
+++ b/solution.py
@@ -36,7 +36,18 @@
     return jnp.where(last, rb, ra), jnp.where(last, ra, rb)
 
 
-def pack_kernel(f_ref, p_ref, d_ref, m_ref, x_ref, east_ref, west_ref):
+def pack_kernel(pairs, f_hbm, p_hbm, d_hbm, m_hbm, map_hbm, x_ref, east_ref, west_ref, reach_ref, choice_ref,
+                f_ref, p_ref, d_ref, m_ref, pivot, sems):
+    copies = [
+        pltpu.make_async_copy(source, target, sems.at[i])
+        for i, (source, target) in enumerate((
+            (m_hbm, m_ref), (d_hbm, d_ref), (f_hbm, f_ref), (p_hbm, p_ref), (map_hbm.at[pl.ds(0, LANES)], pivot),
+        ))
+    ]
+    for copy in copies:
+        copy.start()
+    for copy in copies:
+        copy.wait()
     for g in range(ROWS // 8):
         rows = pl.ds(8 * g, 8)
         flag = m_ref[rows, :].astype(F32)
@@ -60,6 +71,11 @@
         tile = x_ref[q, pl.ds(row, 8), :]
         east_ref[pl.ds(BLK + 8 * slot, 8), :] = tile
         west_ref[pl.ds(BLK + 8 * slot, 8), :] = tile
+    past = pivot[0] + (2 * pairs * LANES - 8)
+    reach = past % (2 * LANES) + 8
+    reach_ref[0] = reach
+    split = jnp.where(reach + EDGE >= 2 * LANES, 1, 0)
+    choice_ref[0] = 2 * ((past // (2 * LANES)) % pairs) + split
 
 
 def unpack_halo(from_west, from_east, q, blk, v, lane):
@@ -111,8 +127,14 @@
 GROUPS = ROWS // 8 + 2
 
 
-def basis_kernel(x_ref, fw_ref, fe_ref, fs_ref, fn_ref, ff_ref, basis_ref, sums_ref,
-                 depth, side, inv, coef, acc):
+def basis_kernel(x_ref, fw_ref, fe_ref, fs_hbm, fn_hbm, ff_hbm, basis_ref, sums_ref,
+                 depth, side, inv, coef, acc, fs_ref, fn_ref, ff_ref, sems):
+    copies = [
+        pltpu.make_async_copy(source, target, sems.at[i])
+        for i, (source, target) in enumerate(((fs_hbm, fs_ref), (fn_hbm, fn_ref), (ff_hbm, ff_ref)))
+    ]
+    for copy in copies:
+        copy.start()
     lane = lanes_of(8)
     zero = jnp.zeros((8, LANES), F32)
     targets = (
@@ -126,6 +148,10 @@
             own[pl.ds(16 + 8 * g, 8), :] = x_ref[q, pl.ds(8 * g, 8), :]
             blk, v = 8 * g // BLK, (8 * g % BLK) // 8
             rim[pl.ds(16 + 8 * g, 8), :] = unpack_halo(fw_ref, fe_ref, q, blk, v, lane)
+    for copy in copies:
+        copy.wait()
+    for q in range(3):
+        own, rim = targets[q](0), targets[q](1)
         for t, ref in ((0, own), (1, rim)):
             at = 32 * t + 8 * q
             ref[pl.ds(8, 8), :] = fs_ref[pl.ds(at, 8), :]
@@ -261,7 +287,7 @@
 
 
 def final_kernel(sum_ref, basis_ref, height_ref, residual_ref):
-    held = jnp.broadcast_to(jnp.sum(sum_ref[...], axis=0, keepdims=True), (8, LANES))
+    products = jnp.broadcast_to(jnp.sum(sum_ref[...], axis=0, keepdims=True), (8, LANES))
     row = lax.broadcasted_iota(jnp.int32, (24, LANES), 0)
     col = lax.broadcasted_iota(jnp.int32, (24, LANES), 1)
     half = STEPS + 1
@@ -277,7 +303,7 @@
     def gathered(index):
         index = jnp.where(inside, index, 6)
         parts = [
-            jnp.take_along_axis(held, index[8 * g : 8 * g + 8], axis=1, mode="promise_in_bounds")
+            jnp.take_along_axis(products, index[8 * g : 8 * g + 8], axis=1, mode="promise_in_bounds")
             for g in range(3)
         ]
         return jnp.concatenate(parts, axis=0)
@@ -329,34 +355,43 @@
 
 
 def shape(*dims):
-    return jax.ShapeDtypeStruct(dims, F32)
+    return pltpu.VMEM(dims, F32)
+
+
+def held(*values, space=pltpu.VMEM):
+    return tuple(pltpu.with_memory_space_constraint(v, space) for v in values)
+
+
+def limit(mib):
+    return pltpu.CompilerParams(vmem_limit_bytes=mib << 20)
 
 
 def per_device(forcing, search_direction, ocean_depth, land_mask, fold_map):
     lat_count, lon_count = lax.axis_size("lat"), lax.axis_size(LON)
-    call = functools.partial(pl.pallas_call, compiler_params=pltpu.CompilerParams())
-    fields, to_east, to_west = call(
-        pack_kernel, name="pack",
-        out_shape=(shape(3, ROWS, LANES), shape(BLK + 32, LANES), shape(BLK + 32, LANES)),
-    )(forcing, search_direction, ocean_depth, land_mask)
+    call = pl.pallas_call
+    fields, to_east, to_west, reach, choice = call(
+        functools.partial(pack_kernel, lon_count // 2), name="pack",
+        in_specs=[pl.BlockSpec(memory_space=pl.ANY)] * 5,
+        out_specs=[pl.BlockSpec(memory_space=pltpu.VMEM)] * 3 + [pl.BlockSpec(memory_space=pltpu.SMEM)] * 2,
+        out_shape=(shape(3, ROWS, LANES), shape(BLK + 32, LANES), shape(BLK + 32, LANES),
+                   pltpu.SMEM((1,), jnp.int32), pltpu.SMEM((1,), jnp.int32)),
+        scratch_shapes=[pltpu.VMEM((ROWS, LANES), F32)] * 3 + [
+            pltpu.VMEM((ROWS, LANES), jnp.int32), pltpu.SMEM((LANES,), jnp.int32), pltpu.SemaphoreType.DMA((5,)),
+        ],
+        compiler_params=limit(4),
+    )(*held(forcing, search_direction, ocean_depth, land_mask, fold_map, space=pltpu.HBM))
     up = [(i, (i + 1) % lon_count) for i in range(lon_count)]
     from_west = lax.ppermute(to_east, LON, up)
     from_east = lax.ppermute(to_west, LON, [(b, a) for a, b in up])
 
-    pivot = fold_map[0]
-    offset = (pivot - 8) % (2 * LANES)
-    reach = offset + 8
-    pairing = ((pivot - reach) // (2 * LANES)) % (lon_count // 2)
-    split = (reach + EDGE >= 2 * LANES).astype(jnp.int32)
     to_north, to_south, across, across_next = call(
         turn_kernel, name="turn",
         in_specs=[pl.BlockSpec(memory_space=pltpu.SMEM)] + [pl.BlockSpec(memory_space=pltpu.VMEM)] * 3,
         out_shape=(shape(64, LANES),) * 4,
         scratch_shapes=[pltpu.VMEM((64, LANES), F32)] * 2,
-    )(reach.reshape(1), fields, from_west, from_east)
-
-    from_south = lax.ppermute(to_north, "lat", [(i, i + 1) for i in range(lat_count - 1)])
-    from_north = lax.ppermute(to_south, "lat", [(i + 1, i) for i in range(lat_count - 1)])
+        compiler_params=limit(4),
+    )(reach, *held(fields, from_west, from_east))
+
     top = (lat_count - 1) * lon_count
 
     def over_fold(value, pairing):
@@ -364,11 +399,19 @@
         return lax.ppermute(value, ("lat",) + LON, pairs)
 
     def branch(index):
-        if index % 2 == 0:
-            return lambda near, far: over_fold(near, index // 2)
-        return lambda near, far: over_fold(near, index // 2) + over_fold(far, index // 2 + 1)
-
-    folded = lax.switch(2 * pairing + split, [branch(i) for i in range(lon_count)], across, across_next)
+        def exchange(near, far, to_north, to_south):
+            folded = over_fold(near, index // 2)
+            if index % 2:
+                folded = folded + over_fold(far, index // 2 + 1)
+            from_south = lax.ppermute(to_north, "lat", [(i, i + 1) for i in range(lat_count - 1)])
+            from_north = lax.ppermute(to_south, "lat", [(i + 1, i) for i in range(lat_count - 1)])
+            return folded, from_south, from_north
+
+        return exchange
+
+    folded, from_south, from_north = lax.switch(
+        choice[0], [branch(i) for i in range(lon_count)], across, across_next, to_north, to_south
+    )
 
     basis, sums = call(
         basis_kernel, name="basis",
@@ -379,14 +422,17 @@
             pltpu.VMEM((2, EXT, LANES), F32),
             pltpu.VMEM((2, 9, EXT, LANES), F32),
             pltpu.VMEM((STEPS, 8, 8, LANES), F32),
-        ],
-    )(fields, from_west, from_east, from_south, from_north, folded)
+        ] + [pltpu.VMEM((64, LANES), F32)] * 3 + [pltpu.SemaphoreType.DMA((3,))],
+        in_specs=[pl.BlockSpec(memory_space=pltpu.VMEM)] * 3 + [pl.BlockSpec(memory_space=pl.ANY)] * 3,
+        compiler_params=limit(12),
+    )(*held(fields, from_west, from_east), *held(from_south, from_north, folded, space=pltpu.HBM))
     sums = lax.all_to_all(sums, LON, split_axis=0, concat_axis=0, tiled=True)
-    sums = call(middle_kernel, name="middle", out_shape=shape(lat_count, LANES))(sums)
+    sums = call(middle_kernel, name="middle", out_shape=shape(lat_count, LANES), compiler_params=limit(2))(*held(sums))
     sums = lax.all_to_all(sums, "lat", split_axis=0, concat_axis=0, tiled=True)
     return call(
-        final_kernel, name="final", out_shape=(shape(ROWS, LANES), shape(ROWS, LANES)),
-    )(sums, basis)
+        final_kernel, name="final", out_shape=(jax.ShapeDtypeStruct((ROWS, LANES), F32),) * 2,
+        compiler_params=limit(4),
+    )(*held(sums, basis))
 
 
 def solution(mesh):

time: 79.4 us -> 70.2 us (0.88)
  Pallas kernels: 16.2 us -> 10 us
  waiting for transfers between devices: 1.6 us -> 4.42 us
  local copies, waits for them, and re-layouts: 2.42 us -> 0 us
  blocking collectives: 33.2 us -> 31.2 us
  between operations: 1.88 us -> 0.69 us
    pallas_call x3, Pallas kernels: 6.91 us -> 3.58 us  [the longest x1 2.32 us: per_device(): call(final_kernel, name='final', out_shape=(jax.ShapeDtypeStruct((ROWS, L...]
    ppermute x2, waiting for transfers between devices: 1.59 us -> 3.39 us  [the longest x1 3.39 us: exchange(): lax.ppermute(to_south, 'lat', [(i + 1, i) for i in range(lat_count - 1)])]
    all_to_all x1, blocking collectives: 17.1 us -> 15.3 us  [per_device(): sums = lax.all_to_all(sums, 'lat', split_axis=0, concat_axis=0, tiled=True)]
    pallas_call x1, Pallas kernels: 1.73 us -> 0.13 us  [per_device(): call(turn_kernel, name='turn', in_specs=[pl.BlockSpec(memory_space=pltpu....]
    pallas_call x1, Pallas kernels: 7.52 us -> 6.29 us  [per_device(): call(basis_kernel, name='basis', out_shape=(shape(VECTORS, EXT, LANES), s...]
    unnamed x8 -> x0, local copies, waits for them, and re-layouts: 1.22 us -> none
    slice x1 -> x0, local copies, waits for them, and re-layouts: 1.2 us -> none  [per_device(): pivot = fold_map[0]]
    ppermute x1, waiting for transfers between devices: 0.01 us -> 1.02 us  [per_device(): from_east = lax.ppermute(to_west, LON, [(b, a) for a, b in up])]
  transfers between devices with their start and end apart: 5 -> 5, of which waited for: 1 -> 2; matrix products, arithmetic and copies ran while one was open for 2% -> 0% of each run, Pallas kernels for 0% -> 0%
where the time goes in v1:
time: 70.2 us; the launch traced here: 69.8 us
  blocking collectives  31.2 us (44%)
  starting transfers between devices  23.4 us (33%)
  Pallas kernels  10 us (14%)
  waiting for transfers between devices  4.42 us (6%)
    all_to_all x1, blocking collectives, per_device(): sums = lax.all_to_all(sums, LON, split_axis=0, concat_axis=0, tiled=True)  15.9 us
    all_to_all x1, blocking collectives, per_device(): sums = lax.all_to_all(sums, 'lat', split_axis=0, concat_axis=0, tiled=True)  15.3 us
    ppermute x1, starting transfers between devices, per_device(): from_east = lax.ppermute(to_west, LON, [(b, a) for a, b in up])  11.7 us
    pallas_call x1, Pallas kernels, per_device(): call(basis_kernel, name='basis', out_shape=(shape(VECTORS, EXT, LANES), s...  6.29 us
    ppermute x1, starting transfers between devices, exchange(): lax.ppermute(to_north, 'lat', [(i, i + 1) for i in range(lat_count - 1)])  4.61 us
    ppermute x1, starting transfers between devices, per_device(): from_west = lax.ppermute(to_east, LON, up)  3.94 us
    ppermute x1, waiting for transfers between devices, exchange(): lax.ppermute(to_south, 'lat', [(i + 1, i) for i in range(lat_count - 1)])  3.39 us
    pallas_call x1, Pallas kernels, per_device(): call(final_kernel, name='final', out_shape=(jax.ShapeDtypeStruct((ROWS, L...  2.32 us
  transfers between devices with their start and end apart: 5, of which 2 were waited for; matrix products, arithmetic and copies ran while one was open for 0% of the time, Pallas kernels for 0%

profile of v1, /device:TPU:1, one launch (start us, length us, event | category | flops | bytes accessed | tf_op | source)
XLA Modules:
  0.0 69.8 jit_solution(12453038910794383710)
XLA Ops:
  0.6 1.2 %pack.1 = (f32[3,160,128]{2,1,0:T(8,128)S(1)}, f32[72,128]{1,0:T(8,128)S(1)}, f32[72,128]{1,0:T(8,128)S(1)}, s32[1]{0:T(128)S(4)}, s32[1]{0:T(128)S(4)}) custom-call(f32[160,128]{1,0:T(8,128)} %f_hbm.1, f32[160,128]{1,0:T(8,128)} %p_hbm.1, f32[160,128]{1,0:T(8,128)} %d_hbm.1, s32[160,128]{1,0:T(8,128)} %m_hbm.1, s32[4096]{0:T(1024)} %map_hbm.1), custom_call_target="tpu_custom_call" | custom-call | tf_op jit(solution)/shard_map/pack/pallas_call | solution.py:372
  1.9 3.9 %collective-permute-start.112 = (f32[72,128]{1,0:T(8,128)S(1)}, f32[72,128]{1,0:T(8,128)S(1)}, u32[]{:S(2)}, u32[]{:S(2)}) collective-permute-start(f32[72,128]{1,0:T(8,128)S(1)} %get-tuple-element.353), channel_id=1, source_target_pairs={{0,1},{1,2},{2,3},{3,4},{4,5},{5,6},{6,7},{7,8},{8,9},{9,10},{10,1... | collective-permute-start | bytes 110600 | tf_op jit(solution)/shard_map/ppermute | solution.py:384
  5.8 11.7 %collective-permute-start.113 = (f32[72,128]{1,0:T(8,128)S(1)}, f32[72,128]{1,0:T(8,128)S(1)}, u32[]{:S(2)}, u32[]{:S(2)}) collective-permute-start(f32[72,128]{1,0:T(8,128)S(1)} %get-tuple-element.354), channel_id=1, source_target_pairs={{1,0},{2,1},{3,2},{4,3},{5,4},{6,5},{7,6},{8,7},{9,8},{10,9},{11,1... | collective-permute-start | bytes 110600 | tf_op jit(solution)/shard_map/ppermute | solution.py:385
  17.5 0.0 collective-permute-done.112.fw_ref
  17.5 1.0 %collective-permute-done.113.fe_ref = f32[72,128]{1,0:T(8,128)S(1)} collective-permute-done((f32[72,128]{1,0:T(8,128)S(1)}, f32[72,128]{1,0:T(8,128)S(1)}, u32[]{:S(2)}, u32[]{:S(2)}) %collective-permute-start.113) | collective-permute-done | bytes 36896 | tf_op jit(solution)/shard_map/ppermute | solution.py:385
  18.5 0.1 turn.1
  18.7 11.3 %conditional.1 = (f32[64,128]{1,0:T(8,128)}, f32[64,128]{1,0:T(8,128)}, f32[64,128]{1,0:T(8,128)}) conditional(s32[]{:T(128)} %bitcast, (f32[64,128]{1,0:T(8,128)S(1)}, f32[64,128]{1,0:T(8,128)S(1)}, f32[64,128]{1,0:T(8,128)S(1)}) %tuple.135, (f32[64,128]{1,0:T(8,128)S(1)}, f32[64,128]{1,0:T(8,128)S(1)}, ...), branch_computations={%region_0.0_spmd, %region_1.0_spmd, %region_2.0_spmd, %region_3.0_... | conditional | flops 8192 | bytes 622776 | solution.py:412
  18.7 1.3 %collective-permute-start.70 = (f32[64,128]{1,0:T(8,128)S(1)}, f32[64,128]{1,0:T(8,128)}, u32[]{:S(2)}, u32[]{:S(2)}) collective-permute-start(f32[64,128]{1,0:T(8,128)S(1)} %get-tuple-element.294), channel_id=1, source_target_pairs={{480,500},{481,499},{482,498},{483,497},{484,496},{485,495},{486,4... | collective-permute-start | bytes 98312 | tf_op jit(solution)/shard_map/cond/branch_20_fun/ppermute | solution.py:399
  20.0 4.6 %collective-permute-start.71 = (f32[64,128]{1,0:T(8,128)S(1)}, f32[64,128]{1,0:T(8,128)}, u32[]{:S(2)}, u32[]{:S(2)}) collective-permute-start(f32[64,128]{1,0:T(8,128)S(1)} %get-tuple-element.295), channel_id=1, source_target_pairs={{0,32},{32,64},{64,96},{96,128},{128,160},{160,192},{192,224},{224... | collective-permute-start | bytes 98312 | tf_op jit(solution)/shard_map/cond/branch_20_fun/ppermute | solution.py:406
  24.6 1.9 %collective-permute-start.72 = (f32[64,128]{1,0:T(8,128)S(1)}, f32[64,128]{1,0:T(8,128)}, u32[]{:S(2)}, u32[]{:S(2)}) collective-permute-start(f32[64,128]{1,0:T(8,128)S(1)} %get-tuple-element.296), channel_id=1, source_target_pairs={{32,0},{64,32},{96,64},{128,96},{160,128},{192,160},{224,192},{256... | collective-permute-start | bytes 98312 | tf_op jit(solution)/shard_map/cond/branch_20_fun/ppermute | solution.py:407
  26.5 0.0 collective-permute-done.70
  26.6 0.0 collective-permute-done.71
  26.6 3.4 %collective-permute-done.72 = f32[64,128]{1,0:T(8,128)} collective-permute-done((f32[64,128]{1,0:T(8,128)S(1)}, f32[64,128]{1,0:T(8,128)}, u32[]{:S(2)}, u32[]{:S(2)}) %collective-permute-start.72) | collective-permute-done | bytes 32800 | tf_op jit(solution)/shard_map/cond/branch_20_fun/ppermute | solution.py:407
  30.0 6.3 %basis.1 = (f32[17,192,128]{2,1,0:T(8,128)S(1)}, f32[32,128]{1,0:T(8,128)S(1)}) custom-call(f32[3,160,128]{2,1,0:T(8,128)S(1)} %get-tuple-element.352.x_ref, f32[72,128]{1,0:T(8,128)S(1)} %collective-permute-done.112.fw_ref, f32[72,128]{1,0:T(8,128)S(1)} %collective-permute-done.113.fe_ref, f32[64,128]{1,0:T(8,128)} %get-tuple-element.361.fs_hbm, ...), custom_call_target="tpu_custom_call" | custom-call | tf_op jit(solution)/shard_map/basis/pallas_call | solution.py:416
  36.3 15.9 %all_to_all.22 = f32[32,1,128]{2,1,0:T(1,128)S(1)} all-to-all(f32[32,1,128]{2,1,0:T(1,128)S(1)} %bitcast.12), channel_id=1, replica_groups=mesh['lat'=16,'lon_0'=8,'lon_1'=4] {'lon_0','lon_1'}, dimensions={0} | all-to-all | bytes 32768 | tf_op jit(solution)/shard_map/all_to_all | solution.py:429
  52.1 15.3 %all_to_all.23 = f32[16,1,128]{2,1,0:T(1,128)S(1)} all-to-all(f32[16,1,128]{2,1,0:T(1,128)S(1)} %bitcast.11), channel_id=1, replica_groups=mesh['lat'=16,'lon_0'=8,'lon_1'=4] {'lat'}, dimensions={0} | all-to-all | bytes 16384 | tf_op jit(solution)/shard_map/all_to_all | solution.py:431
  67.4 2.3 %final.1 = (f32[160,128]{1,0:T(8,128)}, f32[160,128]{1,0:T(8,128)}) custom-call(f32[16,128]{1,0:T(8,128)S(1)} %bitcast.10, f32[17,192,128]{2,1,0:T(8,128)S(1)} %get-tuple-element.365.basis_ref), custom_call_target="tpu_custom_call" | custom-call | tf_op jit(solution)/shard_map/final/pallas_call | solution.py:432
  (1 shorter events, 0.0 us)
Async XLA Ops:
  1.9 15.6 %collective-permute-start.112 = (f32[72,128]{1,0:T(8,128)S(1)}, f32[72,128]{1,0:T(8,128)S(1)}, u32[]{:S(2)}, u32[]{:S(2)}) collective-permute-start(f32[72,128]{1,0:T(8,128)S(1)} %get-tuple-element.353), channel_id=1, source_target_pairs={{0,1},{1,2},{2,3},{3,4},{4,5},{5,6},{6,7},{7,8},{8,9},{9,10},{10,1... | collective-permute-start | bytes 110600 | tf_op jit(solution)/shard_map/ppermute | solution.py:384
  5.8 12.7 %collective-permute-start.113 = (f32[72,128]{1,0:T(8,128)S(1)}, f32[72,128]{1,0:T(8,128)S(1)}, u32[]{:S(2)}, u32[]{:S(2)}) collective-permute-start(f32[72,128]{1,0:T(8,128)S(1)} %get-tuple-element.354), channel_id=1, source_target_pairs={{1,0},{2,1},{3,2},{4,3},{5,4},{6,5},{7,6},{8,7},{9,8},{10,9},{11,1... | collective-permute-start | bytes 110600 | tf_op jit(solution)/shard_map/ppermute | solution.py:385
  18.7 7.8 %collective-permute-start.70 = (f32[64,128]{1,0:T(8,128)S(1)}, f32[64,128]{1,0:T(8,128)}, u32[]{:S(2)}, u32[]{:S(2)}) collective-permute-start(f32[64,128]{1,0:T(8,128)S(1)} %get-tuple-element.294), channel_id=1, source_target_pairs={{480,500},{481,499},{482,498},{483,497},{484,496},{485,495},{486,4... | collective-permute-start | bytes 98312 | tf_op jit(solution)/shard_map/cond/branch_20_fun/ppermute | solution.py:399
  20.0 6.6 %collective-permute-start.71 = (f32[64,128]{1,0:T(8,128)S(1)}, f32[64,128]{1,0:T(8,128)}, u32[]{:S(2)}, u32[]{:S(2)}) collective-permute-start(f32[64,128]{1,0:T(8,128)S(1)} %get-tuple-element.295), channel_id=1, source_target_pairs={{0,32},{32,64},{64,96},{96,128},{128,160},{160,192},{192,224},{224... | collective-permute-start | bytes 98312 | tf_op jit(solution)/shard_map/cond/branch_20_fun/ppermute | solution.py:406
  24.6 5.3 %collective-permute-start.72 = (f32[64,128]{1,0:T(8,128)S(1)}, f32[64,128]{1,0:T(8,128)}, u32[]{:S(2)}, u32[]{:S(2)}) collective-permute-start(f32[64,128]{1,0:T(8,128)S(1)} %get-tuple-element.296), channel_id=1, source_target_pairs={{32,0},{64,32},{96,64},{128,96},{160,128},{192,160},{224,192},{256... | collective-permute-start | bytes 98312 | tf_op jit(solution)/shard_map/cond/branch_20_fun/ppermute | solution.py:407

commit v2 on v1

--- a/solution.py
+++ b/solution.py
@@ -36,8 +36,9 @@
     return jnp.where(last, rb, ra), jnp.where(last, ra, rb)
 
 
-def pack_kernel(pairs, f_hbm, p_hbm, d_hbm, m_hbm, map_hbm, x_ref, east_ref, west_ref, reach_ref, choice_ref,
+def pack_kernel(pairs, f_hbm, p_hbm, d_hbm, m_hbm, map_hbm, x_ref, first_ref, second_ref, reach_ref, choice_ref,
                 f_ref, p_ref, d_ref, m_ref, pivot, sems):
+    even = lax.axis_index(LON) % 2 == 0
     copies = [
         pltpu.make_async_copy(source, target, sems.at[i])
         for i, (source, target) in enumerate((
@@ -65,12 +66,12 @@
                 inside = (lane >= at) & (lane < at + EDGE)
                 west = jnp.where(inside, pltpu.roll(tile, at, 1) if at else tile, west)
                 east = jnp.where(inside, pltpu.roll(tile, (at + EDGE) % LANES, 1), east)
-        east_ref[pl.ds(8 * v, 8), :] = east
-        west_ref[pl.ds(8 * v, 8), :] = west
+        first_ref[pl.ds(8 * v, 8), :] = jnp.where(even, east, west)
+        second_ref[pl.ds(8 * v, 8), :] = jnp.where(even, west, east)
     for slot, (q, row) in enumerate(((0, ROWS - 8), (1, ROWS - 8), (2, ROWS - 8), (0, ROWS - 16))):
         tile = x_ref[q, pl.ds(row, 8), :]
-        east_ref[pl.ds(BLK + 8 * slot, 8), :] = tile
-        west_ref[pl.ds(BLK + 8 * slot, 8), :] = tile
+        first_ref[pl.ds(BLK + 8 * slot, 8), :] = tile
+        second_ref[pl.ds(BLK + 8 * slot, 8), :] = tile
     past = pivot[0] + (2 * pairs * LANES - 8)
     reach = past % (2 * LANES) + 8
     reach_ref[0] = reach
@@ -87,18 +88,43 @@
     return jnp.where(lane < EDGE, right, jnp.where(lane >= LANES - EDGE, left, 0.0))
 
 
-def turn_kernel(r_ref, x_ref, fw_ref, fe_ref, north_ref, south_ref, fold_ref, next_ref, t1_ref, t2_ref):
+def sort_partners(axis, first, second, before, after):
+    even = lax.axis_index(axis) % 2 == 0
+    for g in range(first.shape[0] // 8):
+        rows = pl.ds(8 * g, 8)
+        a, b = first[rows, :], second[rows, :]
+        before[rows, :] = jnp.where(even, b, a)
+        after[rows, :] = jnp.where(even, a, b)
+
+
+def turn_kernel(tops, r_ref, x_ref, first_ref, second_ref, one_ref, two_ref, next_ref,
+                fw_ref, fe_ref, north_ref, south_ref, t1_ref, t2_ref):
     lane = lanes_of(8)
+    lat = lax.axis_index("lat")
+    even, top_row = lat % 2 == 0, lat == tops
+    sort_partners(LON, first_ref, second_ref, fw_ref, fe_ref)
     top, low = ROWS // 8 - 1, 0
-    for slot, (q, g) in enumerate(((0, top), (1, top), (2, top), (0, top - 1))):
-        north_ref[pl.ds(8 * slot, 8), :] = x_ref[q, pl.ds(8 * g, 8), :]
-        blk, v = 8 * g // BLK, (8 * g % BLK) // 8
-        north_ref[pl.ds(32 + 8 * slot, 8), :] = unpack_halo(fw_ref, fe_ref, q, blk, v, lane)
-    for slot, (q, g) in enumerate(((0, low), (1, low), (2, low), (0, low + 1))):
-        south_ref[pl.ds(8 * slot, 8), :] = x_ref[q, pl.ds(8 * g, 8), :]
-        blk, v = 8 * g // BLK, (8 * g % BLK) // 8
-        south_ref[pl.ds(32 + 8 * slot, 8), :] = unpack_halo(fw_ref, fe_ref, q, blk, v, lane)
-    reach = r_ref[0]
+    for ref, rows in (
+        (north_ref, ((0, top), (1, top), (2, top), (0, top - 1))),
+        (south_ref, ((0, low), (1, low), (2, low), (0, low + 1))),
+    ):
+        for slot, (q, g) in enumerate(rows):
+            ref[pl.ds(8 * slot, 8), :] = x_ref[q, pl.ds(8 * g, 8), :]
+            blk, v = 8 * g // BLK, (8 * g % BLK) // 8
+            ref[pl.ds(32 + 8 * slot, 8), :] = unpack_halo(fw_ref, fe_ref, q, blk, v, lane)
+    for g in range(8):
+        rows = pl.ds(8 * g, 8)
+        north, south = north_ref[rows, :], south_ref[rows, :]
+        one_ref[rows, :] = jnp.where(even, north, south)
+        two_ref[rows, :] = jnp.where(even, south, north)
+        next_ref[rows, :] = jnp.zeros((8, LANES), F32)
+
+    @pl.when(top_row)
+    def _():
+        across_fold(r_ref[0], lane, north_ref, fw_ref, fe_ref, two_ref, next_ref, t1_ref, t2_ref)
+
+
+def across_fold(reach, lane, north_ref, fw_ref, fe_ref, fold_ref, next_ref, t1_ref, t2_ref):
     along = reach - lane
     pick = along & (LANES - 1)
     place_a = along
@@ -127,14 +153,11 @@
 GROUPS = ROWS // 8 + 2
 
 
-def basis_kernel(x_ref, fw_ref, fe_ref, fs_hbm, fn_hbm, ff_hbm, basis_ref, sums_ref,
-                 depth, side, inv, coef, acc, fs_ref, fn_ref, ff_ref, sems):
-    copies = [
-        pltpu.make_async_copy(source, target, sems.at[i])
-        for i, (source, target) in enumerate(((fs_hbm, fs_ref), (fn_hbm, fn_ref), (ff_hbm, ff_ref)))
-    ]
-    for copy in copies:
-        copy.start()
+def basis_kernel(x_ref, first_ref, second_ref, one_ref, two_hbm, basis_ref, sums_ref,
+                 depth, side, inv, coef, acc, fw_ref, fe_ref, fs_ref, fn_ref, two_ref, sem):
+    copy = pltpu.make_async_copy(two_hbm, two_ref, sem)
+    copy.start()
+    sort_partners(LON, first_ref, second_ref, fw_ref, fe_ref)
     lane = lanes_of(8)
     zero = jnp.zeros((8, LANES), F32)
     targets = (
@@ -148,18 +171,18 @@
             own[pl.ds(16 + 8 * g, 8), :] = x_ref[q, pl.ds(8 * g, 8), :]
             blk, v = 8 * g // BLK, (8 * g % BLK) // 8
             rim[pl.ds(16 + 8 * g, 8), :] = unpack_halo(fw_ref, fe_ref, q, blk, v, lane)
-    for copy in copies:
-        copy.wait()
+    copy.wait()
+    sort_partners("lat", one_ref, two_ref, fs_ref, fn_ref)
     for q in range(3):
         own, rim = targets[q](0), targets[q](1)
         for t, ref in ((0, own), (1, rim)):
             at = 32 * t + 8 * q
             ref[pl.ds(8, 8), :] = fs_ref[pl.ds(at, 8), :]
-            ref[pl.ds(EXT - 16, 8), :] = fn_ref[pl.ds(at, 8), :] + ff_ref[pl.ds(at, 8), :]
+            ref[pl.ds(EXT - 16, 8), :] = fn_ref[pl.ds(at, 8), :]
             if q == 0:
                 at = 32 * t + 24
                 ref[pl.ds(0, 8), :] = fs_ref[pl.ds(at, 8), :]
-                ref[pl.ds(EXT - 8, 8), :] = fn_ref[pl.ds(at, 8), :] + ff_ref[pl.ds(at, 8), :]
+                ref[pl.ds(EXT - 8, 8), :] = fn_ref[pl.ds(at, 8), :]
             else:
                 ref[pl.ds(0, 8), :] = zero
                 ref[pl.ds(EXT - 8, 8), :] = zero
@@ -369,7 +392,7 @@
 def per_device(forcing, search_direction, ocean_depth, land_mask, fold_map):
     lat_count, lon_count = lax.axis_size("lat"), lax.axis_size(LON)
     call = pl.pallas_call
-    fields, to_east, to_west, reach, choice = call(
+    fields, first, second, reach, choice = call(
         functools.partial(pack_kernel, lon_count // 2), name="pack",
         in_specs=[pl.BlockSpec(memory_space=pl.ANY)] * 5,
         out_specs=[pl.BlockSpec(memory_space=pltpu.VMEM)] * 3 + [pl.BlockSpec(memory_space=pltpu.SMEM)] * 2,
@@ -380,38 +403,37 @@
         ],
         compiler_params=limit(4),
     )(*held(forcing, search_direction, ocean_depth, land_mask, fold_map, space=pltpu.HBM))
-    up = [(i, (i + 1) % lon_count) for i in range(lon_count)]
-    from_west = lax.ppermute(to_east, LON, up)
-    from_east = lax.ppermute(to_west, LON, [(b, a) for a, b in up])
-
-    to_north, to_south, across, across_next = call(
-        turn_kernel, name="turn",
+    evens, odds = range(0, lon_count, 2), range(1, lon_count, 2)
+    first = lax.ppermute(first, LON, [(i, i + 1) for i in evens] + [(i + 1, i) for i in evens])
+    wrap = [(i, (i + 1) % lon_count) for i in odds]
+    second = lax.ppermute(second, LON, wrap + [(b, a) for a, b in wrap])
+
+    one, two, two_next = call(
+        functools.partial(turn_kernel, lat_count - 1), name="turn",
         in_specs=[pl.BlockSpec(memory_space=pltpu.SMEM)] + [pl.BlockSpec(memory_space=pltpu.VMEM)] * 3,
-        out_shape=(shape(64, LANES),) * 4,
-        scratch_shapes=[pltpu.VMEM((64, LANES), F32)] * 2,
+        out_shape=(shape(64, LANES),) * 3,
+        scratch_shapes=[pltpu.VMEM((BLK + 32, LANES), F32)] * 2 + [pltpu.VMEM((64, LANES), F32)] * 4,
         compiler_params=limit(4),
-    )(reach, *held(fields, from_west, from_east))
-
+    )(reach, *held(fields, first, second))
+
+    evens, odds = range(0, lat_count, 2), range(1, lat_count - 1, 2)
+    one = lax.ppermute(one, "lat", [(i, i + 1) for i in evens] + [(i + 1, i) for i in evens])
+    swaps = [
+        (i * lon_count + c, (i + s) * lon_count + c)
+        for k in odds for i, s in ((k, 1), (k + 1, -1)) for c in range(lon_count)
+    ]
     top = (lat_count - 1) * lon_count
 
-    def over_fold(value, pairing):
-        pairs = [(top + i, top + (2 * pairing - i) % lon_count) for i in range(lon_count)]
-        return lax.ppermute(value, ("lat",) + LON, pairs)
+    def second_round(value, pairing):
+        fold = [(top + i, top + (2 * pairing - i) % lon_count) for i in range(lon_count)]
+        return lax.ppermute(value, ("lat",) + LON, swaps + fold)
 
     def branch(index):
-        def exchange(near, far, to_north, to_south):
-            folded = over_fold(near, index // 2)
-            if index % 2:
-                folded = folded + over_fold(far, index // 2 + 1)
-            from_south = lax.ppermute(to_north, "lat", [(i, i + 1) for i in range(lat_count - 1)])
-            from_north = lax.ppermute(to_south, "lat", [(i + 1, i) for i in range(lat_count - 1)])
-            return folded, from_south, from_north
-
-        return exchange
-
-    folded, from_south, from_north = lax.switch(
-        choice[0], [branch(i) for i in range(lon_count)], across, across_next, to_north, to_south
-    )
+        if index % 2 == 0:
+            return lambda near, far: second_round(near, index // 2)
+        return lambda near, far: second_round(near, index // 2) + second_round(far, (index // 2 + 1) % (lon_count // 2))
+
+    two = lax.switch(choice[0], [branch(i) for i in range(lon_count)], two, two_next)
 
     basis, sums = call(
         basis_kernel, name="basis",
@@ -422,10 +444,12 @@
             pltpu.VMEM((2, EXT, LANES), F32),
             pltpu.VMEM((2, 9, EXT, LANES), F32),
             pltpu.VMEM((STEPS, 8, 8, LANES), F32),
-        ] + [pltpu.VMEM((64, LANES), F32)] * 3 + [pltpu.SemaphoreType.DMA((3,))],
-        in_specs=[pl.BlockSpec(memory_space=pltpu.VMEM)] * 3 + [pl.BlockSpec(memory_space=pl.ANY)] * 3,
+        ] + [pltpu.VMEM((BLK + 32, LANES), F32)] * 2 + [pltpu.VMEM((64, LANES), F32)] * 3 + [
+            pltpu.SemaphoreType.DMA,
+        ],
+        in_specs=[pl.BlockSpec(memory_space=pltpu.VMEM)] * 4 + [pl.BlockSpec(memory_space=pl.ANY)],
         compiler_params=limit(12),
-    )(*held(fields, from_west, from_east), *held(from_south, from_north, folded, space=pltpu.HBM))
+    )(*held(fields, first, second, one), *held(two, space=pltpu.HBM))
     sums = lax.all_to_all(sums, LON, split_axis=0, concat_axis=0, tiled=True)
     sums = call(middle_kernel, name="middle", out_shape=shape(lat_count, LANES), compiler_params=limit(2))(*held(sums))
     sums = lax.all_to_all(sums, "lat", split_axis=0, concat_axis=0, tiled=True)

time: 70.2 us -> 69.6 us (level)
  blocking collectives: 31.2 us -> 32.6 us
  waiting for transfers between devices: 4.42 us -> 3.56 us
    all_to_all x1, blocking collectives: 15.3 us -> 17.4 us  [per_device(): sums = lax.all_to_all(sums, 'lat', split_axis=0, concat_axis=0, tiled=True)]
    ppermute x5 -> x4, waiting for transfers between devices: 4.42 us -> 3.56 us  [the longest x1 2.23 us: second_round(): return lax.ppermute(value, ('lat',) + LON, swaps + fold)]
    all_to_all x1, blocking collectives: 15.9 us -> 15.1 us  [per_device(): sums = lax.all_to_all(sums, LON, split_axis=0, concat_axis=0, tiled=True)]
    ppermute x5 -> x4, starting transfers between devices: 23.4 us -> 23 us  [the longest x1 12.2 us: per_device(): second = lax.ppermute(second, LON, wrap + [(b, a) for a, b in wrap])]
  transfers between devices with their start and end apart: 5 -> 4, of which waited for: 2 -> 2; matrix products, arithmetic and copies ran while one was open for 0% -> 0% of each run, Pallas kernels for 0% -> 0%
where the time goes in v2:
time: 69.6 us; the launch traced here: 69.7 us
  blocking collectives  32.6 us (47%)
  starting transfers between devices  23 us (33%)
  Pallas kernels  9.84 us (14%)
  waiting for transfers between devices  3.56 us (5%)
    all_to_all x1, blocking collectives, per_device(): sums = lax.all_to_all(sums, 'lat', split_axis=0, concat_axis=0, tiled=True)  17.4 us
    all_to_all x1, blocking collectives, per_device(): sums = lax.all_to_all(sums, LON, split_axis=0, concat_axis=0, tiled=True)  15.1 us
    ppermute x1, starting transfers between devices, per_device(): second = lax.ppermute(second, LON, wrap + [(b, a) for a, b in wrap])  12.2 us
    pallas_call x1, Pallas kernels, per_device(): call(basis_kernel, name='basis', out_shape=(shape(VECTORS, EXT, LANES), s...  6.16 us
    ppermute x1, starting transfers between devices, per_device(): lax.ppermute(first, LON, [(i, i + 1) for i in evens] + [(i + 1, i) for i...  3.94 us
    ppermute x1, starting transfers between devices, per_device(): lax.ppermute(one, 'lat', [(i, i + 1) for i in evens] + [(i + 1, i) for i...  3.73 us
    ppermute x1, starting transfers between devices, second_round(): return lax.ppermute(value, ('lat',) + LON, swaps + fold)  3.1 us
    pallas_call x1, Pallas kernels, per_device(): call(final_kernel, name='final', out_shape=(jax.ShapeDtypeStruct((ROWS, L...  2.32 us
  transfers between devices with their start and end apart: 4, of which 2 were waited for; matrix products, arithmetic and copies ran while one was open for 0% of the time, Pallas kernels for 0%

profile of v2, /device:TPU:1, one launch (start us, length us, event | category | flops | bytes accessed | tf_op | source)
XLA Modules:
  0.0 69.7 jit_solution(17049204470153127578)
XLA Ops:
  0.6 1.3 %pack.1 = (f32[3,160,128]{2,1,0:T(8,128)S(1)}, f32[72,128]{1,0:T(8,128)S(1)}, f32[72,128]{1,0:T(8,128)S(1)}, s32[1]{0:T(128)S(4)}, s32[1]{0:T(128)S(4)}) custom-call(f32[160,128]{1,0:T(8,128)} %f_hbm.1, f32[160,128]{1,0:T(8,128)} %p_hbm.1, f32[160,128]{1,0:T(8,128)} %d_hbm.1, s32[160,128]{1,0:T(8,128)} %m_hbm.1, s32[4096]{0:T(1024)} %map_hbm.1), custom_call_target="tpu_custom_call" | custom-call | tf_op jit(solution)/shard_map/pack/pallas_call | solution.py:395
  1.9 3.9 %collective-permute-start.48 = (f32[72,128]{1,0:T(8,128)S(1)}, f32[72,128]{1,0:T(8,128)S(1)}, u32[]{:S(2)}, u32[]{:S(2)}) collective-permute-start(f32[72,128]{1,0:T(8,128)S(1)} %get-tuple-element.158), channel_id=1, source_target_pairs={{0,1},{2,3},{4,5},{6,7},{8,9},{10,11},{12,13},{14,15},{16,17},{18,... | collective-permute-start | bytes 110600 | tf_op jit(solution)/shard_map/ppermute | solution.py:407
  5.8 12.2 %collective-permute-start.49 = (f32[72,128]{1,0:T(8,128)S(1)}, f32[72,128]{1,0:T(8,128)S(1)}, u32[]{:S(2)}, u32[]{:S(2)}) collective-permute-start(f32[72,128]{1,0:T(8,128)S(1)} %get-tuple-element.159), channel_id=1, source_target_pairs={{1,2},{3,4},{5,6},{7,8},{9,10},{11,12},{13,14},{15,16},{17,18},{19... | collective-permute-start | bytes 110600 | tf_op jit(solution)/shard_map/ppermute | solution.py:409
  18.0 0.0 collective-permute-done.48.first_ref
  18.1 1.3 %collective-permute-done.49.second_ref = f32[72,128]{1,0:T(8,128)S(1)} collective-permute-done((f32[72,128]{1,0:T(8,128)S(1)}, f32[72,128]{1,0:T(8,128)S(1)}, u32[]{:S(2)}, u32[]{:S(2)}) %collective-permute-start.49) | collective-permute-done | bytes 36896 | tf_op jit(solution)/shard_map/ppermute | solution.py:409
  19.4 0.1 turn.1
  19.5 3.7 %collective-permute-start.50 = (f32[64,128]{1,0:T(8,128)S(1)}, f32[64,128]{1,0:T(8,128)S(1)}, u32[]{:S(2)}, u32[]{:S(2)}) collective-permute-start(f32[64,128]{1,0:T(8,128)S(1)} %get-tuple-element.161), channel_id=1, source_target_pairs={{0,32},{64,96},{128,160},{192,224},{256,288},{320,352},{384,416},{... | collective-permute-start | bytes 98312 | tf_op jit(solution)/shard_map/ppermute | solution.py:420
  23.2 5.4 %conditional.1 = (f32[64,128]{1,0:T(8,128)}) conditional(s32[]{:T(128)} %bitcast, f32[64,128]{1,0:T(8,128)S(1)} %get-tuple-element.163, (f32[64,128]{1,0:T(8,128)S(1)}, f32[64,128]{1,0:T(8,128)S(1)}) %tuple.103, f32[64,128]{1,0:T(8,128)S(1)} %get-tuple-element.163, (f32[64,128]{1,0:T(8,128)S(1)}, ...), branch_computations={%region_0.0_spmd, %region_1.0_spmd, %region_2.0_spmd, %region_3.0_... | conditional | flops 8192 | bytes 360536 | solution.py:436
  23.3 3.1 %collective-permute-start.18 = (f32[64,128]{1,0:T(8,128)S(1)}, f32[64,128]{1,0:T(8,128)}, u32[]{:S(2)}, u32[]{:S(2)}) collective-permute-start(f32[64,128]{1,0:T(8,128)S(1)} %param.12), channel_id=1, source_target_pairs={{32,64},{33,65},{34,66},{35,67},{36,68},{37,69},{38,70},{39,71},{4... | collective-permute-start | bytes 98312 | tf_op jit(solution)/shard_map/cond/branch_12_fun/ppermute | solution.py:429
  26.4 2.2 %collective-permute-done.18 = f32[64,128]{1,0:T(8,128)} collective-permute-done((f32[64,128]{1,0:T(8,128)S(1)}, f32[64,128]{1,0:T(8,128)}, u32[]{:S(2)}, u32[]{:S(2)}) %collective-permute-start.18) | collective-permute-done | bytes 32800 | tf_op jit(solution)/shard_map/cond/branch_12_fun/ppermute | solution.py:429
  28.6 0.0 collective-permute-done.50.one_ref
  28.6 6.2 %basis.1 = (f32[17,192,128]{2,1,0:T(8,128)S(1)}, f32[32,128]{1,0:T(8,128)S(1)}) custom-call(f32[3,160,128]{2,1,0:T(8,128)S(1)} %get-tuple-element.157.x_ref, f32[72,128]{1,0:T(8,128)S(1)} %collective-permute-done.48.first_ref, f32[72,128]{1,0:T(8,128)S(1)} %collective-permute-done.49.second_ref, f32[64,128]{1,0:T(8,128)S(1)} %collective-permute-done.50.one_ref, ...), custom_call_target="tpu_custom_call" | custom-call | tf_op jit(solution)/shard_map/basis/pallas_call | solution.py:438
  34.8 15.1 %all_to_all.22 = f32[32,1,128]{2,1,0:T(1,128)S(1)} all-to-all(f32[32,1,128]{2,1,0:T(1,128)S(1)} %bitcast.12), channel_id=1, replica_groups=mesh['lat'=16,'lon_0'=8,'lon_1'=4] {'lon_0','lon_1'}, dimensions={0} | all-to-all | bytes 32768 | tf_op jit(solution)/shard_map/all_to_all | solution.py:453
  49.9 17.4 %all_to_all.23 = f32[16,1,128]{2,1,0:T(1,128)S(1)} all-to-all(f32[16,1,128]{2,1,0:T(1,128)S(1)} %bitcast.11), channel_id=1, replica_groups=mesh['lat'=16,'lon_0'=8,'lon_1'=4] {'lat'}, dimensions={0} | all-to-all | bytes 16384 | tf_op jit(solution)/shard_map/all_to_all | solution.py:455
  67.4 2.3 %final.1 = (f32[160,128]{1,0:T(8,128)}, f32[160,128]{1,0:T(8,128)}) custom-call(f32[16,128]{1,0:T(8,128)S(1)} %bitcast.10, f32[17,192,128]{2,1,0:T(8,128)S(1)} %get-tuple-element.166.basis_ref), custom_call_target="tpu_custom_call" | custom-call | tf_op jit(solution)/shard_map/final/pallas_call | solution.py:456
  (1 shorter events, 0.0 us)
Async XLA Ops:
  1.9 16.2 %collective-permute-start.48 = (f32[72,128]{1,0:T(8,128)S(1)}, f32[72,128]{1,0:T(8,128)S(1)}, u32[]{:S(2)}, u32[]{:S(2)}) collective-permute-start(f32[72,128]{1,0:T(8,128)S(1)} %get-tuple-element.158), channel_id=1, source_target_pairs={{0,1},{2,3},{4,5},{6,7},{8,9},{10,11},{12,13},{14,15},{16,17},{18,... | collective-permute-start | bytes 110600 | tf_op jit(solution)/shard_map/ppermute | solution.py:407
  5.8 13.5 %collective-permute-start.49 = (f32[72,128]{1,0:T(8,128)S(1)}, f32[72,128]{1,0:T(8,128)S(1)}, u32[]{:S(2)}, u32[]{:S(2)}) collective-permute-start(f32[72,128]{1,0:T(8,128)S(1)} %get-tuple-element.159), channel_id=1, source_target_pairs={{1,2},{3,4},{5,6},{7,8},{9,10},{11,12},{13,14},{15,16},{17,18},{19... | collective-permute-start | bytes 110600 | tf_op jit(solution)/shard_map/ppermute | solution.py:409
  19.5 9.1 %collective-permute-start.50 = (f32[64,128]{1,0:T(8,128)S(1)}, f32[64,128]{1,0:T(8,128)S(1)}, u32[]{:S(2)}, u32[]{:S(2)}) collective-permute-start(f32[64,128]{1,0:T(8,128)S(1)} %get-tuple-element.161), channel_id=1, source_target_pairs={{0,32},{64,96},{128,160},{192,224},{256,288},{320,352},{384,416},{... | collective-permute-start | bytes 98312 | tf_op jit(solution)/shard_map/ppermute | solution.py:420
  23.3 5.3 %collective-permute-start.18 = (f32[64,128]{1,0:T(8,128)S(1)}, f32[64,128]{1,0:T(8,128)}, u32[]{:S(2)}, u32[]{:S(2)}) collective-permute-start(f32[64,128]{1,0:T(8,128)S(1)} %param.12), channel_id=1, source_target_pairs={{32,64},{33,65},{34,66},{35,67},{36,68},{37,69},{38,70},{39,71},{4... | collective-permute-start | bytes 98312 | tf_op jit(solution)/shard_map/cond/branch_12_fun/ppermute | solution.py:429

commit v3 on v2

--- a/solution.py
+++ b/solution.py
@@ -13,6 +13,7 @@
 ROWS = 160
 LANES = 128
 EXT = ROWS + 32
+PITCH = 216
 EDGE = 9
 BLK = 40
 LON = ("lon_0", "lon_1")
@@ -153,10 +154,12 @@
 GROUPS = ROWS // 8 + 2
 
 
-def basis_kernel(x_ref, first_ref, second_ref, one_ref, two_hbm, basis_ref, sums_ref,
-                 depth, side, inv, coef, acc, fw_ref, fe_ref, fs_ref, fn_ref, two_ref, sem):
-    copy = pltpu.make_async_copy(two_hbm, two_ref, sem)
-    copy.start()
+def land_kernel(in_ref, out_ref):
+    out_ref[...] = in_ref[...]
+
+
+def basis_kernel(x_ref, first_ref, second_ref, one_ref, two_ref, basis_ref, sums_ref,
+                 depth, side, inv, coef, acc, fw_ref, fe_ref, fs_ref, fn_ref):
     sort_partners(LON, first_ref, second_ref, fw_ref, fe_ref)
     lane = lanes_of(8)
     zero = jnp.zeros((8, LANES), F32)
@@ -171,7 +174,6 @@
             own[pl.ds(16 + 8 * g, 8), :] = x_ref[q, pl.ds(8 * g, 8), :]
             blk, v = 8 * g // BLK, (8 * g % BLK) // 8
             rim[pl.ds(16 + 8 * g, 8), :] = unpack_halo(fw_ref, fe_ref, q, blk, v, lane)
-    copy.wait()
     sort_partners("lat", one_ref, two_ref, fs_ref, fn_ref)
     for q in range(3):
         own, rim = targets[q](0), targets[q](1)
@@ -194,7 +196,7 @@
         inv[t, pl.ds(0, 8), :] = zero
         inv[t, pl.ds(EXT - 8, 8), :] = zero
 
-    def root_of(g, carry):
+    def root_of(g):
         at = 8 + 8 * g
         vert, mid, wet_mid, deep = [], [], [], []
         for t in range(2):
@@ -216,11 +218,8 @@
             links = 0.5 * (deep[t] * sums[1][t] + sums[0][t])
             diagonal = wet_mid[t] * (deep[t] / (REACH * REACH) + links) + (1.0 - wet_mid[t])
             inv[t, pl.ds(at, 8), :] = lax.rsqrt(diagonal) * wet_mid[t]
-        return carry
-
-    lax.fori_loop(0, GROUPS, root_of, 0, unroll=2)
-
-    def coefs_of(g, carry):
+
+    def coefs_of(g):
         at = 8 + 8 * g
         d = [[depth[t, pl.ds(at + s, 8), :] for s in (-1, 0, 1)] for t in range(2)]
         r = [[inv[t, pl.ds(at + s, 8), :] for s in (-1, 0, 1)] for t in range(2)]
@@ -234,9 +233,11 @@
                     whole = base == 0 or s == 1
                     c = (dc + d[t][s]) * (rc * r[t][s])
                     coef[t, 3 * base + s, pl.ds(at, 8), :] = c * (-1.0 if whole else -0.5)
-        return carry
-
-    lax.fori_loop(0, GROUPS, coefs_of, 0, unroll=2)
+
+    for g in range(GROUPS):
+        root_of(g)
+    for g in range(GROUPS):
+        coefs_of(g)
 
     def twice_applied(k, at, tiles, weights):
         parts = []
@@ -334,8 +335,11 @@
     high = jnp.where(total == 2 * STEPS, 8 * (STEPS - 1) + 3, 8 * (total >> 1) + slot)
     gram = gathered(high) + gathered(8 * (apart >> 1) + slot) - gathered(slot)
 
-    lead_r = (row == 0) | (row == half)
+    lead_r, lead_c = (row == 0) | (row == half), (col == 0) | (col == half)
     tail_r = (row == STEPS) | (row >= VECTORS - 1)
+    tail_c = (col == STEPS) | (col >= VECTORS - 1)
+    mapped = jnp.where(tail_c, 0.0, gram + jnp.where(lead_c, 1.0, 0.5) * pltpu.roll(gram, LANES - 1, 1)
+                       + jnp.where(lead_c, 0.0, 0.5) * pltpu.roll(gram, 1, 1))
     same = (row_p == col_p) & inside & ~tail_r
     h_turned = jnp.where(same & (row == col), 1.0, 0.0)
     h_turned = h_turned + jnp.where(same & (col == row + 1), jnp.where(lead_r, 1.0, 0.5), 0.0)
@@ -344,26 +348,27 @@
     to_next = jnp.where(tail_r, 0.0, jnp.where(lead_r, 1.0, 0.5))
     to_last = jnp.where(tail_r | lead_r, 0.0, 0.5)
 
-    def as_row(matrix, column):
-        return jnp.sum(matrix * column, axis=0, keepdims=True)
-
-    def dot(a, b):
-        return jnp.sum(a * b, axis=1, keepdims=True)
+    def down(value):
+        return jnp.sum(value, axis=0, keepdims=True)
 
     xc = jnp.zeros((24, LANES), F32)
     pc, rc = jnp.where(row == 0, 1.0, 0.0), jnp.where(row == half, 1.0, 0.0)
-    pr, rr_row = jnp.where(col[:1] == 0, 1.0, 0.0), jnp.where(col[:1] == half, 1.0, 0.0)
-    norm = dot(as_row(gram, rc), rr_row)
+    p_row, r_row = jnp.where(col[:1] == 0, 1.0, 0.0), jnp.where(col[:1] == half, 1.0, 0.0)
+    gr = jnp.broadcast_to(jnp.sum(gram * r_row, axis=1, keepdims=True), (24, LANES))
+    norm = down(rc * gr)
     for _ in range(STEPS):
-        q_row = as_row(h_turned, pc)
+        z = jnp.broadcast_to(jnp.sum(mapped * p_row, axis=1, keepdims=True), (24, LANES))
+        q_row = down(h_turned * pc)
         q_col = keep * pc + pltpu.roll(to_next * pc, 1, 0) + pltpu.roll(to_last * pc, 23, 0)
-        t = norm / dot(as_row(gram, pc), q_row)
+        t = norm / down(pc * z)
         xc = xc + t * pc
         rc = rc - t * q_col
-        rr_row = rr_row - t * q_row
-        new = dot(as_row(gram, rc), rr_row)
+        r_row = r_row - t * q_row
+        gr = gr - t * z
+        new = down(rc * gr)
         ratio = new / norm
         pc = rc + ratio * pc
+        p_row = r_row + ratio * p_row
         norm = new
     xs = [jnp.broadcast_to(xc[k : k + 1, :], (8, LANES)) for k in range(VECTORS)]
     rs = [jnp.broadcast_to(rc[k : k + 1, :], (8, LANES)) for k in range(VECTORS)]
@@ -429,27 +434,28 @@
         return lax.ppermute(value, ("lat",) + LON, swaps + fold)
 
     def branch(index):
-        if index % 2 == 0:
-            return lambda near, far: second_round(near, index // 2)
-        return lambda near, far: second_round(near, index // 2) + second_round(far, (index // 2 + 1) % (lon_count // 2))
+        def exchange(near, far):
+            value = second_round(near, index // 2)
+            if index % 2:
+                value = value + second_round(far, (index // 2 + 1) % (lon_count // 2))
+            return call(land_kernel, name="land", out_shape=shape(64, LANES), compiler_params=limit(2))(*held(value))
+
+        return exchange
 
     two = lax.switch(choice[0], [branch(i) for i in range(lon_count)], two, two_next)
 
     basis, sums = call(
         basis_kernel, name="basis",
-        out_shape=(shape(VECTORS, EXT, LANES), shape(lon_count, LANES)),
+        out_shape=(shape(VECTORS, PITCH, LANES), shape(lon_count, LANES)),
         scratch_shapes=[
-            pltpu.VMEM((2, EXT, LANES), F32),
-            pltpu.VMEM((VECTORS, EXT, LANES), F32),
-            pltpu.VMEM((2, EXT, LANES), F32),
-            pltpu.VMEM((2, 9, EXT, LANES), F32),
+            pltpu.VMEM((2, PITCH, LANES), F32),
+            pltpu.VMEM((VECTORS, PITCH, LANES), F32),
+            pltpu.VMEM((2, PITCH, LANES), F32),
+            pltpu.VMEM((2, 9, PITCH, LANES), F32),
             pltpu.VMEM((STEPS, 8, 8, LANES), F32),
-        ] + [pltpu.VMEM((BLK + 32, LANES), F32)] * 2 + [pltpu.VMEM((64, LANES), F32)] * 3 + [
-            pltpu.SemaphoreType.DMA,
-        ],
-        in_specs=[pl.BlockSpec(memory_space=pltpu.VMEM)] * 4 + [pl.BlockSpec(memory_space=pl.ANY)],
+        ] + [pltpu.VMEM((BLK + 32, LANES), F32)] * 2 + [pltpu.VMEM((64, LANES), F32)] * 2,
         compiler_params=limit(12),
-    )(*held(fields, first, second, one), *held(two, space=pltpu.HBM))
+    )(*held(fields, first, second, one, two))
     sums = lax.all_to_all(sums, LON, split_axis=0, concat_axis=0, tiled=True)
     sums = call(middle_kernel, name="middle", out_shape=shape(lat_count, LANES), compiler_params=limit(2))(*held(sums))
     sums = lax.all_to_all(sums, "lat", split_axis=0, concat_axis=0, tiled=True)

time: 69.6 us -> 65.8 us (0.945)
  Pallas kernels: 9.84 us -> 6.57 us
  blocking collectives: 32.6 us -> 31.7 us
    pallas_call x1 -> x2, Pallas kernels: 6.16 us -> 3.35 us  [the longest x1 3.35 us: per_device(): call(basis_kernel, name='basis', out_shape=(shape(VECTORS, PITCH, LANES),...]
    all_to_all x1, blocking collectives: 17.4 us -> 16.6 us  [per_device(): sums = lax.all_to_all(sums, 'lat', split_axis=0, concat_axis=0, tiled=True)]
where the time goes in v3:
time: 65.8 us; the launch traced here: 65.5 us
  blocking collectives  31.7 us (48%)
  starting transfers between devices  23 us (35%)
  Pallas kernels  6.57 us (10%)
  waiting for transfers between devices  3.45 us (5%)
  between operations  0.69 us (1%)
    all_to_all x1, blocking collectives, per_device(): sums = lax.all_to_all(sums, 'lat', split_axis=0, concat_axis=0, tiled=True)  16.6 us
    all_to_all x1, blocking collectives, per_device(): sums = lax.all_to_all(sums, LON, split_axis=0, concat_axis=0, tiled=True)  15.1 us
    ppermute x1, starting transfers between devices, per_device(): second = lax.ppermute(second, LON, wrap + [(b, a) for a, b in wrap])  12.2 us
    ppermute x1, starting transfers between devices, per_device(): lax.ppermute(first, LON, [(i, i + 1) for i in evens] + [(i + 1, i) for i...  3.94 us
    ppermute x1, starting transfers between devices, per_device(): lax.ppermute(one, 'lat', [(i, i + 1) for i in evens] + [(i + 1, i) for i...  3.73 us
    pallas_call x1, Pallas kernels, per_device(): call(basis_kernel, name='basis', out_shape=(shape(VECTORS, PITCH, LANES),...  3.35 us
    ppermute x1, starting transfers between devices, second_round(): return lax.ppermute(value, ('lat',) + LON, swaps + fold)  3.1 us
    ppermute x1, waiting for transfers between devices, second_round(): return lax.ppermute(value, ('lat',) + LON, swaps + fold)  2.12 us
  transfers between devices with their start and end apart: 4, of which 2 were waited for; matrix products, arithmetic and copies ran while one was open for 0% of the time, Pallas kernels for 0%

profile of v3, /device:TPU:1, one launch (start us, length us, event | category | flops | bytes accessed | tf_op | source)
XLA Modules:
  0.0 65.5 jit_solution(7748515429310834428)
XLA Ops:
  0.6 1.3 %pack.1 = (f32[3,160,128]{2,1,0:T(8,128)S(1)}, f32[72,128]{1,0:T(8,128)S(1)}, f32[72,128]{1,0:T(8,128)S(1)}, s32[1]{0:T(128)S(4)}, s32[1]{0:T(128)S(4)}) custom-call(f32[160,128]{1,0:T(8,128)} %f_hbm.1, f32[160,128]{1,0:T(8,128)} %p_hbm.1, f32[160,128]{1,0:T(8,128)} %d_hbm.1, s32[160,128]{1,0:T(8,128)} %m_hbm.1, s32[4096]{0:T(1024)} %map_hbm.1), custom_call_target="tpu_custom_call" | custom-call | tf_op jit(solution)/shard_map/pack/pallas_call | solution.py:400
  1.9 3.9 %collective-permute-start.48 = (f32[72,128]{1,0:T(8,128)S(1)}, f32[72,128]{1,0:T(8,128)S(1)}, u32[]{:S(2)}, u32[]{:S(2)}) collective-permute-start(f32[72,128]{1,0:T(8,128)S(1)} %get-tuple-element.158), channel_id=1, source_target_pairs={{0,1},{2,3},{4,5},{6,7},{8,9},{10,11},{12,13},{14,15},{16,17},{18,... | collective-permute-start | bytes 110600 | tf_op jit(solution)/shard_map/ppermute | solution.py:412
  5.8 12.2 %collective-permute-start.49 = (f32[72,128]{1,0:T(8,128)S(1)}, f32[72,128]{1,0:T(8,128)S(1)}, u32[]{:S(2)}, u32[]{:S(2)}) collective-permute-start(f32[72,128]{1,0:T(8,128)S(1)} %get-tuple-element.159), channel_id=1, source_target_pairs={{1,2},{3,4},{5,6},{7,8},{9,10},{11,12},{13,14},{15,16},{17,18},{19... | collective-permute-start | bytes 110600 | tf_op jit(solution)/shard_map/ppermute | solution.py:414
  18.0 0.0 collective-permute-done.48.first_ref
  18.1 1.3 %collective-permute-done.49.second_ref = f32[72,128]{1,0:T(8,128)S(1)} collective-permute-done((f32[72,128]{1,0:T(8,128)S(1)}, f32[72,128]{1,0:T(8,128)S(1)}, u32[]{:S(2)}, u32[]{:S(2)}) %collective-permute-start.49) | collective-permute-done | bytes 36896 | tf_op jit(solution)/shard_map/ppermute | solution.py:414
  19.4 0.1 turn.1
  19.5 3.7 %collective-permute-start.50 = (f32[64,128]{1,0:T(8,128)S(1)}, f32[64,128]{1,0:T(8,128)S(1)}, u32[]{:S(2)}, u32[]{:S(2)}) collective-permute-start(f32[64,128]{1,0:T(8,128)S(1)} %get-tuple-element.161), channel_id=1, source_target_pairs={{0,32},{64,96},{128,160},{192,224},{256,288},{320,352},{384,416},{... | collective-permute-start | bytes 98312 | tf_op jit(solution)/shard_map/ppermute | solution.py:425
  23.2 5.3 %conditional.1 = (f32[64,128]{1,0:T(8,128)S(1)}) conditional(s32[]{:T(128)} %bitcast, f32[64,128]{1,0:T(8,128)S(1)} %get-tuple-element.163, (f32[64,128]{1,0:T(8,128)S(1)}, f32[64,128]{1,0:T(8,128)S(1)}) %tuple.103, f32[64,128]{1,0:T(8,128)S(1)} %get-tuple-element.163, (f32[64,128]{1,0:T(8,128)S(1)}, ...), branch_computations={%region_0.0_spmd, %region_1.0_spmd, %region_2.0_spmd, %region_3.0_... | conditional | flops 8192 | bytes 360536 | solution.py:445
  23.3 3.1 %collective-permute-start.3 = (f32[64,128]{1,0:T(8,128)S(1)}, f32[64,128]{1,0:T(8,128)S(1)}, u32[]{:S(2)}, u32[]{:S(2)}) collective-permute-start(f32[64,128]{1,0:T(8,128)S(1)} %param.2), channel_id=1, source_target_pairs={{32,64},{33,65},{34,66},{35,67},{36,68},{37,69},{38,70},{39,71},{4... | collective-permute-start | bytes 98312 | tf_op jit(solution)/shard_map/cond/branch_2_fun/ppermute | solution.py:434
  26.4 2.1 %collective-permute-done.3.in_ref = f32[64,128]{1,0:T(8,128)S(1)} collective-permute-done((f32[64,128]{1,0:T(8,128)S(1)}, f32[64,128]{1,0:T(8,128)S(1)}, u32[]{:S(2)}, u32[]{:S(2)}) %collective-permute-start.3) | collective-permute-done | bytes 32800 | tf_op jit(solution)/shard_map/cond/branch_2_fun/ppermute | solution.py:434
  28.5 0.0 collective-permute-done.50.one_ref
  28.5 3.3 %basis.1 = (f32[17,216,128]{2,1,0:T(8,128)S(1)}, f32[32,128]{1,0:T(8,128)S(1)}) custom-call(f32[3,160,128]{2,1,0:T(8,128)S(1)} %get-tuple-element.157.x_ref, f32[72,128]{1,0:T(8,128)S(1)} %collective-permute-done.48.first_ref, f32[72,128]{1,0:T(8,128)S(1)} %collective-permute-done.49.second_ref, f32[64,128]{1,0:T(8,128)S(1)} %collective-permute-done.50.one_ref, ...), custom_call_target="tpu_custom_call" | custom-call | tf_op jit(solution)/shard_map/basis/pallas_call | solution.py:447
  31.8 15.1 %all_to_all.22 = f32[32,1,128]{2,1,0:T(1,128)S(1)} all-to-all(f32[32,1,128]{2,1,0:T(1,128)S(1)} %bitcast.12), channel_id=1, replica_groups=mesh['lat'=16,'lon_0'=8,'lon_1'=4] {'lon_0','lon_1'}, dimensions={0} | all-to-all | bytes 32768 | tf_op jit(solution)/shard_map/all_to_all | solution.py:459
  47.0 16.6 %all_to_all.23 = f32[16,1,128]{2,1,0:T(1,128)S(1)} all-to-all(f32[16,1,128]{2,1,0:T(1,128)S(1)} %bitcast.11), channel_id=1, replica_groups=mesh['lat'=16,'lon_0'=8,'lon_1'=4] {'lat'}, dimensions={0} | all-to-all | bytes 16384 | tf_op jit(solution)/shard_map/all_to_all | solution.py:461
  63.6 1.9 %final.1 = (f32[160,128]{1,0:T(8,128)}, f32[160,128]{1,0:T(8,128)}) custom-call(f32[16,128]{1,0:T(8,128)S(1)} %bitcast.10, f32[17,216,128]{2,1,0:T(8,128)S(1)} %get-tuple-element.166.basis_ref), custom_call_target="tpu_custom_call" | custom-call | tf_op jit(solution)/shard_map/final/pallas_call | solution.py:462
  (2 shorter events, 0.0 us)
Async XLA Ops:
  1.9 16.2 %collective-permute-start.48 = (f32[72,128]{1,0:T(8,128)S(1)}, f32[72,128]{1,0:T(8,128)S(1)}, u32[]{:S(2)}, u32[]{:S(2)}) collective-permute-start(f32[72,128]{1,0:T(8,128)S(1)} %get-tuple-element.158), channel_id=1, source_target_pairs={{0,1},{2,3},{4,5},{6,7},{8,9},{10,11},{12,13},{14,15},{16,17},{18,... | collective-permute-start | bytes 110600 | tf_op jit(solution)/shard_map/ppermute | solution.py:412
  5.8 13.5 %collective-permute-start.49 = (f32[72,128]{1,0:T(8,128)S(1)}, f32[72,128]{1,0:T(8,128)S(1)}, u32[]{:S(2)}, u32[]{:S(2)}) collective-permute-start(f32[72,128]{1,0:T(8,128)S(1)} %get-tuple-element.159), channel_id=1, source_target_pairs={{1,2},{3,4},{5,6},{7,8},{9,10},{11,12},{13,14},{15,16},{17,18},{19... | collective-permute-start | bytes 110600 | tf_op jit(solution)/shard_map/ppermute | solution.py:414
  19.5 9.0 %collective-permute-start.50 = (f32[64,128]{1,0:T(8,128)S(1)}, f32[64,128]{1,0:T(8,128)S(1)}, u32[]{:S(2)}, u32[]{:S(2)}) collective-permute-start(f32[64,128]{1,0:T(8,128)S(1)} %get-tuple-element.161), channel_id=1, source_target_pairs={{0,32},{64,96},{128,160},{192,224},{256,288},{320,352},{384,416},{... | collective-permute-start | bytes 98312 | tf_op jit(solution)/shard_map/ppermute | solution.py:425
  23.3 5.2 %collective-permute-start.3 = (f32[64,128]{1,0:T(8,128)S(1)}, f32[64,128]{1,0:T(8,128)S(1)}, u32[]{:S(2)}, u32[]{:S(2)}) collective-permute-start(f32[64,128]{1,0:T(8,128)S(1)} %param.2), channel_id=1, source_target_pairs={{32,64},{33,65},{34,66},{35,67},{36,68},{37,69},{38,70},{39,71},{4... | collective-permute-start | bytes 98312 | tf_op jit(solution)/shard_map/cond/branch_2_fun/ppermute | solution.py:434

commit v4 on v3

--- a/solution.py
+++ b/solution.py
@@ -98,7 +98,7 @@
         after[rows, :] = jnp.where(even, a, b)
 
 
-def turn_kernel(tops, r_ref, x_ref, first_ref, second_ref, one_ref, two_ref, next_ref,
+def turn_kernel(tops, r_ref, x_ref, second_ref, first_ref, one_ref, two_ref, next_ref,
                 fw_ref, fe_ref, north_ref, south_ref, t1_ref, t2_ref):
     lane = lanes_of(8)
     lat = lax.axis_index("lat")
@@ -154,12 +154,12 @@
 GROUPS = ROWS // 8 + 2
 
 
-def land_kernel(in_ref, out_ref):
-    out_ref[...] = in_ref[...]
-
-
-def basis_kernel(x_ref, first_ref, second_ref, one_ref, two_ref, basis_ref, sums_ref,
-                 depth, side, inv, coef, acc, fw_ref, fe_ref, fs_ref, fn_ref):
+def land_kernel(two_ref, one_ref, south_ref, north_ref):
+    sort_partners("lat", one_ref, two_ref, south_ref, north_ref)
+
+
+def basis_kernel(x_ref, second_ref, first_ref, fs_ref, fn_ref, basis_ref, sums_ref,
+                 depth, side, inv, coef, acc, fw_ref, fe_ref):
     sort_partners(LON, first_ref, second_ref, fw_ref, fe_ref)
     lane = lanes_of(8)
     zero = jnp.zeros((8, LANES), F32)
@@ -174,7 +174,6 @@
             own[pl.ds(16 + 8 * g, 8), :] = x_ref[q, pl.ds(8 * g, 8), :]
             blk, v = 8 * g // BLK, (8 * g % BLK) // 8
             rim[pl.ds(16 + 8 * g, 8), :] = unpack_halo(fw_ref, fe_ref, q, blk, v, lane)
-    sort_partners("lat", one_ref, two_ref, fs_ref, fn_ref)
     for q in range(3):
         own, rim = targets[q](0), targets[q](1)
         for t, ref in ((0, own), (1, rim)):
@@ -409,9 +408,9 @@
         compiler_params=limit(4),
     )(*held(forcing, search_direction, ocean_depth, land_mask, fold_map, space=pltpu.HBM))
     evens, odds = range(0, lon_count, 2), range(1, lon_count, 2)
-    first = lax.ppermute(first, LON, [(i, i + 1) for i in evens] + [(i + 1, i) for i in evens])
     wrap = [(i, (i + 1) % lon_count) for i in odds]
     second = lax.ppermute(second, LON, wrap + [(b, a) for a, b in wrap])
+    first = lax.ppermute(first, LON, [(i, i + 1) for i in evens] + [(i + 1, i) for i in evens])
 
     one, two, two_next = call(
         functools.partial(turn_kernel, lat_count - 1), name="turn",
@@ -419,10 +418,10 @@
         out_shape=(shape(64, LANES),) * 3,
         scratch_shapes=[pltpu.VMEM((BLK + 32, LANES), F32)] * 2 + [pltpu.VMEM((64, LANES), F32)] * 4,
         compiler_params=limit(4),
-    )(reach, *held(fields, first, second))
+    )(reach, *held(fields, second, first))
 
     evens, odds = range(0, lat_count, 2), range(1, lat_count - 1, 2)
-    one = lax.ppermute(one, "lat", [(i, i + 1) for i in evens] + [(i + 1, i) for i in evens])
+    pairs = [(i, i + 1) for i in evens] + [(i + 1, i) for i in evens]
     swaps = [
         (i * lon_count + c, (i + s) * lon_count + c)
         for k in odds for i, s in ((k, 1), (k + 1, -1)) for c in range(lon_count)
@@ -434,15 +433,18 @@
         return lax.ppermute(value, ("lat",) + LON, swaps + fold)
 
     def branch(index):
-        def exchange(near, far):
+        def exchange(one, near, far):
             value = second_round(near, index // 2)
             if index % 2:
                 value = value + second_round(far, (index // 2 + 1) % (lon_count // 2))
-            return call(land_kernel, name="land", out_shape=shape(64, LANES), compiler_params=limit(2))(*held(value))
+            one = lax.ppermute(one, "lat", pairs)
+            return call(
+                land_kernel, name="land", out_shape=(shape(64, LANES),) * 2, compiler_params=limit(2),
+            )(*held(value, one))
 
         return exchange
 
-    two = lax.switch(choice[0], [branch(i) for i in range(lon_count)], two, two_next)
+    south, north = lax.switch(choice[0], [branch(i) for i in range(lon_count)], one, two, two_next)
 
     basis, sums = call(
         basis_kernel, name="basis",
@@ -453,9 +455,9 @@
             pltpu.VMEM((2, PITCH, LANES), F32),
             pltpu.VMEM((2, 9, PITCH, LANES), F32),
             pltpu.VMEM((STEPS, 8, 8, LANES), F32),
-        ] + [pltpu.VMEM((BLK + 32, LANES), F32)] * 2 + [pltpu.VMEM((64, LANES), F32)] * 2,
+        ] + [pltpu.VMEM((BLK + 32, LANES), F32)] * 2,
         compiler_params=limit(12),
-    )(*held(fields, first, second, one, two))
+    )(*held(fields, second, first, south, north))
     sums = lax.all_to_all(sums, LON, split_axis=0, concat_axis=0, tiled=True)
     sums = call(middle_kernel, name="middle", out_shape=shape(lat_count, LANES), compiler_params=limit(2))(*held(sums))
     sums = lax.all_to_all(sums, "lat", split_axis=0, concat_axis=0, tiled=True)

time: 65.8 us -> 61.9 us (0.941)
  blocking collectives: 31.7 us -> 27.3 us
    all_to_all x1, blocking collectives: 15.1 us -> 11.6 us  [per_device(): sums = lax.all_to_all(sums, LON, split_axis=0, concat_axis=0, tiled=True)]
    ppermute x1, waiting for transfers between devices: 0.01 us -> 2.76 us  [per_device(): lax.ppermute(first, LON, [(i, i + 1) for i in evens] + [(i + 1, i) for i...]
    ppermute x1, waiting for transfers between devices: 2.12 us -> 0.01 us  [second_round(): return lax.ppermute(value, ('lat',) + LON, swaps + fold)]
    ppermute x1, starting transfers between devices: 3.1 us -> 5.19 us  [second_round(): return lax.ppermute(value, ('lat',) + LON, swaps + fold)]
    ppermute x1, starting transfers between devices: 3.94 us -> 1.92 us  [per_device(): lax.ppermute(first, LON, [(i, i + 1) for i in evens] + [(i + 1, i) for i...]
    ppermute x1, starting transfers between devices: 3.73 us -> 1.92 us  [exchange(): one = lax.ppermute(one, 'lat', pairs)]
    ppermute x1, starting transfers between devices: 12.2 us -> 13.7 us  [per_device(): second = lax.ppermute(second, LON, wrap + [(b, a) for a, b in wrap])]
    ppermute x1, waiting for transfers between devices: 1.32 us -> 0.01 us  [per_device(): second = lax.ppermute(second, LON, wrap + [(b, a) for a, b in wrap])]
where the time goes in v4:
time: 61.9 us; the launch traced here: 61.3 us
  blocking collectives  27.3 us (44%)
  starting transfers between devices  22.7 us (37%)
  Pallas kernels  6.58 us (11%)
  waiting for transfers between devices  3.93 us (6%)
  between operations  0.68 us (1%)
    all_to_all x1, blocking collectives, per_device(): sums = lax.all_to_all(sums, 'lat', split_axis=0, concat_axis=0, tiled=True)  15.7 us
    ppermute x1, starting transfers between devices, per_device(): second = lax.ppermute(second, LON, wrap + [(b, a) for a, b in wrap])  13.7 us
    all_to_all x1, blocking collectives, per_device(): sums = lax.all_to_all(sums, LON, split_axis=0, concat_axis=0, tiled=True)  11.6 us
    ppermute x1, starting transfers between devices, second_round(): return lax.ppermute(value, ('lat',) + LON, swaps + fold)  5.19 us
    pallas_call x1, Pallas kernels, per_device(): call(basis_kernel, name='basis', out_shape=(shape(VECTORS, PITCH, LANES),...  3.35 us
    ppermute x1, waiting for transfers between devices, per_device(): lax.ppermute(first, LON, [(i, i + 1) for i in evens] + [(i + 1, i) for i...  2.76 us
    ppermute x1, starting transfers between devices, per_device(): lax.ppermute(first, LON, [(i, i + 1) for i in evens] + [(i + 1, i) for i...  1.92 us
    ppermute x1, starting transfers between devices, exchange(): one = lax.ppermute(one, 'lat', pairs)  1.92 us
  transfers between devices with their start and end apart: 4, of which 2 were waited for; matrix products, arithmetic and copies ran while one was open for 0% of the time, Pallas kernels for 0%

profile of v4, /device:TPU:1, one launch (start us, length us, event | category | flops | bytes accessed | tf_op | source)
XLA Modules:
  0.0 61.3 jit_solution(6239257784399971605)
XLA Ops:
  0.6 1.3 %pack.1 = (f32[3,160,128]{2,1,0:T(8,128)S(1)}, f32[72,128]{1,0:T(8,128)S(1)}, f32[72,128]{1,0:T(8,128)S(1)}, s32[1]{0:T(128)S(4)}, s32[1]{0:T(128)S(4)}) custom-call(f32[160,128]{1,0:T(8,128)} %f_hbm.1, f32[160,128]{1,0:T(8,128)} %p_hbm.1, f32[160,128]{1,0:T(8,128)} %d_hbm.1, s32[160,128]{1,0:T(8,128)} %m_hbm.1, s32[4096]{0:T(1024)} %map_hbm.1), custom_call_target="tpu_custom_call" | custom-call | tf_op jit(solution)/shard_map/pack/pallas_call | solution.py:399
  1.9 13.7 %collective-permute-start.80 = (f32[72,128]{1,0:T(8,128)S(1)}, f32[72,128]{1,0:T(8,128)S(1)}, u32[]{:S(2)}, u32[]{:S(2)}) collective-permute-start(f32[72,128]{1,0:T(8,128)S(1)} %get-tuple-element.255), channel_id=1, source_target_pairs={{1,2},{3,4},{5,6},{7,8},{9,10},{11,12},{13,14},{15,16},{17,18},{19... | collective-permute-start | bytes 110600 | tf_op jit(solution)/shard_map/ppermute | solution.py:412
  15.6 1.9 %collective-permute-start.81 = (f32[72,128]{1,0:T(8,128)S(1)}, f32[72,128]{1,0:T(8,128)S(1)}, u32[]{:S(2)}, u32[]{:S(2)}) collective-permute-start(f32[72,128]{1,0:T(8,128)S(1)} %get-tuple-element.256), channel_id=1, source_target_pairs={{0,1},{2,3},{4,5},{6,7},{8,9},{10,11},{12,13},{14,15},{16,17},{18,... | collective-permute-start | bytes 110600 | tf_op jit(solution)/shard_map/ppermute | solution.py:413
  17.5 0.0 collective-permute-done.80.second_ref
  17.5 2.8 %collective-permute-done.81.first_ref = f32[72,128]{1,0:T(8,128)S(1)} collective-permute-done((f32[72,128]{1,0:T(8,128)S(1)}, f32[72,128]{1,0:T(8,128)S(1)}, u32[]{:S(2)}, u32[]{:S(2)}) %collective-permute-start.81) | collective-permute-done | bytes 36896 | tf_op jit(solution)/shard_map/ppermute | solution.py:413
  20.3 0.1 turn.1
  20.4 8.4 %conditional.1 = ((f32[64,128]{1,0:T(8,128)S(1)}, f32[64,128]{1,0:T(8,128)S(1)})) conditional(s32[]{:T(128)} %bitcast, (f32[64,128]{1,0:T(8,128)S(1)}, f32[64,128]{1,0:T(8,128)S(1)}) %tuple.103, (f32[64,128]{1,0:T(8,128)S(1)}, f32[64,128]{1,0:T(8,128)S(1)}, f32[64,128]{1,0:T(8,128)S(1)}) %tuple.104, ...), branch_computations={%region_0.0_spmd, %region_1.0_spmd, %region_2.0_spmd, %region_3.0_... | conditional | flops 8192 | bytes 491648 | solution.py:447
  20.4 5.2 %collective-permute-start.50 = (f32[64,128]{1,0:T(8,128)S(1)}, f32[64,128]{1,0:T(8,128)S(1)}, u32[]{:S(2)}, u32[]{:S(2)}) collective-permute-start(f32[64,128]{1,0:T(8,128)S(1)} %get-tuple-element.210), channel_id=1, source_target_pairs={{32,64},{33,65},{34,66},{35,67},{36,68},{37,69},{38,70},{39,71},{4... | collective-permute-start | bytes 98312 | tf_op jit(solution)/shard_map/cond/branch_20_fun/ppermute | solution.py:433
  25.6 1.9 %collective-permute-start.51 = (f32[64,128]{1,0:T(8,128)S(1)}, f32[64,128]{1,0:T(8,128)S(1)}, u32[]{:S(2)}, u32[]{:S(2)}) collective-permute-start(f32[64,128]{1,0:T(8,128)S(1)} %get-tuple-element.211), channel_id=1, source_target_pairs={{0,32},{64,96},{128,160},{192,224},{256,288},{320,352},{384,416},{... | collective-permute-start | bytes 98312 | tf_op jit(solution)/shard_map/cond/branch_20_fun/ppermute | solution.py:440
  27.6 0.0 collective-permute-done.50.two_ref
  27.6 1.2 %collective-permute-done.51.one_ref = f32[64,128]{1,0:T(8,128)S(1)} collective-permute-done((f32[64,128]{1,0:T(8,128)S(1)}, f32[64,128]{1,0:T(8,128)S(1)}, u32[]{:S(2)}, u32[]{:S(2)}) %collective-permute-start.51) | collective-permute-done | bytes 32800 | tf_op jit(solution)/shard_map/cond/branch_20_fun/ppermute | solution.py:440
  28.8 3.4 %basis.1 = (f32[17,216,128]{2,1,0:T(8,128)S(1)}, f32[32,128]{1,0:T(8,128)S(1)}) custom-call(f32[3,160,128]{2,1,0:T(8,128)S(1)} %get-tuple-element.254.x_ref, f32[72,128]{1,0:T(8,128)S(1)} %collective-permute-done.80.second_ref, f32[72,128]{1,0:T(8,128)S(1)} %collective-permute-done.81.first_ref, f32[64,128]{1,0:T(8,128)S(1)} %get-tuple-element.262.fs_ref, ...), custom_call_target="tpu_custom_call" | custom-call | tf_op jit(solution)/shard_map/basis/pallas_call | solution.py:449
  32.1 11.6 %all_to_all.22 = f32[32,1,128]{2,1,0:T(1,128)S(1)} all-to-all(f32[32,1,128]{2,1,0:T(1,128)S(1)} %bitcast.12), channel_id=1, replica_groups=mesh['lat'=16,'lon_0'=8,'lon_1'=4] {'lon_0','lon_1'}, dimensions={0} | all-to-all | bytes 32768 | tf_op jit(solution)/shard_map/all_to_all | solution.py:461
  43.7 15.7 %all_to_all.23 = f32[16,1,128]{2,1,0:T(1,128)S(1)} all-to-all(f32[16,1,128]{2,1,0:T(1,128)S(1)} %bitcast.11), channel_id=1, replica_groups=mesh['lat'=16,'lon_0'=8,'lon_1'=4] {'lat'}, dimensions={0} | all-to-all | bytes 16384 | tf_op jit(solution)/shard_map/all_to_all | solution.py:463
  59.5 1.9 %final.1 = (f32[160,128]{1,0:T(8,128)}, f32[160,128]{1,0:T(8,128)}) custom-call(f32[16,128]{1,0:T(8,128)S(1)} %bitcast.10, f32[17,216,128]{2,1,0:T(8,128)S(1)} %get-tuple-element.265.basis_ref), custom_call_target="tpu_custom_call" | custom-call | tf_op jit(solution)/shard_map/final/pallas_call | solution.py:464
  (2 shorter events, 0.0 us)
Async XLA Ops:
  1.9 15.6 %collective-permute-start.80 = (f32[72,128]{1,0:T(8,128)S(1)}, f32[72,128]{1,0:T(8,128)S(1)}, u32[]{:S(2)}, u32[]{:S(2)}) collective-permute-start(f32[72,128]{1,0:T(8,128)S(1)} %get-tuple-element.255), channel_id=1, source_target_pairs={{1,2},{3,4},{5,6},{7,8},{9,10},{11,12},{13,14},{15,16},{17,18},{19... | collective-permute-start | bytes 110600 | tf_op jit(solution)/shard_map/ppermute | solution.py:412
  15.6 4.7 %collective-permute-start.81 = (f32[72,128]{1,0:T(8,128)S(1)}, f32[72,128]{1,0:T(8,128)S(1)}, u32[]{:S(2)}, u32[]{:S(2)}) collective-permute-start(f32[72,128]{1,0:T(8,128)S(1)} %get-tuple-element.256), channel_id=1, source_target_pairs={{0,1},{2,3},{4,5},{6,7},{8,9},{10,11},{12,13},{14,15},{16,17},{18,... | collective-permute-start | bytes 110600 | tf_op jit(solution)/shard_map/ppermute | solution.py:413
  20.4 7.1 %collective-permute-start.50 = (f32[64,128]{1,0:T(8,128)S(1)}, f32[64,128]{1,0:T(8,128)S(1)}, u32[]{:S(2)}, u32[]{:S(2)}) collective-permute-start(f32[64,128]{1,0:T(8,128)S(1)} %get-tuple-element.210), channel_id=1, source_target_pairs={{32,64},{33,65},{34,66},{35,67},{36,68},{37,69},{38,70},{39,71},{4... | collective-permute-start | bytes 98312 | tf_op jit(solution)/shard_map/cond/branch_20_fun/ppermute | solution.py:433
  25.6 3.1 %collective-permute-start.51 = (f32[64,128]{1,0:T(8,128)S(1)}, f32[64,128]{1,0:T(8,128)S(1)}, u32[]{:S(2)}, u32[]{:S(2)}) collective-permute-start(f32[64,128]{1,0:T(8,128)S(1)} %get-tuple-element.211), channel_id=1, source_target_pairs={{0,32},{64,96},{128,160},{192,224},{256,288},{320,352},{384,416},{... | collective-permute-start | bytes 98312 | tf_op jit(solution)/shard_map/cond/branch_20_fun/ppermute | solution.py:440

commit v5 on v4

--- a/solution.py
+++ b/solution.py
@@ -154,26 +154,91 @@
 GROUPS = ROWS // 8 + 2
 
 
+def root_of(depth, inv, at, lane):
+    vert, mid, wet_mid, deep = [], [], [], []
+    for t in range(2):
+        down = depth[t, pl.ds(at - 1, 8), :]
+        here = depth[t, pl.ds(at, 8), :]
+        up = depth[t, pl.ds(at + 1, 8), :]
+        wet = jnp.where(here > 0.0, 1.0, 0.0)
+        wets = jnp.where(down > 0.0, 1.0, 0.0) + jnp.where(up > 0.0, 1.0, 0.0)
+        vert.append((down + up, wets))
+        mid.append((here + 0.5 * (down + up), wet + 0.5 * wets))
+        deep.append(here)
+        wet_mid.append(wet)
+    sums = []
+    for c in range(2):
+        ea, eb = shift_east(mid[0][c], mid[1][c], lane)
+        wa, wb = shift_west(mid[0][c], mid[1][c], lane)
+        sums.append((vert[0][c] + (ea + wa), vert[1][c] + (eb + wb)))
+    for t in range(2):
+        links = 0.5 * (deep[t] * sums[1][t] + sums[0][t])
+        diagonal = wet_mid[t] * (deep[t] / (REACH * REACH) + links) + (1.0 - wet_mid[t])
+        inv[t, pl.ds(at, 8), :] = lax.rsqrt(diagonal) * wet_mid[t]
+
+
+def coefs_of(depth, inv, coef, at, lane):
+    d = [[depth[t, pl.ds(at + s, 8), :] for s in (-1, 0, 1)] for t in range(2)]
+    r = [[inv[t, pl.ds(at + s, 8), :] for s in (-1, 0, 1)] for t in range(2)]
+    de, re = shift_east(d[0][1], d[1][1], lane), shift_east(r[0][1], r[1][1], lane)
+    dw, rw = shift_west(d[0][1], d[1][1], lane), shift_west(r[0][1], r[1][1], lane)
+    for t in range(2):
+        for base, (dc, rc) in enumerate(((d[t][1], r[t][1]), (de[t], re[t]), (dw[t], rw[t]))):
+            for s in range(3):
+                if base == 0 and s == 1:
+                    continue
+                whole = base == 0 or s == 1
+                c = (dc + d[t][s]) * (rc * r[t][s])
+                coef[t, 3 * base + s, pl.ds(at, 8), :] = c * (-1.0 if whole else -0.5)
+
+
+def prepare_kernel(x_ref, second_ref, first_ref, depth, side, inv, coef, fw_ref, fe_ref):
+    sort_partners(LON, first_ref, second_ref, fw_ref, fe_ref)
+    lane = lanes_of(8)
+
+    def unpack(v, carry):
+        for q, ref in ((0, depth.at[1]), (1, side.at[1]), (2, side.at[0])):
+            for blk in range(4):
+                rows = pl.ds(pl.multiple_of(16 + BLK * blk + 8 * v, 8), 8)
+                ref[rows, :] = unpack_halo(fw_ref, fe_ref, q, blk, v, lane)
+        return carry
+
+    for g in range(ROWS // 8):
+        depth[0, pl.ds(16 + 8 * g, 8), :] = x_ref[0, pl.ds(8 * g, 8), :]
+    lax.fori_loop(0, BLK // 8, unpack, 0)
+
+    def roots(i, carry):
+        for g in range(6):
+            root_of(depth, inv, pl.multiple_of(24 + 48 * i, 8) + 8 * g, lane)
+        return carry
+
+    def coefs(i, carry):
+        for g in range(4):
+            coefs_of(depth, inv, coef, pl.multiple_of(32 + 32 * i, 8) + 8 * g, lane)
+        return carry
+
+    lax.fori_loop(0, 3, roots, 0)
+    lax.fori_loop(0, 4, coefs, 0)
+
+
 def land_kernel(two_ref, one_ref, south_ref, north_ref):
     sort_partners("lat", one_ref, two_ref, south_ref, north_ref)
 
 
-def basis_kernel(x_ref, second_ref, first_ref, fs_ref, fn_ref, basis_ref, sums_ref,
-                 depth, side, inv, coef, acc, fw_ref, fe_ref):
-    sort_partners(LON, first_ref, second_ref, fw_ref, fe_ref)
+def basis_kernel(x_ref, side_ref, _depth, _inv, _coef, fs_ref, fn_ref, basis_ref, sums_ref, depth, inv, coef,
+                 side, acc):
     lane = lanes_of(8)
     zero = jnp.zeros((8, LANES), F32)
+    for q, k in ((1, STEPS + 1), (2, 0)):
+        for g in range(ROWS // 8):
+            rows = pl.ds(16 + 8 * g, 8)
+            basis_ref[k, rows, :] = x_ref[q, pl.ds(8 * g, 8), :]
+            side[k, rows, :] = side_ref[2 - q, rows, :]
     targets = (
         lambda t: depth.at[t],
         lambda t: (basis_ref if t == 0 else side).at[STEPS + 1],
         lambda t: (basis_ref if t == 0 else side).at[0],
     )
-    for q in range(3):
-        own, rim = targets[q](0), targets[q](1)
-        for g in range(ROWS // 8):
-            own[pl.ds(16 + 8 * g, 8), :] = x_ref[q, pl.ds(8 * g, 8), :]
-            blk, v = 8 * g // BLK, (8 * g % BLK) // 8
-            rim[pl.ds(16 + 8 * g, 8), :] = unpack_halo(fw_ref, fe_ref, q, blk, v, lane)
     for q in range(3):
         own, rim = targets[q](0), targets[q](1)
         for t, ref in ((0, own), (1, rim)):
@@ -195,48 +260,10 @@
         inv[t, pl.ds(0, 8), :] = zero
         inv[t, pl.ds(EXT - 8, 8), :] = zero
 
-    def root_of(g):
-        at = 8 + 8 * g
-        vert, mid, wet_mid, deep = [], [], [], []
-        for t in range(2):
-            down = depth[t, pl.ds(at - 1, 8), :]
-            here = depth[t, pl.ds(at, 8), :]
-            up = depth[t, pl.ds(at + 1, 8), :]
-            wet = jnp.where(here > 0.0, 1.0, 0.0)
-            wets = jnp.where(down > 0.0, 1.0, 0.0) + jnp.where(up > 0.0, 1.0, 0.0)
-            vert.append((down + up, wets))
-            mid.append((here + 0.5 * (down + up), wet + 0.5 * wets))
-            deep.append(here)
-            wet_mid.append(wet)
-        sums = []
-        for c in range(2):
-            ea, eb = shift_east(mid[0][c], mid[1][c], lane)
-            wa, wb = shift_west(mid[0][c], mid[1][c], lane)
-            sums.append((vert[0][c] + (ea + wa), vert[1][c] + (eb + wb)))
-        for t in range(2):
-            links = 0.5 * (deep[t] * sums[1][t] + sums[0][t])
-            diagonal = wet_mid[t] * (deep[t] / (REACH * REACH) + links) + (1.0 - wet_mid[t])
-            inv[t, pl.ds(at, 8), :] = lax.rsqrt(diagonal) * wet_mid[t]
-
-    def coefs_of(g):
-        at = 8 + 8 * g
-        d = [[depth[t, pl.ds(at + s, 8), :] for s in (-1, 0, 1)] for t in range(2)]
-        r = [[inv[t, pl.ds(at + s, 8), :] for s in (-1, 0, 1)] for t in range(2)]
-        de, re = shift_east(d[0][1], d[1][1], lane), shift_east(r[0][1], r[1][1], lane)
-        dw, rw = shift_west(d[0][1], d[1][1], lane), shift_west(r[0][1], r[1][1], lane)
-        for t in range(2):
-            for base, (dc, rc) in enumerate(((d[t][1], r[t][1]), (de[t], re[t]), (dw[t], rw[t]))):
-                for s in range(3):
-                    if base == 0 and s == 1:
-                        continue
-                    whole = base == 0 or s == 1
-                    c = (dc + d[t][s]) * (rc * r[t][s])
-                    coef[t, 3 * base + s, pl.ds(at, 8), :] = c * (-1.0 if whole else -0.5)
-
-    for g in range(GROUPS):
-        root_of(g)
-    for g in range(GROUPS):
-        coefs_of(g)
+    for g in (0, 1, GROUPS - 2, GROUPS - 1):
+        root_of(depth, inv, 8 + 8 * g, lane)
+    for g in (0, 1, 2, GROUPS - 3, GROUPS - 2, GROUPS - 1):
+        coefs_of(depth, inv, coef, 8 + 8 * g, lane)
 
     def twice_applied(k, at, tiles, weights):
         parts = []
@@ -433,31 +460,41 @@
         return lax.ppermute(value, ("lat",) + LON, swaps + fold)
 
     def branch(index):
-        def exchange(one, near, far):
+        def exchange(one, near, far, fields, second, first):
             value = second_round(near, index // 2)
             if index % 2:
                 value = value + second_round(far, (index // 2 + 1) % (lon_count // 2))
             one = lax.ppermute(one, "lat", pairs)
-            return call(
+            ready = call(
+                prepare_kernel, name="prepare",
+                out_shape=(shape(2, PITCH, LANES), shape(2, PITCH, LANES), shape(2, PITCH, LANES),
+                           shape(2, 9, PITCH, LANES)),
+                scratch_shapes=[pltpu.VMEM((BLK + 32, LANES), F32)] * 2,
+                compiler_params=limit(4),
+                cost_estimate=pl.CostEstimate(flops=4_000_000, transcendentals=0, bytes_accessed=0),
+            )(*held(fields, second, first))
+            landed = call(
                 land_kernel, name="land", out_shape=(shape(64, LANES),) * 2, compiler_params=limit(2),
             )(*held(value, one))
+            return *ready, *landed
 
         return exchange
 
-    south, north = lax.switch(choice[0], [branch(i) for i in range(lon_count)], one, two, two_next)
-
-    basis, sums = call(
+    depth, side, inv, coef, south, north = lax.switch(
+        choice[0], [branch(i) for i in range(lon_count)], one, two, two_next, fields, second, first
+    )
+
+    basis, sums, *_ = call(
         basis_kernel, name="basis",
-        out_shape=(shape(VECTORS, PITCH, LANES), shape(lon_count, LANES)),
+        out_shape=(shape(VECTORS, PITCH, LANES), shape(lon_count, LANES), shape(2, PITCH, LANES),
+                   shape(2, PITCH, LANES), shape(2, 9, PITCH, LANES)),
         scratch_shapes=[
-            pltpu.VMEM((2, PITCH, LANES), F32),
             pltpu.VMEM((VECTORS, PITCH, LANES), F32),
-            pltpu.VMEM((2, PITCH, LANES), F32),
-            pltpu.VMEM((2, 9, PITCH, LANES), F32),
             pltpu.VMEM((STEPS, 8, 8, LANES), F32),
-        ] + [pltpu.VMEM((BLK + 32, LANES), F32)] * 2,
+        ],
+        input_output_aliases={2: 2, 3: 3, 4: 4},
         compiler_params=limit(12),
-    )(*held(fields, second, first, south, north))
+    )(*held(fields, side, depth, inv, coef, south, north))
     sums = lax.all_to_all(sums, LON, split_axis=0, concat_axis=0, tiled=True)
     sums = call(middle_kernel, name="middle", out_shape=shape(lat_count, LANES), compiler_params=limit(2))(*held(sums))
     sums = lax.all_to_all(sums, "lat", split_axis=0, concat_axis=0, tiled=True)

time: 61.9 us -> 61.1 us (0.987)
  waiting for transfers between devices: 3.93 us -> 2.77 us
  Pallas kernels: 6.58 us -> 7.5 us
    pallas_call x0 -> x1, Pallas kernels: none -> 1.33 us  [exchange(): call(prepare_kernel, name='prepare', out_shape=(shape(2, PITCH, LANES), s...]
    ppermute x1, waiting for transfers between devices: 1.16 us -> 0.01 us  [exchange(): one = lax.ppermute(one, 'lat', pairs)]
  transfers between devices with their start and end apart: 4 -> 4, of which waited for: 2 -> 1; matrix products, arithmetic and copies ran while one was open for 0% -> 0% of each run, Pallas kernels for 0% -> 2%
where the time goes in v5:
time: 61.1 us; the launch traced here: 60.5 us
  blocking collectives  26.7 us (44%)
  starting transfers between devices  22.7 us (37%)
  Pallas kernels  7.5 us (12%)
  waiting for transfers between devices  2.77 us (5%)
  between operations  0.68 us (1%)
    all_to_all x1, blocking collectives, per_device(): sums = lax.all_to_all(sums, 'lat', split_axis=0, concat_axis=0, tiled=True)  15.1 us
    ppermute x1, starting transfers between devices, per_device(): second = lax.ppermute(second, LON, wrap + [(b, a) for a, b in wrap])  13.7 us
    all_to_all x1, blocking collectives, per_device(): sums = lax.all_to_all(sums, LON, split_axis=0, concat_axis=0, tiled=True)  11.6 us
    ppermute x1, starting transfers between devices, second_round(): return lax.ppermute(value, ('lat',) + LON, swaps + fold)  5.19 us
    pallas_call x1, Pallas kernels, per_device(): call(basis_kernel, name='basis', out_shape=(shape(VECTORS, PITCH, LANES),...  2.93 us
    ppermute x1, waiting for transfers between devices, per_device(): lax.ppermute(first, LON, [(i, i + 1) for i in evens] + [(i + 1, i) for i...  2.76 us
    ppermute x1, starting transfers between devices, per_device(): lax.ppermute(first, LON, [(i, i + 1) for i in evens] + [(i + 1, i) for i...  1.92 us
    ppermute x1, starting transfers between devices, exchange(): one = lax.ppermute(one, 'lat', pairs)  1.92 us
  transfers between devices with their start and end apart: 4, of which 1 were waited for; matrix products, arithmetic and copies ran while one was open for 0% of the time, Pallas kernels for 2%

profile of v5, /device:TPU:1, one launch (start us, length us, event | category | flops | bytes accessed | tf_op | source)
XLA Modules:
  0.0 60.5 jit_solution(5110304822767621259)
XLA Ops:
  0.6 1.3 %pack.1 = (f32[3,160,128]{2,1,0:T(8,128)S(1)}, f32[72,128]{1,0:T(8,128)S(1)}, f32[72,128]{1,0:T(8,128)S(1)}, s32[1]{0:T(128)S(4)}, s32[1]{0:T(128)S(4)}) custom-call(f32[160,128]{1,0:T(8,128)} %f_hbm.1, f32[160,128]{1,0:T(8,128)} %p_hbm.1, f32[160,128]{1,0:T(8,128)} %d_hbm.1, s32[160,128]{1,0:T(8,128)} %m_hbm.1, s32[4096]{0:T(1024)} %map_hbm.1), custom_call_target="tpu_custom_call" | custom-call | tf_op jit(solution)/shard_map/pack/pallas_call | solution.py:426
  1.9 13.7 %collective-permute-start.80 = (f32[72,128]{1,0:T(8,128)S(1)}, f32[72,128]{1,0:T(8,128)S(1)}, u32[]{:S(2)}, u32[]{:S(2)}) collective-permute-start(f32[72,128]{1,0:T(8,128)S(1)} %get-tuple-element.740), channel_id=1, source_target_pairs={{1,2},{3,4},{5,6},{7,8},{9,10},{11,12},{13,14},{15,16},{17,18},{19... | collective-permute-start | bytes 110600 | tf_op jit(solution)/shard_map/ppermute | solution.py:439
  15.6 1.9 %collective-permute-start.81 = (f32[72,128]{1,0:T(8,128)S(1)}, f32[72,128]{1,0:T(8,128)S(1)}, u32[]{:S(2)}, u32[]{:S(2)}) collective-permute-start(f32[72,128]{1,0:T(8,128)S(1)} %get-tuple-element.741), channel_id=1, source_target_pairs={{0,1},{2,3},{4,5},{6,7},{8,9},{10,11},{12,13},{14,15},{16,17},{18,... | collective-permute-start | bytes 110600 | tf_op jit(solution)/shard_map/ppermute | solution.py:440
  17.5 0.0 collective-permute-done.80.second_ref
  17.5 2.8 %collective-permute-done.81.first_ref = f32[72,128]{1,0:T(8,128)S(1)} collective-permute-done((f32[72,128]{1,0:T(8,128)S(1)}, f32[72,128]{1,0:T(8,128)S(1)}, u32[]{:S(2)}, u32[]{:S(2)}) %collective-permute-start.81) | collective-permute-done | bytes 36896 | tf_op jit(solution)/shard_map/ppermute | solution.py:440
  20.3 0.1 turn.1
  20.4 8.6 %conditional.1 = (f32[2,216,128]{2,1,0:T(8,128)S(1)}, f32[2,216,128]{2,1,0:T(8,128)S(1)}, f32[2,216,128]{2,1,0:T(8,128)S(1)}, f32[2,9,216,128]{3,2,1,0:T(8,128)S...) conditional(s32[]{:T(128)} %bitcast, (f32[3,160,128]{2,1,0:T(8,128)S(1)}, ...), branch_computations={%region_0.0_spmd, %region_1.0_spmd, %region_2.0_spmd, %region_3.0_... | conditional | flops 4008192 | bytes 491688 | solution.py:483
  20.4 5.2 %collective-permute-start = (f32[64,128]{1,0:T(8,128)S(1)}, f32[64,128]{1,0:T(8,128)S(1)}, u32[]{:S(2)}, u32[]{:S(2)}) collective-permute-start(f32[64,128]{1,0:T(8,128)S(1)} %get-tuple-element.359), channel_id=1, source_target_pairs={{32,64},{33,65},{34,66},{35,67},{36,68},{37,69},{38,70},{39,71},{4... | collective-permute-start | bytes 98312 | tf_op jit(solution)/shard_map/cond/branch_0_fun/ppermute | solution.py:460
  25.6 1.9 %collective-permute-start.1 = (f32[64,128]{1,0:T(8,128)S(1)}, f32[64,128]{1,0:T(8,128)S(1)}, u32[]{:S(2)}, u32[]{:S(2)}) collective-permute-start(f32[64,128]{1,0:T(8,128)S(1)} %get-tuple-element.360), channel_id=1, source_target_pairs={{0,32},{64,96},{128,160},{192,224},{256,288},{320,352},{384,416},{... | collective-permute-start | bytes 98312 | tf_op jit(solution)/shard_map/cond/branch_0_fun/ppermute | solution.py:467
  27.5 1.3 %prepare.32 = (f32[2,216,128]{2,1,0:T(8,128)S(1)}, f32[2,216,128]{2,1,0:T(8,128)S(1)}, f32[2,216,128]{2,1,0:T(8,128)S(1)}, f32[2,9,216,128]{3,2,1,0:T(8,128)S(1)}) custom-call(f32[3,160,128]{2,1,0:T(8,128)S(1)} %get-tuple-element.352.x_ref, f32[72,128]{1,0:T(8,128)S(1)} %get-tuple-element.353.second_ref, f32[72,128]{1,0:T(8,128)S(1)} %get-tuple-element.354.first_ref), custom_call_target="tpu_custom_call" | custom-call | flops 4000000 | tf_op jit(solution)/shard_map/cond/branch_0_fun/prepare/pallas_call | solution.py:468
  28.9 0.0 collective-permute-done.two_ref
  28.9 0.0 collective-permute-done.1.one_ref
  29.0 2.9 %basis.1 = (f32[17,216,128]{2,1,0:T(8,128)S(1)}, f32[32,128]{1,0:T(8,128)S(1)}, f32[2,216,128]{2,1,0:T(8,128)S(1)}, f32[2,216,128]{2,1,0:T(8,128)S(1)}, f32[2,9,216,128]{3,2,1,0:T(8,128)S(1)}) custom-call(f32[3,160,128]{2,1,0:T(8,128)S(1)} %get-tuple-element.738.x_ref, ...), custom_call_target="tpu_custom_call", output_to_operand_aliasing={{2}: (2, {}), {3}: (3, {}), {4}: (4, {})} | custom-call | tf_op jit(solution)/shard_map/basis/pallas_call | solution.py:487
  31.9 11.6 %all_to_all.22 = f32[32,1,128]{2,1,0:T(1,128)S(1)} all-to-all(f32[32,1,128]{2,1,0:T(1,128)S(1)} %bitcast.12), channel_id=1, replica_groups=mesh['lat'=16,'lon_0'=8,'lon_1'=4] {'lon_0','lon_1'}, dimensions={0} | all-to-all | bytes 32768 | tf_op jit(solution)/shard_map/all_to_all | solution.py:498
  43.5 15.1 %all_to_all.23 = f32[16,1,128]{2,1,0:T(1,128)S(1)} all-to-all(f32[16,1,128]{2,1,0:T(1,128)S(1)} %bitcast.11), channel_id=1, replica_groups=mesh['lat'=16,'lon_0'=8,'lon_1'=4] {'lat'}, dimensions={0} | all-to-all | bytes 16384 | tf_op jit(solution)/shard_map/all_to_all | solution.py:500
  58.7 1.9 %final.1 = (f32[160,128]{1,0:T(8,128)}, f32[160,128]{1,0:T(8,128)}) custom-call(f32[16,128]{1,0:T(8,128)S(1)} %bitcast.10, f32[17,216,128]{2,1,0:T(8,128)S(1)} %get-tuple-element.753.basis_ref), custom_call_target="tpu_custom_call" | custom-call | tf_op jit(solution)/shard_map/final/pallas_call | solution.py:501
  (2 shorter events, 0.0 us)
Async XLA Ops:
  1.9 15.6 %collective-permute-start.80 = (f32[72,128]{1,0:T(8,128)S(1)}, f32[72,128]{1,0:T(8,128)S(1)}, u32[]{:S(2)}, u32[]{:S(2)}) collective-permute-start(f32[72,128]{1,0:T(8,128)S(1)} %get-tuple-element.740), channel_id=1, source_target_pairs={{1,2},{3,4},{5,6},{7,8},{9,10},{11,12},{13,14},{15,16},{17,18},{19... | collective-permute-start | bytes 110600 | tf_op jit(solution)/shard_map/ppermute | solution.py:439
  15.6 4.7 %collective-permute-start.81 = (f32[72,128]{1,0:T(8,128)S(1)}, f32[72,128]{1,0:T(8,128)S(1)}, u32[]{:S(2)}, u32[]{:S(2)}) collective-permute-start(f32[72,128]{1,0:T(8,128)S(1)} %get-tuple-element.741), channel_id=1, source_target_pairs={{0,1},{2,3},{4,5},{6,7},{8,9},{10,11},{12,13},{14,15},{16,17},{18,... | collective-permute-start | bytes 110600 | tf_op jit(solution)/shard_map/ppermute | solution.py:440
  20.4 8.5 %collective-permute-start = (f32[64,128]{1,0:T(8,128)S(1)}, f32[64,128]{1,0:T(8,128)S(1)}, u32[]{:S(2)}, u32[]{:S(2)}) collective-permute-start(f32[64,128]{1,0:T(8,128)S(1)} %get-tuple-element.359), channel_id=1, source_target_pairs={{32,64},{33,65},{34,66},{35,67},{36,68},{37,69},{38,70},{39,71},{4... | collective-permute-start | bytes 98312 | tf_op jit(solution)/shard_map/cond/branch_0_fun/ppermute | solution.py:460
  25.6 3.3 %collective-permute-start.1 = (f32[64,128]{1,0:T(8,128)S(1)}, f32[64,128]{1,0:T(8,128)S(1)}, u32[]{:S(2)}, u32[]{:S(2)}) collective-permute-start(f32[64,128]{1,0:T(8,128)S(1)} %get-tuple-element.360), channel_id=1, source_target_pairs={{0,32},{64,96},{128,160},{192,224},{256,288},{320,352},{384,416},{... | collective-permute-start | bytes 98312 | tf_op jit(solution)/shard_map/cond/branch_0_fun/ppermute | solution.py:467

commit v6 on v5

--- a/solution.py
+++ b/solution.py
@@ -339,65 +339,51 @@
 def final_kernel(sum_ref, basis_ref, height_ref, residual_ref):
     products = jnp.broadcast_to(jnp.sum(sum_ref[...], axis=0, keepdims=True), (8, LANES))
     row = lax.broadcasted_iota(jnp.int32, (24, LANES), 0)
-    col = lax.broadcasted_iota(jnp.int32, (24, LANES), 1)
-    half = STEPS + 1
-    i = jnp.where(row < half, row, row - half)
-    j = jnp.where(col < half, col, col - half)
-    row_p, col_p = row < half, col < half
-    inside = (row < VECTORS) & (col < VECTORS)
-    total, apart = i + j, jnp.abs(i - j)
-    even = (total & 1) == 0
-    slot = jnp.where(row_p & col_p, 0, jnp.where(row_p | col_p, 4, 2))
-    slot = slot + jnp.where(even, 0, 1)
+    first = row == 0
+    odd = row & 1
 
     def gathered(index):
-        index = jnp.where(inside, index, 6)
         parts = [
             jnp.take_along_axis(products, index[8 * g : 8 * g + 8], axis=1, mode="promise_in_bounds")
             for g in range(3)
         ]
         return jnp.concatenate(parts, axis=0)
 
-    high = jnp.where(total == 2 * STEPS, 8 * (STEPS - 1) + 3, 8 * (total >> 1) + slot)
-    gram = gathered(high) + gathered(8 * (apart >> 1) + slot) - gathered(slot)
-
-    lead_r, lead_c = (row == 0) | (row == half), (col == 0) | (col == half)
-    tail_r = (row == STEPS) | (row >= VECTORS - 1)
-    tail_c = (col == STEPS) | (col >= VECTORS - 1)
-    mapped = jnp.where(tail_c, 0.0, gram + jnp.where(lead_c, 1.0, 0.5) * pltpu.roll(gram, LANES - 1, 1)
-                       + jnp.where(lead_c, 0.0, 0.5) * pltpu.roll(gram, 1, 1))
-    same = (row_p == col_p) & inside & ~tail_r
-    h_turned = jnp.where(same & (row == col), 1.0, 0.0)
-    h_turned = h_turned + jnp.where(same & (col == row + 1), jnp.where(lead_r, 1.0, 0.5), 0.0)
-    h_turned = h_turned + jnp.where(same & (col == row - 1) & ~lead_r, 0.5, 0.0)
-    keep = jnp.where(tail_r, 0.0, 1.0)
-    to_next = jnp.where(tail_r, 0.0, jnp.where(lead_r, 1.0, 0.5))
-    to_last = jnp.where(tail_r | lead_r, 0.0, 0.5)
-
-    def down(value):
-        return jnp.sum(value, axis=0, keepdims=True)
-
-    xc = jnp.zeros((24, LANES), F32)
-    pc, rc = jnp.where(row == 0, 1.0, 0.0), jnp.where(row == half, 1.0, 0.0)
-    p_row, r_row = jnp.where(col[:1] == 0, 1.0, 0.0), jnp.where(col[:1] == half, 1.0, 0.0)
-    gr = jnp.broadcast_to(jnp.sum(gram * r_row, axis=1, keepdims=True), (24, LANES))
-    norm = down(rc * gr)
+    def moments(slot, count):
+        index = jnp.where(row < count, 8 * (row >> 1) + odd + slot, 6)
+        if count > 2 * STEPS:
+            index = jnp.where(row == 2 * STEPS, 8 * (STEPS - 1) + 3, index)
+        return 2.0 * gathered(index) - gathered(jnp.where(row < count, odd + slot, 6))
+
+    def raised(v):
+        up = pltpu.roll(v, 23, 0)
+        return v + 0.5 * (up + jnp.where(first, up, pltpu.roll(v, 1, 0)))
+
+    def mapped(v):
+        down = pltpu.roll(jnp.where(first, v, 0.5 * v), 1, 0)
+        return v + down + pltpu.roll(jnp.where(first, 0.0, 0.5 * v), 23, 0)
+
+    def dot(u, v):
+        return jnp.sum(u[0] * v[0] + u[1] * v[1], axis=0, keepdims=True)
+
+    pair = (0, 1)
+    unit, zero = jnp.where(first, 1.0, 0.0), jnp.zeros((24, LANES), F32)
+    pp, rr, pr = moments(0, 2 * STEPS + 1), moments(2, 2 * STEPS - 1), moments(4, 2 * STEPS)
+    xc, pc, rc = (zero, zero), (unit, zero), (zero, unit)
+    with_r, with_q = (pr, rr), (raised(pp), raised(pr))
+    norm = dot(rc, with_r)
     for _ in range(STEPS):
-        z = jnp.broadcast_to(jnp.sum(mapped * p_row, axis=1, keepdims=True), (24, LANES))
-        q_row = down(h_turned * pc)
-        q_col = keep * pc + pltpu.roll(to_next * pc, 1, 0) + pltpu.roll(to_last * pc, 23, 0)
-        t = norm / down(pc * z)
-        xc = xc + t * pc
-        rc = rc - t * q_col
-        r_row = r_row - t * q_row
-        gr = gr - t * z
-        new = down(rc * gr)
-        ratio = new / norm
-        pc = rc + ratio * pc
-        p_row = r_row + ratio * p_row
-        norm = new
-    xs = [jnp.broadcast_to(xc[k : k + 1, :], (8, LANES)) for k in range(VECTORS)]
-    rs = [jnp.broadcast_to(rc[k : k + 1, :], (8, LANES)) for k in range(VECTORS)]
+        t = norm / dot(pc, with_q)
+        inverse = 1.0 / norm
+        with_r = [with_r[i] - t * with_q[i] for i in pair]
+        rc, xc = [rc[i] - t * mapped(pc[i]) for i in pair], [xc[i] + t * pc[i] for i in pair]
+        norm = dot(rc, with_r)
+        ratio = norm * inverse
+        with_q = [raised(with_r[i]) + ratio * with_q[i] for i in pair]
+        pc = [rc[i] + ratio * pc[i] for i in pair]
+    spots = [(0, k) for k in range(STEPS + 1)] + [(1, k) for k in range(STEPS)]
+    xs = [jnp.broadcast_to(xc[i][k : k + 1, :], (8, LANES)) for i, k in spots]
+    rs = [jnp.broadcast_to(rc[i][k : k + 1, :], (8, LANES)) for i, k in spots]
     for g in range(ROWS // 8):
         first = second = None
         for k in range(VECTORS):

time: 61.1 us -> 60.7 us (level)
  Pallas kernels: 7.5 us -> 6.87 us
    pallas_call x1, Pallas kernels: 1.87 us -> 1.24 us  [per_device(): call(final_kernel, name='final', out_shape=(jax.ShapeDtypeStruct((ROWS, L...]
where the time goes in v6:
time: 60.7 us; the launch traced here: 59.9 us
  blocking collectives  26.7 us (44%)
  starting transfers between devices  22.7 us (37%)
  Pallas kernels  6.87 us (11%)
  waiting for transfers between devices  2.77 us (5%)
  between operations  0.68 us (1%)
    all_to_all x1, blocking collectives, per_device(): sums = lax.all_to_all(sums, 'lat', split_axis=0, concat_axis=0, tiled=True)  15.1 us
    ppermute x1, starting transfers between devices, per_device(): second = lax.ppermute(second, LON, wrap + [(b, a) for a, b in wrap])  13.7 us
    all_to_all x1, blocking collectives, per_device(): sums = lax.all_to_all(sums, LON, split_axis=0, concat_axis=0, tiled=True)  11.6 us
    ppermute x1, starting transfers between devices, second_round(): return lax.ppermute(value, ('lat',) + LON, swaps + fold)  5.19 us
    pallas_call x1, Pallas kernels, per_device(): call(basis_kernel, name='basis', out_shape=(shape(VECTORS, PITCH, LANES),...  2.93 us
    ppermute x1, waiting for transfers between devices, per_device(): lax.ppermute(first, LON, [(i, i + 1) for i in evens] + [(i + 1, i) for i...  2.76 us
    ppermute x1, starting transfers between devices, per_device(): lax.ppermute(first, LON, [(i, i + 1) for i in evens] + [(i + 1, i) for i...  1.92 us
    ppermute x1, starting transfers between devices, exchange(): one = lax.ppermute(one, 'lat', pairs)  1.92 us
  transfers between devices with their start and end apart: 4, of which 1 were waited for; matrix products, arithmetic and copies ran while one was open for 0% of the time, Pallas kernels for 2%

profile of v6, /device:TPU:1, one launch (start us, length us, event | category | flops | bytes accessed | tf_op | source)
XLA Modules:
  0.0 59.9 jit_solution(9229158138108722762)
XLA Ops:
  0.6 1.3 %pack.1 = (f32[3,160,128]{2,1,0:T(8,128)S(1)}, f32[72,128]{1,0:T(8,128)S(1)}, f32[72,128]{1,0:T(8,128)S(1)}, s32[1]{0:T(128)S(4)}, s32[1]{0:T(128)S(4)}) custom-call(f32[160,128]{1,0:T(8,128)} %f_hbm.1, f32[160,128]{1,0:T(8,128)} %p_hbm.1, f32[160,128]{1,0:T(8,128)} %d_hbm.1, s32[160,128]{1,0:T(8,128)} %m_hbm.1, s32[4096]{0:T(1024)} %map_hbm.1), custom_call_target="tpu_custom_call" | custom-call | tf_op jit(solution)/shard_map/pack/pallas_call | solution.py:412
  1.9 13.7 %collective-permute-start.80 = (f32[72,128]{1,0:T(8,128)S(1)}, f32[72,128]{1,0:T(8,128)S(1)}, u32[]{:S(2)}, u32[]{:S(2)}) collective-permute-start(f32[72,128]{1,0:T(8,128)S(1)} %get-tuple-element.740), channel_id=1, source_target_pairs={{1,2},{3,4},{5,6},{7,8},{9,10},{11,12},{13,14},{15,16},{17,18},{19... | collective-permute-start | bytes 110600 | tf_op jit(solution)/shard_map/ppermute | solution.py:425
  15.6 1.9 %collective-permute-start.81 = (f32[72,128]{1,0:T(8,128)S(1)}, f32[72,128]{1,0:T(8,128)S(1)}, u32[]{:S(2)}, u32[]{:S(2)}) collective-permute-start(f32[72,128]{1,0:T(8,128)S(1)} %get-tuple-element.741), channel_id=1, source_target_pairs={{0,1},{2,3},{4,5},{6,7},{8,9},{10,11},{12,13},{14,15},{16,17},{18,... | collective-permute-start | bytes 110600 | tf_op jit(solution)/shard_map/ppermute | solution.py:426
  17.5 0.0 collective-permute-done.80.second_ref
  17.5 2.8 %collective-permute-done.81.first_ref = f32[72,128]{1,0:T(8,128)S(1)} collective-permute-done((f32[72,128]{1,0:T(8,128)S(1)}, f32[72,128]{1,0:T(8,128)S(1)}, u32[]{:S(2)}, u32[]{:S(2)}) %collective-permute-start.81) | collective-permute-done | bytes 36896 | tf_op jit(solution)/shard_map/ppermute | solution.py:426
  20.3 0.1 turn.1
  20.4 8.6 %conditional.1 = (f32[2,216,128]{2,1,0:T(8,128)S(1)}, f32[2,216,128]{2,1,0:T(8,128)S(1)}, f32[2,216,128]{2,1,0:T(8,128)S(1)}, f32[2,9,216,128]{3,2,1,0:T(8,128)S...) conditional(s32[]{:T(128)} %bitcast, (f32[3,160,128]{2,1,0:T(8,128)S(1)}, ...), branch_computations={%region_0.0_spmd, %region_1.0_spmd, %region_2.0_spmd, %region_3.0_... | conditional | flops 4008192 | bytes 491688 | solution.py:469
  20.4 5.2 %collective-permute-start.25 = (f32[64,128]{1,0:T(8,128)S(1)}, f32[64,128]{1,0:T(8,128)S(1)}, u32[]{:S(2)}, u32[]{:S(2)}) collective-permute-start(f32[64,128]{1,0:T(8,128)S(1)} %get-tuple-element.474), channel_id=1, source_target_pairs={{32,64},{33,65},{34,66},{35,67},{36,68},{37,69},{38,70},{39,71},{4... | collective-permute-start | bytes 98312 | tf_op jit(solution)/shard_map/cond/branch_10_fun/ppermute | solution.py:446
  25.6 1.9 %collective-permute-start.26 = (f32[64,128]{1,0:T(8,128)S(1)}, f32[64,128]{1,0:T(8,128)S(1)}, u32[]{:S(2)}, u32[]{:S(2)}) collective-permute-start(f32[64,128]{1,0:T(8,128)S(1)} %get-tuple-element.475), channel_id=1, source_target_pairs={{0,32},{64,96},{128,160},{192,224},{256,288},{320,352},{384,416},{... | collective-permute-start | bytes 98312 | tf_op jit(solution)/shard_map/cond/branch_10_fun/ppermute | solution.py:453
  27.6 1.3 %prepare.42 = (f32[2,216,128]{2,1,0:T(8,128)S(1)}, f32[2,216,128]{2,1,0:T(8,128)S(1)}, f32[2,216,128]{2,1,0:T(8,128)S(1)}, f32[2,9,216,128]{3,2,1,0:T(8,128)S(1)}) custom-call(f32[3,160,128]{2,1,0:T(8,128)S(1)} %get-tuple-element.467.x_ref, f32[72,128]{1,0:T(8,128)S(1)} %get-tuple-element.468.second_ref, f32[72,128]{1,0:T(8,128)S(1)} %get-tuple-element.469.first_ref), custom_call_target="tpu_custom_call" | custom-call | flops 4000000 | tf_op jit(solution)/shard_map/cond/branch_10_fun/prepare/pallas_call | solution.py:454
  28.9 0.0 collective-permute-done.25.two_ref
  28.9 0.0 collective-permute-done.26.one_ref
  29.0 2.9 %basis.1 = (f32[17,216,128]{2,1,0:T(8,128)S(1)}, f32[32,128]{1,0:T(8,128)S(1)}, f32[2,216,128]{2,1,0:T(8,128)S(1)}, f32[2,216,128]{2,1,0:T(8,128)S(1)}, f32[2,9,216,128]{3,2,1,0:T(8,128)S(1)}) custom-call(f32[3,160,128]{2,1,0:T(8,128)S(1)} %get-tuple-element.738.x_ref, ...), custom_call_target="tpu_custom_call", output_to_operand_aliasing={{2}: (2, {}), {3}: (3, {}), {4}: (4, {})} | custom-call | tf_op jit(solution)/shard_map/basis/pallas_call | solution.py:473
  31.9 11.6 %all_to_all.22 = f32[32,1,128]{2,1,0:T(1,128)S(1)} all-to-all(f32[32,1,128]{2,1,0:T(1,128)S(1)} %bitcast.12), channel_id=1, replica_groups=mesh['lat'=16,'lon_0'=8,'lon_1'=4] {'lon_0','lon_1'}, dimensions={0} | all-to-all | bytes 32768 | tf_op jit(solution)/shard_map/all_to_all | solution.py:484
  43.5 15.1 %all_to_all.23 = f32[16,1,128]{2,1,0:T(1,128)S(1)} all-to-all(f32[16,1,128]{2,1,0:T(1,128)S(1)} %bitcast.11), channel_id=1, replica_groups=mesh['lat'=16,'lon_0'=8,'lon_1'=4] {'lat'}, dimensions={0} | all-to-all | bytes 16384 | tf_op jit(solution)/shard_map/all_to_all | solution.py:486
  58.7 1.2 %final.1 = (f32[160,128]{1,0:T(8,128)}, f32[160,128]{1,0:T(8,128)}) custom-call(f32[16,128]{1,0:T(8,128)S(1)} %bitcast.10, f32[17,216,128]{2,1,0:T(8,128)S(1)} %get-tuple-element.753.basis_ref), custom_call_target="tpu_custom_call" | custom-call | tf_op jit(solution)/shard_map/final/pallas_call | solution.py:487
  (2 shorter events, 0.0 us)
Async XLA Ops:
  1.9 15.6 %collective-permute-start.80 = (f32[72,128]{1,0:T(8,128)S(1)}, f32[72,128]{1,0:T(8,128)S(1)}, u32[]{:S(2)}, u32[]{:S(2)}) collective-permute-start(f32[72,128]{1,0:T(8,128)S(1)} %get-tuple-element.740), channel_id=1, source_target_pairs={{1,2},{3,4},{5,6},{7,8},{9,10},{11,12},{13,14},{15,16},{17,18},{19... | collective-permute-start | bytes 110600 | tf_op jit(solution)/shard_map/ppermute | solution.py:425
  15.6 4.7 %collective-permute-start.81 = (f32[72,128]{1,0:T(8,128)S(1)}, f32[72,128]{1,0:T(8,128)S(1)}, u32[]{:S(2)}, u32[]{:S(2)}) collective-permute-start(f32[72,128]{1,0:T(8,128)S(1)} %get-tuple-element.741), channel_id=1, source_target_pairs={{0,1},{2,3},{4,5},{6,7},{8,9},{10,11},{12,13},{14,15},{16,17},{18,... | collective-permute-start | bytes 110600 | tf_op jit(solution)/shard_map/ppermute | solution.py:426
  20.4 8.5 %collective-permute-start.25 = (f32[64,128]{1,0:T(8,128)S(1)}, f32[64,128]{1,0:T(8,128)S(1)}, u32[]{:S(2)}, u32[]{:S(2)}) collective-permute-start(f32[64,128]{1,0:T(8,128)S(1)} %get-tuple-element.474), channel_id=1, source_target_pairs={{32,64},{33,65},{34,66},{35,67},{36,68},{37,69},{38,70},{39,71},{4... | collective-permute-start | bytes 98312 | tf_op jit(solution)/shard_map/cond/branch_10_fun/ppermute | solution.py:446
  25.6 3.3 %collective-permute-start.26 = (f32[64,128]{1,0:T(8,128)S(1)}, f32[64,128]{1,0:T(8,128)S(1)}, u32[]{:S(2)}, u32[]{:S(2)}) collective-permute-start(f32[64,128]{1,0:T(8,128)S(1)} %get-tuple-element.475), channel_id=1, source_target_pairs={{0,32},{64,96},{128,160},{192,224},{256,288},{320,352},{384,416},{... | collective-permute-start | bytes 98312 | tf_op jit(solution)/shard_map/cond/branch_10_fun/ppermute | solution.py:453

commit v7 on v6

--- a/solution.py
+++ b/solution.py
@@ -15,10 +15,14 @@
 EXT = ROWS + 32
 PITCH = 216
 EDGE = 9
-BLK = 40
+BLK = 32
 LON = ("lon_0", "lon_1")
 VECTORS = 2 * STEPS + 1
 F32 = jnp.float32
+
+
+def edge_of(q, blk):
+    return 25 * blk + (0, 9, 17)[q], (9, 8, 8)[q]
 
 
 def lanes_of(rows):
@@ -61,12 +65,12 @@
         east = jnp.zeros((8, LANES), F32)
         west = jnp.zeros((8, LANES), F32)
         for q in range(3):
-            for blk in range(4):
-                at = EDGE * (4 * q + blk)
+            for blk in range(ROWS // BLK):
+                at, width = edge_of(q, blk)
                 tile = x_ref[q, pl.ds(BLK * blk + 8 * v, 8), :]
-                inside = (lane >= at) & (lane < at + EDGE)
+                inside = (lane >= at) & (lane < at + width)
                 west = jnp.where(inside, pltpu.roll(tile, at, 1) if at else tile, west)
-                east = jnp.where(inside, pltpu.roll(tile, (at + EDGE) % LANES, 1), east)
+                east = jnp.where(inside, pltpu.roll(tile, (at + width) % LANES, 1), east)
         first_ref[pl.ds(8 * v, 8), :] = jnp.where(even, east, west)
         second_ref[pl.ds(8 * v, 8), :] = jnp.where(even, west, east)
     for slot, (q, row) in enumerate(((0, ROWS - 8), (1, ROWS - 8), (2, ROWS - 8), (0, ROWS - 16))):
@@ -81,11 +85,11 @@
 
 
 def unpack_halo(from_west, from_east, q, blk, v, lane):
-    at = EDGE * (4 * q + blk)
+    at, width = edge_of(q, blk)
     right = from_east[pl.ds(8 * v, 8), :]
     left = from_west[pl.ds(8 * v, 8), :]
     right = pltpu.roll(right, LANES - at, 1) if at else right
-    left = pltpu.roll(left, (2 * LANES - EDGE - at) % LANES, 1)
+    left = pltpu.roll(left, (2 * LANES - width - at) % LANES, 1)
     return jnp.where(lane < EDGE, right, jnp.where(lane >= LANES - EDGE, left, 0.0))
 
 
@@ -198,7 +202,7 @@
 
     def unpack(v, carry):
         for q, ref in ((0, depth.at[1]), (1, side.at[1]), (2, side.at[0])):
-            for blk in range(4):
+            for blk in range(ROWS // BLK):
                 rows = pl.ds(pl.multiple_of(16 + BLK * blk + 8 * v, 8), 8)
                 ref[rows, :] = unpack_halo(fw_ref, fe_ref, q, blk, v, lane)
         return carry
@@ -309,9 +313,7 @@
                 total[4] += p * r
                 total[5] += new[0] * r
         for i in range(6):
-            acc[k, i, :, :] = total[i]
-        acc[k, 6, :, :] = zero
-        acc[k, 7, :, :] = zero
+            acc[6 * k + i, :, :] = total[i]
 
     step(0, True, False)
 
@@ -322,12 +324,9 @@
     lax.fori_loop(1, STEPS - 1, middle, 0)
     step(STEPS - 1, False, True)
 
-    flat = jnp.sum(acc[...].reshape(8 * STEPS, 8, LANES), axis=1)
-    flat = jnp.concatenate([flat, jnp.zeros_like(flat)], axis=0)
-    row = lax.dot_general(
-        jnp.ones((8, LANES), F32), flat, (((1,), (1,)), ((), ())),
-        precision=lax.Precision.HIGHEST, preferred_element_type=F32,
-    )
+    flat = jnp.sum(acc[...], axis=1)
+    flat = jnp.concatenate([flat, jnp.zeros((LANES - 6 * STEPS, LANES), F32)], axis=0)
+    row = jnp.broadcast_to(jnp.sum(flat.T, axis=0, keepdims=True), (8, LANES))
     for g in range(sums_ref.shape[0] // 8):
         sums_ref[pl.ds(8 * g, 8), :] = row
 
@@ -336,7 +335,7 @@
     out_ref[...] = jnp.broadcast_to(jnp.sum(in_ref[...], axis=0, keepdims=True), out_ref.shape)
 
 
-def final_kernel(sum_ref, basis_ref, height_ref, residual_ref):
+def final_kernel(sum_ref, basis_ref, height_hbm, residual_hbm, height_ref, residual_ref, sems):
     products = jnp.broadcast_to(jnp.sum(sum_ref[...], axis=0, keepdims=True), (8, LANES))
     row = lax.broadcasted_iota(jnp.int32, (24, LANES), 0)
     first = row == 0
@@ -350,10 +349,10 @@
         return jnp.concatenate(parts, axis=0)
 
     def moments(slot, count):
-        index = jnp.where(row < count, 8 * (row >> 1) + odd + slot, 6)
+        index = jnp.where(row < count, 6 * (row >> 1) + odd + slot, LANES - 1)
         if count > 2 * STEPS:
-            index = jnp.where(row == 2 * STEPS, 8 * (STEPS - 1) + 3, index)
-        return 2.0 * gathered(index) - gathered(jnp.where(row < count, odd + slot, 6))
+            index = jnp.where(row == 2 * STEPS, 6 * (STEPS - 1) + 3, index)
+        return 2.0 * gathered(index) - gathered(jnp.where(row < count, odd + slot, LANES - 1))
 
     def raised(v):
         up = pltpu.roll(v, 23, 0)
@@ -384,14 +383,22 @@
     spots = [(0, k) for k in range(STEPS + 1)] + [(1, k) for k in range(STEPS)]
     xs = [jnp.broadcast_to(xc[i][k : k + 1, :], (8, LANES)) for i, k in spots]
     rs = [jnp.broadcast_to(rc[i][k : k + 1, :], (8, LANES)) for i, k in spots]
-    for g in range(ROWS // 8):
-        first = second = None
-        for k in range(VECTORS):
-            tile = basis_ref[k, pl.ds(16 + 8 * g, 8), :]
-            first = xs[k] * tile if first is None else first + xs[k] * tile
-            second = rs[k] * tile if second is None else second + rs[k] * tile
-        height_ref[pl.ds(8 * g, 8), :] = first
-        residual_ref[pl.ds(8 * g, 8), :] = second
+    copies = []
+    for part in range(4):
+        for g in range(part * ROWS // 32, (part + 1) * ROWS // 32):
+            above = below = None
+            for k in range(VECTORS):
+                tile = basis_ref[k, pl.ds(16 + 8 * g, 8), :]
+                above = xs[k] * tile if above is None else above + xs[k] * tile
+                below = rs[k] * tile if below is None else below + rs[k] * tile
+            height_ref[pl.ds(8 * g, 8), :] = above
+            residual_ref[pl.ds(8 * g, 8), :] = below
+        rows = pl.ds(part * ROWS // 4, ROWS // 4)
+        for i, (source, target) in enumerate(((height_ref, height_hbm), (residual_ref, residual_hbm))):
+            copies.append(pltpu.make_async_copy(source.at[rows], target.at[rows], sems.at[2 * part + i]))
+            copies[-1].start()
+    for copy in copies:
+        copy.wait()
 
 
 def shape(*dims):
@@ -441,15 +448,16 @@
     ]
     top = (lat_count - 1) * lon_count
 
-    def second_round(value, pairing):
+    def second_round(value, pairing, others):
         fold = [(top + i, top + (2 * pairing - i) % lon_count) for i in range(lon_count)]
-        return lax.ppermute(value, ("lat",) + LON, swaps + fold)
+        return lax.ppermute(value, ("lat",) + LON, others + fold)
 
     def branch(index):
         def exchange(one, near, far, fields, second, first):
-            value = second_round(near, index // 2)
+            value = second_round(near, index // 2, swaps)
             if index % 2:
-                value = value + second_round(far, (index // 2 + 1) % (lon_count // 2))
+                pairing = (index // 2 + 1) % (lon_count // 2)
+                value = value + second_round(far, pairing, swaps if pairing == 0 else [])
             one = lax.ppermute(one, "lat", pairs)
             ready = call(
                 prepare_kernel, name="prepare",
@@ -476,7 +484,7 @@
                    shape(2, PITCH, LANES), shape(2, 9, PITCH, LANES)),
         scratch_shapes=[
             pltpu.VMEM((VECTORS, PITCH, LANES), F32),
-            pltpu.VMEM((STEPS, 8, 8, LANES), F32),
+            pltpu.VMEM((6 * STEPS, 8, LANES), F32),
         ],
         input_output_aliases={2: 2, 3: 3, 4: 4},
         compiler_params=limit(12),
@@ -486,6 +494,8 @@
     sums = lax.all_to_all(sums, "lat", split_axis=0, concat_axis=0, tiled=True)
     return call(
         final_kernel, name="final", out_shape=(jax.ShapeDtypeStruct((ROWS, LANES), F32),) * 2,
+        out_specs=[pl.BlockSpec(memory_space=pl.ANY)] * 2,
+        scratch_shapes=[pltpu.VMEM((ROWS, LANES), F32)] * 2 + [pltpu.SemaphoreType.DMA((8,))],
         compiler_params=limit(4),
     )(*held(sums, basis))
 

time: 60.7 us -> 60.1 us (level)
  no operation moved by 1% of the time
where the time goes in v7:
time: 60.1 us; the launch traced here: 59.8 us
  blocking collectives  26.8 us (45%)
  starting transfers between devices  22.7 us (38%)
  Pallas kernels  6.73 us (11%)
  waiting for transfers between devices  2.72 us (5%)
  between operations  0.69 us (1%)
    all_to_all x1, blocking collectives, per_device(): sums = lax.all_to_all(sums, 'lat', split_axis=0, concat_axis=0, tiled=True)  15.2 us
    ppermute x1, starting transfers between devices, per_device(): second = lax.ppermute(second, LON, wrap + [(b, a) for a, b in wrap])  13.7 us
    all_to_all x1, blocking collectives, per_device(): sums = lax.all_to_all(sums, LON, split_axis=0, concat_axis=0, tiled=True)  11.6 us
    ppermute x1, starting transfers between devices, second_round(): return lax.ppermute(value, ('lat',) + LON, others + fold)  5.19 us
    pallas_call x1, Pallas kernels, per_device(): call(basis_kernel, name='basis', out_shape=(shape(VECTORS, PITCH, LANES),...  2.82 us
    ppermute x1, waiting for transfers between devices, per_device(): lax.ppermute(first, LON, [(i, i + 1) for i in evens] + [(i + 1, i) for i...  2.71 us
    ppermute x1, starting transfers between devices, exchange(): one = lax.ppermute(one, 'lat', pairs)  1.92 us
    ppermute x1, starting transfers between devices, per_device(): lax.ppermute(first, LON, [(i, i + 1) for i in evens] + [(i + 1, i) for i...  1.92 us
  transfers between devices with their start and end apart: 4, of which 1 were waited for; matrix products, arithmetic and copies ran while one was open for 0% of the time, Pallas kernels for 2%

profile of v7, /device:TPU:1, one launch (start us, length us, event | category | flops | bytes accessed | tf_op | source)
XLA Modules:
  0.0 59.8 jit_solution(884391332913505374)
XLA Ops:
  0.6 1.3 %pack.1 = (f32[3,160,128]{2,1,0:T(8,128)S(1)}, f32[64,128]{1,0:T(8,128)S(1)}, f32[64,128]{1,0:T(8,128)S(1)}, s32[1]{0:T(128)S(4)}, s32[1]{0:T(128)S(4)}) custom-call(f32[160,128]{1,0:T(8,128)} %f_hbm.1, f32[160,128]{1,0:T(8,128)} %p_hbm.1, f32[160,128]{1,0:T(8,128)} %d_hbm.1, s32[160,128]{1,0:T(8,128)} %m_hbm.1, s32[4096]{0:T(1024)} %map_hbm.1), custom_call_target="tpu_custom_call" | custom-call | tf_op jit(solution)/shard_map/pack/pallas_call | solution.py:419
  1.9 13.7 %collective-permute-start.80 = (f32[64,128]{1,0:T(8,128)S(1)}, f32[64,128]{1,0:T(8,128)S(1)}, u32[]{:S(2)}, u32[]{:S(2)}) collective-permute-start(f32[64,128]{1,0:T(8,128)S(1)} %get-tuple-element.740), channel_id=1, source_target_pairs={{1,2},{3,4},{5,6},{7,8},{9,10},{11,12},{13,14},{15,16},{17,18},{19... | collective-permute-start | bytes 98312 | tf_op jit(solution)/shard_map/ppermute | solution.py:432
  15.6 1.9 %collective-permute-start.81 = (f32[64,128]{1,0:T(8,128)S(1)}, f32[64,128]{1,0:T(8,128)S(1)}, u32[]{:S(2)}, u32[]{:S(2)}) collective-permute-start(f32[64,128]{1,0:T(8,128)S(1)} %get-tuple-element.741), channel_id=1, source_target_pairs={{0,1},{2,3},{4,5},{6,7},{8,9},{10,11},{12,13},{14,15},{16,17},{18,... | collective-permute-start | bytes 98312 | tf_op jit(solution)/shard_map/ppermute | solution.py:433
  17.5 0.0 collective-permute-done.80.second_ref
  17.5 2.7 %collective-permute-done.81.first_ref = f32[64,128]{1,0:T(8,128)S(1)} collective-permute-done((f32[64,128]{1,0:T(8,128)S(1)}, f32[64,128]{1,0:T(8,128)S(1)}, u32[]{:S(2)}, u32[]{:S(2)}) %collective-permute-start.81) | collective-permute-done | bytes 32800 | tf_op jit(solution)/shard_map/ppermute | solution.py:433
  20.2 0.1 turn.1
  20.3 8.5 %conditional.1 = (f32[2,216,128]{2,1,0:T(8,128)S(1)}, f32[2,216,128]{2,1,0:T(8,128)S(1)}, f32[2,216,128]{2,1,0:T(8,128)S(1)}, f32[2,9,216,128]{3,2,1,0:T(8,128)S...) conditional(s32[]{:T(128)} %bitcast, (f32[3,160,128]{2,1,0:T(8,128)S(1)}, ...), branch_computations={%region_0.0_spmd, %region_1.0_spmd, %region_2.0_spmd, %region_3.0_... | conditional | flops 4008192 | bytes 491688 | solution.py:477
  20.4 5.2 %collective-permute-start.15 = (f32[64,128]{1,0:T(8,128)S(1)}, f32[64,128]{1,0:T(8,128)S(1)}, u32[]{:S(2)}, u32[]{:S(2)}) collective-permute-start(f32[64,128]{1,0:T(8,128)S(1)} %get-tuple-element.428), channel_id=1, source_target_pairs={{32,64},{33,65},{34,66},{35,67},{36,68},{37,69},{38,70},{39,71},{4... | collective-permute-start | bytes 98312 | tf_op jit(solution)/shard_map/cond/branch_6_fun/ppermute | solution.py:453
  25.6 1.9 %collective-permute-start.16 = (f32[64,128]{1,0:T(8,128)S(1)}, f32[64,128]{1,0:T(8,128)S(1)}, u32[]{:S(2)}, u32[]{:S(2)}) collective-permute-start(f32[64,128]{1,0:T(8,128)S(1)} %get-tuple-element.429), channel_id=1, source_target_pairs={{0,32},{64,96},{128,160},{192,224},{256,288},{320,352},{384,416},{... | collective-permute-start | bytes 98312 | tf_op jit(solution)/shard_map/cond/branch_6_fun/ppermute | solution.py:461
  27.5 1.3 %prepare.38 = (f32[2,216,128]{2,1,0:T(8,128)S(1)}, f32[2,216,128]{2,1,0:T(8,128)S(1)}, f32[2,216,128]{2,1,0:T(8,128)S(1)}, f32[2,9,216,128]{3,2,1,0:T(8,128)S(1)}) custom-call(f32[3,160,128]{2,1,0:T(8,128)S(1)} %get-tuple-element.421.x_ref, f32[64,128]{1,0:T(8,128)S(1)} %get-tuple-element.422.second_ref, f32[64,128]{1,0:T(8,128)S(1)} %get-tuple-element.423.first_ref), custom_call_target="tpu_custom_call" | custom-call | flops 4000000 | tf_op jit(solution)/shard_map/cond/branch_6_fun/prepare/pallas_call | solution.py:462
  28.8 0.0 collective-permute-done.15.two_ref
  28.8 0.0 collective-permute-done.16.one_ref
  28.9 2.8 %basis.1 = (f32[17,216,128]{2,1,0:T(8,128)S(1)}, f32[32,128]{1,0:T(8,128)S(1)}, f32[2,216,128]{2,1,0:T(8,128)S(1)}, f32[2,216,128]{2,1,0:T(8,128)S(1)}, f32[2,9,216,128]{3,2,1,0:T(8,128)S(1)}) custom-call(f32[3,160,128]{2,1,0:T(8,128)S(1)} %get-tuple-element.738.x_ref, ...), custom_call_target="tpu_custom_call", output_to_operand_aliasing={{2}: (2, {}), {3}: (3, {}), {4}: (4, {})} | custom-call | tf_op jit(solution)/shard_map/basis/pallas_call | solution.py:481
  31.7 11.6 %all_to_all.22 = f32[32,1,128]{2,1,0:T(1,128)S(1)} all-to-all(f32[32,1,128]{2,1,0:T(1,128)S(1)} %bitcast.12), channel_id=1, replica_groups=mesh['lat'=16,'lon_0'=8,'lon_1'=4] {'lon_0','lon_1'}, dimensions={0} | all-to-all | bytes 32768 | tf_op jit(solution)/shard_map/all_to_all | solution.py:492
  43.3 15.2 %all_to_all.23 = f32[16,1,128]{2,1,0:T(1,128)S(1)} all-to-all(f32[16,1,128]{2,1,0:T(1,128)S(1)} %bitcast.11), channel_id=1, replica_groups=mesh['lat'=16,'lon_0'=8,'lon_1'=4] {'lat'}, dimensions={0} | all-to-all | bytes 16384 | tf_op jit(solution)/shard_map/all_to_all | solution.py:494
  58.5 1.3 %final.1 = (f32[160,128]{1,0:T(8,128)}, f32[160,128]{1,0:T(8,128)}) custom-call(f32[16,128]{1,0:T(8,128)S(1)} %bitcast.10, f32[17,216,128]{2,1,0:T(8,128)S(1)} %get-tuple-element.753.basis_ref), custom_call_target="tpu_custom_call" | custom-call | tf_op jit(solution)/shard_map/final/pallas_call | solution.py:495
  (2 shorter events, 0.0 us)
Async XLA Ops:
  1.9 15.6 %collective-permute-start.80 = (f32[64,128]{1,0:T(8,128)S(1)}, f32[64,128]{1,0:T(8,128)S(1)}, u32[]{:S(2)}, u32[]{:S(2)}) collective-permute-start(f32[64,128]{1,0:T(8,128)S(1)} %get-tuple-element.740), channel_id=1, source_target_pairs={{1,2},{3,4},{5,6},{7,8},{9,10},{11,12},{13,14},{15,16},{17,18},{19... | collective-permute-start | bytes 98312 | tf_op jit(solution)/shard_map/ppermute | solution.py:432
  15.6 4.7 %collective-permute-start.81 = (f32[64,128]{1,0:T(8,128)S(1)}, f32[64,128]{1,0:T(8,128)S(1)}, u32[]{:S(2)}, u32[]{:S(2)}) collective-permute-start(f32[64,128]{1,0:T(8,128)S(1)} %get-tuple-element.741), channel_id=1, source_target_pairs={{0,1},{2,3},{4,5},{6,7},{8,9},{10,11},{12,13},{14,15},{16,17},{18,... | collective-permute-start | bytes 98312 | tf_op jit(solution)/shard_map/ppermute | solution.py:433
  20.4 8.4 %collective-permute-start.15 = (f32[64,128]{1,0:T(8,128)S(1)}, f32[64,128]{1,0:T(8,128)S(1)}, u32[]{:S(2)}, u32[]{:S(2)}) collective-permute-start(f32[64,128]{1,0:T(8,128)S(1)} %get-tuple-element.428), channel_id=1, source_target_pairs={{32,64},{33,65},{34,66},{35,67},{36,68},{37,69},{38,70},{39,71},{4... | collective-permute-start | bytes 98312 | tf_op jit(solution)/shard_map/cond/branch_6_fun/ppermute | solution.py:453
  25.6 3.2 %collective-permute-start.16 = (f32[64,128]{1,0:T(8,128)S(1)}, f32[64,128]{1,0:T(8,128)S(1)}, u32[]{:S(2)}, u32[]{:S(2)}) collective-permute-start(f32[64,128]{1,0:T(8,128)S(1)} %get-tuple-element.429), channel_id=1, source_target_pairs={{0,32},{64,96},{128,160},{192,224},{256,288},{320,352},{384,416},{... | collective-permute-start | bytes 98312 | tf_op jit(solution)/shard_map/cond/branch_6_fun/ppermute | solution.py:461

commit v8 on v7

--- a/solution.py
+++ b/solution.py
@@ -43,7 +43,7 @@
 
 def pack_kernel(pairs, f_hbm, p_hbm, d_hbm, m_hbm, map_hbm, x_ref, first_ref, second_ref, reach_ref, choice_ref,
                 f_ref, p_ref, d_ref, m_ref, pivot, sems):
-    even = lax.axis_index(LON) % 2 == 0
+    even = turns(LON)
     copies = [
         pltpu.make_async_copy(source, target, sems.at[i])
         for i, (source, target) in enumerate((
@@ -93,8 +93,15 @@
     return jnp.where(lane < EDGE, right, jnp.where(lane >= LANES - EDGE, left, 0.0))
 
 
+def turns(axis):
+    place = lax.axis_index("lat")
+    if axis == LON:
+        place = place + lax.axis_index(LON)
+    return place % 2 == 0
+
+
 def sort_partners(axis, first, second, before, after):
-    even = lax.axis_index(axis) % 2 == 0
+    even = turns(axis)
     for g in range(first.shape[0] // 8):
         rows = pl.ds(8 * g, 8)
         a, b = first[rows, :], second[rows, :]
@@ -427,10 +434,16 @@
         ],
         compiler_params=limit(4),
     )(*held(forcing, search_direction, ocean_depth, land_mask, fold_map, space=pltpu.HBM))
-    evens, odds = range(0, lon_count, 2), range(1, lon_count, 2)
-    wrap = [(i, (i + 1) % lon_count) for i in odds]
-    second = lax.ppermute(second, LON, wrap + [(b, a) for a, b in wrap])
-    first = lax.ppermute(first, LON, [(i, i + 1) for i in evens] + [(i + 1, i) for i in evens])
+    def lon_round(start):
+        pairs = []
+        for row in range(lat_count):
+            for i in range((start + row) % 2, lon_count, 2):
+                a, b = row * lon_count + i, row * lon_count + (i + 1) % lon_count
+                pairs += [(a, b), (b, a)]
+        return pairs
+
+    second = lax.ppermute(second, ("lat",) + LON, lon_round(1))
+    first = lax.ppermute(first, ("lat",) + LON, lon_round(0))
 
     one, two, two_next = call(
         functools.partial(turn_kernel, lat_count - 1), name="turn",

time: 60.1 us -> 60.3 us (level)
  starting transfers between devices: 22.7 us -> 24.2 us
  waiting for transfers between devices: 2.72 us -> 1.28 us
    ppermute x2, waiting for transfers between devices: 2.72 us -> 1.28 us  [the longest x1 1.27 us: per_device(): first = lax.ppermute(first, ('lat',) + LON, lon_round(0))]
    ppermute x1, starting transfers between devices: 5.19 us -> 6.1 us  [second_round(): return lax.ppermute(value, ('lat',) + LON, others + fold)]
where the time goes in v8:
time: 60.3 us; the launch traced here: 59.8 us
  blocking collectives  26.8 us (44%)
  starting transfers between devices  24.2 us (40%)
  Pallas kernels  6.73 us (11%)
  waiting for transfers between devices  1.28 us (2%)
  between operations  0.69 us (1%)
    all_to_all x1, blocking collectives, per_device(): sums = lax.all_to_all(sums, 'lat', split_axis=0, concat_axis=0, tiled=True)  15.2 us
    ppermute x1, starting transfers between devices, per_device(): first = lax.ppermute(first, ('lat',) + LON, lon_round(0))  12.2 us
    all_to_all x1, blocking collectives, per_device(): sums = lax.all_to_all(sums, LON, split_axis=0, concat_axis=0, tiled=True)  11.6 us
    ppermute x1, starting transfers between devices, second_round(): return lax.ppermute(value, ('lat',) + LON, others + fold)  6.1 us
    ppermute x1, starting transfers between devices, per_device(): second = lax.ppermute(second, ('lat',) + LON, lon_round(1))  3.94 us
    pallas_call x1, Pallas kernels, per_device(): call(basis_kernel, name='basis', out_shape=(shape(VECTORS, PITCH, LANES),...  2.82 us
    ppermute x1, starting transfers between devices, exchange(): one = lax.ppermute(one, 'lat', pairs)  1.92 us
    ppermute x1, waiting for transfers between devices, per_device(): first = lax.ppermute(first, ('lat',) + LON, lon_round(0))  1.27 us
  transfers between devices with their start and end apart: 4, of which 1 were waited for; matrix products, arithmetic and copies ran while one was open for 0% of the time, Pallas kernels for 2%

profile of v8, /device:TPU:1, one launch (start us, length us, event | category | flops | bytes accessed | tf_op | source)
XLA Modules:
  0.0 59.8 jit_solution(5428647138150902682)
XLA Ops:
  0.6 1.3 %pack.1 = (f32[3,160,128]{2,1,0:T(8,128)S(1)}, f32[64,128]{1,0:T(8,128)S(1)}, f32[64,128]{1,0:T(8,128)S(1)}, s32[1]{0:T(128)S(4)}, s32[1]{0:T(128)S(4)}) custom-call(f32[160,128]{1,0:T(8,128)} %f_hbm.1, f32[160,128]{1,0:T(8,128)} %p_hbm.1, f32[160,128]{1,0:T(8,128)} %d_hbm.1, s32[160,128]{1,0:T(8,128)} %m_hbm.1, s32[4096]{0:T(1024)} %map_hbm.1), custom_call_target="tpu_custom_call" | custom-call | tf_op jit(solution)/shard_map/pack/pallas_call | solution.py:426
  1.9 3.9 %collective-permute-start.80 = (f32[64,128]{1,0:T(8,128)S(1)}, f32[64,128]{1,0:T(8,128)S(1)}, u32[]{:S(2)}, u32[]{:S(2)}) collective-permute-start(f32[64,128]{1,0:T(8,128)S(1)} %get-tuple-element.740), channel_id=1, source_target_pairs={{1,2},{2,1},{3,4},{4,3},{5,6},{6,5},{7,8},{8,7},{9,10},{10,9},{11,... | collective-permute-start | bytes 98312 | tf_op jit(solution)/shard_map/ppermute | solution.py:445
  5.8 12.2 %collective-permute-start.81 = (f32[64,128]{1,0:T(8,128)S(1)}, f32[64,128]{1,0:T(8,128)S(1)}, u32[]{:S(2)}, u32[]{:S(2)}) collective-permute-start(f32[64,128]{1,0:T(8,128)S(1)} %get-tuple-element.741), channel_id=1, source_target_pairs={{0,1},{1,0},{2,3},{3,2},{4,5},{5,4},{6,7},{7,6},{8,9},{9,8},{10,11... | collective-permute-start | bytes 98312 | tf_op jit(solution)/shard_map/ppermute | solution.py:446
  18.1 0.0 collective-permute-done.80.second_ref
  18.1 1.3 %collective-permute-done.81.first_ref = f32[64,128]{1,0:T(8,128)S(1)} collective-permute-done((f32[64,128]{1,0:T(8,128)S(1)}, f32[64,128]{1,0:T(8,128)S(1)}, u32[]{:S(2)}, u32[]{:S(2)}) %collective-permute-start.81) | collective-permute-done | bytes 32800 | tf_op jit(solution)/shard_map/ppermute | solution.py:446
  19.3 0.1 turn.1
  19.4 9.4 %conditional.1 = (f32[2,216,128]{2,1,0:T(8,128)S(1)}, f32[2,216,128]{2,1,0:T(8,128)S(1)}, f32[2,216,128]{2,1,0:T(8,128)S(1)}, f32[2,9,216,128]{3,2,1,0:T(8,128)S...) conditional(s32[]{:T(128)} %bitcast, (f32[3,160,128]{2,1,0:T(8,128)S(1)}, ...), branch_computations={%region_0.0_spmd, %region_1.0_spmd, %region_2.0_spmd, %region_3.0_... | conditional | flops 4008192 | bytes 491688 | solution.py:490
  19.5 6.1 %collective-permute-start.5 = (f32[64,128]{1,0:T(8,128)S(1)}, f32[64,128]{1,0:T(8,128)S(1)}, u32[]{:S(2)}, u32[]{:S(2)}) collective-permute-start(f32[64,128]{1,0:T(8,128)S(1)} %get-tuple-element.382), channel_id=1, source_target_pairs={{32,64},{33,65},{34,66},{35,67},{36,68},{37,69},{38,70},{39,71},{4... | collective-permute-start | bytes 98312 | tf_op jit(solution)/shard_map/cond/branch_2_fun/ppermute | solution.py:466
  25.6 1.9 %collective-permute-start.6 = (f32[64,128]{1,0:T(8,128)S(1)}, f32[64,128]{1,0:T(8,128)S(1)}, u32[]{:S(2)}, u32[]{:S(2)}) collective-permute-start(f32[64,128]{1,0:T(8,128)S(1)} %get-tuple-element.383), channel_id=1, source_target_pairs={{0,32},{64,96},{128,160},{192,224},{256,288},{320,352},{384,416},{... | collective-permute-start | bytes 98312 | tf_op jit(solution)/shard_map/cond/branch_2_fun/ppermute | solution.py:474
  27.5 1.3 %prepare.34 = (f32[2,216,128]{2,1,0:T(8,128)S(1)}, f32[2,216,128]{2,1,0:T(8,128)S(1)}, f32[2,216,128]{2,1,0:T(8,128)S(1)}, f32[2,9,216,128]{3,2,1,0:T(8,128)S(1)}) custom-call(f32[3,160,128]{2,1,0:T(8,128)S(1)} %get-tuple-element.375.x_ref, f32[64,128]{1,0:T(8,128)S(1)} %get-tuple-element.376.second_ref, f32[64,128]{1,0:T(8,128)S(1)} %get-tuple-element.377.first_ref), custom_call_target="tpu_custom_call" | custom-call | flops 4000000 | tf_op jit(solution)/shard_map/cond/branch_2_fun/prepare/pallas_call | solution.py:475
  28.8 0.0 collective-permute-done.5.two_ref
  28.8 0.0 collective-permute-done.6.one_ref
  28.9 2.8 %basis.1 = (f32[17,216,128]{2,1,0:T(8,128)S(1)}, f32[32,128]{1,0:T(8,128)S(1)}, f32[2,216,128]{2,1,0:T(8,128)S(1)}, f32[2,216,128]{2,1,0:T(8,128)S(1)}, f32[2,9,216,128]{3,2,1,0:T(8,128)S(1)}) custom-call(f32[3,160,128]{2,1,0:T(8,128)S(1)} %get-tuple-element.738.x_ref, ...), custom_call_target="tpu_custom_call", output_to_operand_aliasing={{2}: (2, {}), {3}: (3, {}), {4}: (4, {})} | custom-call | tf_op jit(solution)/shard_map/basis/pallas_call | solution.py:494
  31.7 11.6 %all_to_all.22 = f32[32,1,128]{2,1,0:T(1,128)S(1)} all-to-all(f32[32,1,128]{2,1,0:T(1,128)S(1)} %bitcast.12), channel_id=1, replica_groups=mesh['lat'=16,'lon_0'=8,'lon_1'=4] {'lon_0','lon_1'}, dimensions={0} | all-to-all | bytes 32768 | tf_op jit(solution)/shard_map/all_to_all | solution.py:505
  43.3 15.2 %all_to_all.23 = f32[16,1,128]{2,1,0:T(1,128)S(1)} all-to-all(f32[16,1,128]{2,1,0:T(1,128)S(1)} %bitcast.11), channel_id=1, replica_groups=mesh['lat'=16,'lon_0'=8,'lon_1'=4] {'lat'}, dimensions={0} | all-to-all | bytes 16384 | tf_op jit(solution)/shard_map/all_to_all | solution.py:507
  58.5 1.3 %final.1 = (f32[160,128]{1,0:T(8,128)}, f32[160,128]{1,0:T(8,128)}) custom-call(f32[16,128]{1,0:T(8,128)S(1)} %bitcast.10, f32[17,216,128]{2,1,0:T(8,128)S(1)} %get-tuple-element.753.basis_ref), custom_call_target="tpu_custom_call" | custom-call | tf_op jit(solution)/shard_map/final/pallas_call | solution.py:508
  (2 shorter events, 0.0 us)
Async XLA Ops:
  1.9 16.2 %collective-permute-start.80 = (f32[64,128]{1,0:T(8,128)S(1)}, f32[64,128]{1,0:T(8,128)S(1)}, u32[]{:S(2)}, u32[]{:S(2)}) collective-permute-start(f32[64,128]{1,0:T(8,128)S(1)} %get-tuple-element.740), channel_id=1, source_target_pairs={{1,2},{2,1},{3,4},{4,3},{5,6},{6,5},{7,8},{8,7},{9,10},{10,9},{11,... | collective-permute-start | bytes 98312 | tf_op jit(solution)/shard_map/ppermute | solution.py:445
  5.8 13.5 %collective-permute-start.81 = (f32[64,128]{1,0:T(8,128)S(1)}, f32[64,128]{1,0:T(8,128)S(1)}, u32[]{:S(2)}, u32[]{:S(2)}) collective-permute-start(f32[64,128]{1,0:T(8,128)S(1)} %get-tuple-element.741), channel_id=1, source_target_pairs={{0,1},{1,0},{2,3},{3,2},{4,5},{5,4},{6,7},{7,6},{8,9},{9,8},{10,11... | collective-permute-start | bytes 98312 | tf_op jit(solution)/shard_map/ppermute | solution.py:446
  19.5 9.3 %collective-permute-start.5 = (f32[64,128]{1,0:T(8,128)S(1)}, f32[64,128]{1,0:T(8,128)S(1)}, u32[]{:S(2)}, u32[]{:S(2)}) collective-permute-start(f32[64,128]{1,0:T(8,128)S(1)} %get-tuple-element.382), channel_id=1, source_target_pairs={{32,64},{33,65},{34,66},{35,67},{36,68},{37,69},{38,70},{39,71},{4... | collective-permute-start | bytes 98312 | tf_op jit(solution)/shard_map/cond/branch_2_fun/ppermute | solution.py:466
  25.6 3.2 %collective-permute-start.6 = (f32[64,128]{1,0:T(8,128)S(1)}, f32[64,128]{1,0:T(8,128)S(1)}, u32[]{:S(2)}, u32[]{:S(2)}) collective-permute-start(f32[64,128]{1,0:T(8,128)S(1)} %get-tuple-element.383), channel_id=1, source_target_pairs={{0,32},{64,96},{128,160},{192,224},{256,288},{320,352},{384,416},{... | collective-permute-start | bytes 98312 | tf_op jit(solution)/shard_map/cond/branch_2_fun/ppermute | solution.py:474

commit v9 on v8

--- a/solution.py
+++ b/solution.py
@@ -22,7 +22,7 @@
 
 
 def edge_of(q, blk):
-    return 25 * blk + (0, 9, 17)[q], (9, 8, 8)[q]
+    return (9 * blk, 45 + 8 * blk, 85 + 8 * blk)[q], (9, 8, 8)[q]
 
 
 def lanes_of(rows):
@@ -68,9 +68,10 @@
             for blk in range(ROWS // BLK):
                 at, width = edge_of(q, blk)
                 tile = x_ref[q, pl.ds(BLK * blk + 8 * v, 8), :]
-                inside = (lane >= at) & (lane < at + width)
-                west = jnp.where(inside, pltpu.roll(tile, at, 1) if at else tile, west)
-                east = jnp.where(inside, pltpu.roll(tile, (at + width) % LANES, 1), east)
+                tile = pltpu.roll(tile, at, 1) if at else tile
+                west = jnp.where((lane >= at) & (lane < at + width), tile, west)
+                start = (at - width) % LANES
+                east = jnp.where((lane >= start) & (lane < start + width), tile, east)
         first_ref[pl.ds(8 * v, 8), :] = jnp.where(even, east, west)
         second_ref[pl.ds(8 * v, 8), :] = jnp.where(even, west, east)
     for slot, (q, row) in enumerate(((0, ROWS - 8), (1, ROWS - 8), (2, ROWS - 8), (0, ROWS - 16))):
@@ -88,9 +89,9 @@
     at, width = edge_of(q, blk)
     right = from_east[pl.ds(8 * v, 8), :]
     left = from_west[pl.ds(8 * v, 8), :]
-    right = pltpu.roll(right, LANES - at, 1) if at else right
-    left = pltpu.roll(left, (2 * LANES - width - at) % LANES, 1)
-    return jnp.where(lane < EDGE, right, jnp.where(lane >= LANES - EDGE, left, 0.0))
+    both = jnp.where((lane >= at) & (lane < at + EDGE), right, left)
+    both = pltpu.roll(both, LANES - at, 1) if at else both
+    return jnp.where((lane < EDGE) | (lane >= LANES - EDGE), both, 0.0)
 
 
 def turns(axis):
@@ -328,7 +329,7 @@
         step(k, False, False)
         return carry
 
-    lax.fori_loop(1, STEPS - 1, middle, 0)
+    lax.fori_loop(1, STEPS - 1, middle, 0, unroll=2)
     step(STEPS - 1, False, True)
 
     flat = jnp.sum(acc[...], axis=1)

time: 60.3 us -> 60 us (level)
  no operation moved by 1% of the time
where the time goes in v9:
time: 60 us; the launch traced here: 59.5 us
  blocking collectives  26.8 us (45%)
  starting transfers between devices  24.1 us (40%)
  Pallas kernels  6.5 us (11%)
  waiting for transfers between devices  1.28 us (2%)
  between operations  0.68 us (1%)
    all_to_all x1, blocking collectives, per_device(): sums = lax.all_to_all(sums, 'lat', split_axis=0, concat_axis=0, tiled=True)  15.3 us
    ppermute x1, starting transfers between devices, per_device(): first = lax.ppermute(first, ('lat',) + LON, lon_round(0))  12.2 us
    all_to_all x1, blocking collectives, per_device(): sums = lax.all_to_all(sums, LON, split_axis=0, concat_axis=0, tiled=True)  11.6 us
    ppermute x1, starting transfers between devices, second_round(): return lax.ppermute(value, ('lat',) + LON, others + fold)  6.09 us
    ppermute x1, starting transfers between devices, per_device(): second = lax.ppermute(second, ('lat',) + LON, lon_round(1))  3.94 us
    pallas_call x1, Pallas kernels, per_device(): call(basis_kernel, name='basis', out_shape=(shape(VECTORS, PITCH, LANES),...  2.71 us
    ppermute x1, starting transfers between devices, exchange(): one = lax.ppermute(one, 'lat', pairs)  1.92 us
    ppermute x1, waiting for transfers between devices, per_device(): first = lax.ppermute(first, ('lat',) + LON, lon_round(0))  1.27 us
  transfers between devices with their start and end apart: 4, of which 1 were waited for; matrix products, arithmetic and copies ran while one was open for 0% of the time, Pallas kernels for 2%

profile of v9, /device:TPU:1, one launch (start us, length us, event | category | flops | bytes accessed | tf_op | source)
XLA Modules:
  0.0 59.5 jit_solution(17797518317428431127)
XLA Ops:
  0.6 1.2 %pack.1 = (f32[3,160,128]{2,1,0:T(8,128)S(1)}, f32[64,128]{1,0:T(8,128)S(1)}, f32[64,128]{1,0:T(8,128)S(1)}, s32[1]{0:T(128)S(4)}, s32[1]{0:T(128)S(4)}) custom-call(f32[160,128]{1,0:T(8,128)} %f_hbm.1, f32[160,128]{1,0:T(8,128)} %p_hbm.1, f32[160,128]{1,0:T(8,128)} %d_hbm.1, s32[160,128]{1,0:T(8,128)} %m_hbm.1, s32[4096]{0:T(1024)} %map_hbm.1), custom_call_target="tpu_custom_call" | custom-call | tf_op jit(solution)/shard_map/pack/pallas_call | solution.py:427
  1.8 3.9 %collective-permute-start.80 = (f32[64,128]{1,0:T(8,128)S(1)}, f32[64,128]{1,0:T(8,128)S(1)}, u32[]{:S(2)}, u32[]{:S(2)}) collective-permute-start(f32[64,128]{1,0:T(8,128)S(1)} %get-tuple-element.740), channel_id=1, source_target_pairs={{1,2},{2,1},{3,4},{4,3},{5,6},{6,5},{7,8},{8,7},{9,10},{10,9},{11,... | collective-permute-start | bytes 98312 | tf_op jit(solution)/shard_map/ppermute | solution.py:446
  5.8 12.2 %collective-permute-start.81 = (f32[64,128]{1,0:T(8,128)S(1)}, f32[64,128]{1,0:T(8,128)S(1)}, u32[]{:S(2)}, u32[]{:S(2)}) collective-permute-start(f32[64,128]{1,0:T(8,128)S(1)} %get-tuple-element.741), channel_id=1, source_target_pairs={{0,1},{1,0},{2,3},{3,2},{4,5},{5,4},{6,7},{7,6},{8,9},{9,8},{10,11... | collective-permute-start | bytes 98312 | tf_op jit(solution)/shard_map/ppermute | solution.py:447
  18.0 0.0 collective-permute-done.80.second_ref
  18.0 1.3 %collective-permute-done.81.first_ref = f32[64,128]{1,0:T(8,128)S(1)} collective-permute-done((f32[64,128]{1,0:T(8,128)S(1)}, f32[64,128]{1,0:T(8,128)S(1)}, u32[]{:S(2)}, u32[]{:S(2)}) %collective-permute-start.81) | collective-permute-done | bytes 32800 | tf_op jit(solution)/shard_map/ppermute | solution.py:447
  19.3 0.1 turn.1
  19.4 9.3 %conditional.1 = (f32[2,216,128]{2,1,0:T(8,128)S(1)}, f32[2,216,128]{2,1,0:T(8,128)S(1)}, f32[2,216,128]{2,1,0:T(8,128)S(1)}, f32[2,9,216,128]{3,2,1,0:T(8,128)S...) conditional(s32[]{:T(128)} %bitcast, (f32[3,160,128]{2,1,0:T(8,128)S(1)}, ...), branch_computations={%region_0.0_spmd, %region_1.0_spmd, %region_2.0_spmd, %region_3.0_... | conditional | flops 4008192 | bytes 491688 | solution.py:491
  19.4 6.1 %collective-permute-start.5 = (f32[64,128]{1,0:T(8,128)S(1)}, f32[64,128]{1,0:T(8,128)S(1)}, u32[]{:S(2)}, u32[]{:S(2)}) collective-permute-start(f32[64,128]{1,0:T(8,128)S(1)} %get-tuple-element.382), channel_id=1, source_target_pairs={{32,64},{33,65},{34,66},{35,67},{36,68},{37,69},{38,70},{39,71},{4... | collective-permute-start | bytes 98312 | tf_op jit(solution)/shard_map/cond/branch_2_fun/ppermute | solution.py:467
  25.5 1.9 %collective-permute-start.6 = (f32[64,128]{1,0:T(8,128)S(1)}, f32[64,128]{1,0:T(8,128)S(1)}, u32[]{:S(2)}, u32[]{:S(2)}) collective-permute-start(f32[64,128]{1,0:T(8,128)S(1)} %get-tuple-element.383), channel_id=1, source_target_pairs={{0,32},{64,96},{128,160},{192,224},{256,288},{320,352},{384,416},{... | collective-permute-start | bytes 98312 | tf_op jit(solution)/shard_map/cond/branch_2_fun/ppermute | solution.py:475
  27.4 1.2 %prepare.34 = (f32[2,216,128]{2,1,0:T(8,128)S(1)}, f32[2,216,128]{2,1,0:T(8,128)S(1)}, f32[2,216,128]{2,1,0:T(8,128)S(1)}, f32[2,9,216,128]{3,2,1,0:T(8,128)S(1)}) custom-call(f32[3,160,128]{2,1,0:T(8,128)S(1)} %get-tuple-element.375.x_ref, f32[64,128]{1,0:T(8,128)S(1)} %get-tuple-element.376.second_ref, f32[64,128]{1,0:T(8,128)S(1)} %get-tuple-element.377.first_ref), custom_call_target="tpu_custom_call" | custom-call | flops 4000000 | tf_op jit(solution)/shard_map/cond/branch_2_fun/prepare/pallas_call | solution.py:476
  28.6 0.0 collective-permute-done.5.two_ref
  28.6 0.0 collective-permute-done.6.one_ref
  28.7 2.7 %basis.1 = (f32[17,216,128]{2,1,0:T(8,128)S(1)}, f32[32,128]{1,0:T(8,128)S(1)}, f32[2,216,128]{2,1,0:T(8,128)S(1)}, f32[2,216,128]{2,1,0:T(8,128)S(1)}, f32[2,9,216,128]{3,2,1,0:T(8,128)S(1)}) custom-call(f32[3,160,128]{2,1,0:T(8,128)S(1)} %get-tuple-element.738.x_ref, ...), custom_call_target="tpu_custom_call", output_to_operand_aliasing={{2}: (2, {}), {3}: (3, {}), {4}: (4, {})} | custom-call | tf_op jit(solution)/shard_map/basis/pallas_call | solution.py:495
  31.4 11.6 %all_to_all.22 = f32[32,1,128]{2,1,0:T(1,128)S(1)} all-to-all(f32[32,1,128]{2,1,0:T(1,128)S(1)} %bitcast.12), channel_id=1, replica_groups=mesh['lat'=16,'lon_0'=8,'lon_1'=4] {'lon_0','lon_1'}, dimensions={0} | all-to-all | bytes 32768 | tf_op jit(solution)/shard_map/all_to_all | solution.py:506
  43.0 15.3 %all_to_all.23 = f32[16,1,128]{2,1,0:T(1,128)S(1)} all-to-all(f32[16,1,128]{2,1,0:T(1,128)S(1)} %bitcast.11), channel_id=1, replica_groups=mesh['lat'=16,'lon_0'=8,'lon_1'=4] {'lat'}, dimensions={0} | all-to-all | bytes 16384 | tf_op jit(solution)/shard_map/all_to_all | solution.py:508
  58.3 1.3 %final.1 = (f32[160,128]{1,0:T(8,128)}, f32[160,128]{1,0:T(8,128)}) custom-call(f32[16,128]{1,0:T(8,128)S(1)} %bitcast.10, f32[17,216,128]{2,1,0:T(8,128)S(1)} %get-tuple-element.753.basis_ref), custom_call_target="tpu_custom_call" | custom-call | tf_op jit(solution)/shard_map/final/pallas_call | solution.py:509
  (2 shorter events, 0.0 us)
Async XLA Ops:
  1.8 16.2 %collective-permute-start.80 = (f32[64,128]{1,0:T(8,128)S(1)}, f32[64,128]{1,0:T(8,128)S(1)}, u32[]{:S(2)}, u32[]{:S(2)}) collective-permute-start(f32[64,128]{1,0:T(8,128)S(1)} %get-tuple-element.740), channel_id=1, source_target_pairs={{1,2},{2,1},{3,4},{4,3},{5,6},{6,5},{7,8},{8,7},{9,10},{10,9},{11,... | collective-permute-start | bytes 98312 | tf_op jit(solution)/shard_map/ppermute | solution.py:446
  5.8 13.5 %collective-permute-start.81 = (f32[64,128]{1,0:T(8,128)S(1)}, f32[64,128]{1,0:T(8,128)S(1)}, u32[]{:S(2)}, u32[]{:S(2)}) collective-permute-start(f32[64,128]{1,0:T(8,128)S(1)} %get-tuple-element.741), channel_id=1, source_target_pairs={{0,1},{1,0},{2,3},{3,2},{4,5},{5,4},{6,7},{7,6},{8,9},{9,8},{10,11... | collective-permute-start | bytes 98312 | tf_op jit(solution)/shard_map/ppermute | solution.py:447
  19.4 9.2 %collective-permute-start.5 = (f32[64,128]{1,0:T(8,128)S(1)}, f32[64,128]{1,0:T(8,128)S(1)}, u32[]{:S(2)}, u32[]{:S(2)}) collective-permute-start(f32[64,128]{1,0:T(8,128)S(1)} %get-tuple-element.382), channel_id=1, source_target_pairs={{32,64},{33,65},{34,66},{35,67},{36,68},{37,69},{38,70},{39,71},{4... | collective-permute-start | bytes 98312 | tf_op jit(solution)/shard_map/cond/branch_2_fun/ppermute | solution.py:467
  25.5 3.2 %collective-permute-start.6 = (f32[64,128]{1,0:T(8,128)S(1)}, f32[64,128]{1,0:T(8,128)S(1)}, u32[]{:S(2)}, u32[]{:S(2)}) collective-permute-start(f32[64,128]{1,0:T(8,128)S(1)} %get-tuple-element.383), channel_id=1, source_target_pairs={{0,32},{64,96},{128,160},{192,224},{256,288},{320,352},{384,416},{... | collective-permute-start | bytes 98312 | tf_op jit(solution)/shard_map/cond/branch_2_fun/ppermute | solution.py:475

commit v10 on v9

--- a/solution.py
+++ b/solution.py
@@ -494,7 +494,7 @@
 
     basis, sums, *_ = call(
         basis_kernel, name="basis",
-        out_shape=(shape(VECTORS, PITCH, LANES), shape(lon_count, LANES), shape(2, PITCH, LANES),
+        out_shape=(shape(VECTORS, PITCH, LANES), shape(lat_count, LANES), shape(2, PITCH, LANES),
                    shape(2, PITCH, LANES), shape(2, 9, PITCH, LANES)),
         scratch_shapes=[
             pltpu.VMEM((VECTORS, PITCH, LANES), F32),
@@ -503,9 +503,9 @@
         input_output_aliases={2: 2, 3: 3, 4: 4},
         compiler_params=limit(12),
     )(*held(fields, side, depth, inv, coef, south, north))
+    sums = lax.all_to_all(sums, "lat", split_axis=0, concat_axis=0, tiled=True)
+    sums = call(middle_kernel, name="middle", out_shape=shape(lon_count, LANES), compiler_params=limit(2))(*held(sums))
     sums = lax.all_to_all(sums, LON, split_axis=0, concat_axis=0, tiled=True)
-    sums = call(middle_kernel, name="middle", out_shape=shape(lat_count, LANES), compiler_params=limit(2))(*held(sums))
-    sums = lax.all_to_all(sums, "lat", split_axis=0, concat_axis=0, tiled=True)
     return call(
         final_kernel, name="final", out_shape=(jax.ShapeDtypeStruct((ROWS, LANES), F32),) * 2,
         out_specs=[pl.BlockSpec(memory_space=pl.ANY)] * 2,

time: 60 us -> 59.7 us (level)
    all_to_all x1, blocking collectives: 11.6 us -> 13 us  [per_device(): sums = lax.all_to_all(sums, LON, split_axis=0, concat_axis=0, tiled=True)]
    all_to_all x1, blocking collectives: 15.3 us -> 14.1 us  [per_device(): sums = lax.all_to_all(sums, 'lat', split_axis=0, concat_axis=0, tiled=True)]
where the time goes in v10:
time: 59.7 us; the launch traced here: 59.8 us
  blocking collectives  27.1 us (45%)
  starting transfers between devices  24.2 us (41%)
  Pallas kernels  6.5 us (11%)
  waiting for transfers between devices  1.28 us (2%)
  between operations  0.68 us (1%)
    all_to_all x1, blocking collectives, per_device(): sums = lax.all_to_all(sums, 'lat', split_axis=0, concat_axis=0, tiled=True)  14.1 us
    all_to_all x1, blocking collectives, per_device(): sums = lax.all_to_all(sums, LON, split_axis=0, concat_axis=0, tiled=True)  13 us
    ppermute x1, starting transfers between devices, per_device(): first = lax.ppermute(first, ('lat',) + LON, lon_round(0))  12.2 us
    ppermute x1, starting transfers between devices, second_round(): return lax.ppermute(value, ('lat',) + LON, others + fold)  6.1 us
    ppermute x1, starting transfers between devices, per_device(): second = lax.ppermute(second, ('lat',) + LON, lon_round(1))  3.94 us
    pallas_call x1, Pallas kernels, per_device(): call(basis_kernel, name='basis', out_shape=(shape(VECTORS, PITCH, LANES),...  2.71 us
    ppermute x1, starting transfers between devices, exchange(): one = lax.ppermute(one, 'lat', pairs)  1.92 us
    ppermute x1, waiting for transfers between devices, per_device(): first = lax.ppermute(first, ('lat',) + LON, lon_round(0))  1.27 us
  transfers between devices with their start and end apart: 4, of which 1 were waited for; matrix products, arithmetic and copies ran while one was open for 0% of the time, Pallas kernels for 2%

profile of v10, /device:TPU:1, one launch (start us, length us, event | category | flops | bytes accessed | tf_op | source)
XLA Modules:
  0.0 59.8 jit_solution(1718388908764416493)
XLA Ops:
  0.6 1.2 %pack.1 = (f32[3,160,128]{2,1,0:T(8,128)S(1)}, f32[64,128]{1,0:T(8,128)S(1)}, f32[64,128]{1,0:T(8,128)S(1)}, s32[1]{0:T(128)S(4)}, s32[1]{0:T(128)S(4)}) custom-call(f32[160,128]{1,0:T(8,128)} %f_hbm.1, f32[160,128]{1,0:T(8,128)} %p_hbm.1, f32[160,128]{1,0:T(8,128)} %d_hbm.1, s32[160,128]{1,0:T(8,128)} %m_hbm.1, s32[4096]{0:T(1024)} %map_hbm.1), custom_call_target="tpu_custom_call" | custom-call | tf_op jit(solution)/shard_map/pack/pallas_call | solution.py:427
  1.8 3.9 %collective-permute-start.80 = (f32[64,128]{1,0:T(8,128)S(1)}, f32[64,128]{1,0:T(8,128)S(1)}, u32[]{:S(2)}, u32[]{:S(2)}) collective-permute-start(f32[64,128]{1,0:T(8,128)S(1)} %get-tuple-element.740), channel_id=1, source_target_pairs={{1,2},{2,1},{3,4},{4,3},{5,6},{6,5},{7,8},{8,7},{9,10},{10,9},{11,... | collective-permute-start | bytes 98312 | tf_op jit(solution)/shard_map/ppermute | solution.py:446
  5.8 12.2 %collective-permute-start.81 = (f32[64,128]{1,0:T(8,128)S(1)}, f32[64,128]{1,0:T(8,128)S(1)}, u32[]{:S(2)}, u32[]{:S(2)}) collective-permute-start(f32[64,128]{1,0:T(8,128)S(1)} %get-tuple-element.741), channel_id=1, source_target_pairs={{0,1},{1,0},{2,3},{3,2},{4,5},{5,4},{6,7},{7,6},{8,9},{9,8},{10,11... | collective-permute-start | bytes 98312 | tf_op jit(solution)/shard_map/ppermute | solution.py:447
  18.0 0.0 collective-permute-done.80.second_ref
  18.0 1.3 %collective-permute-done.81.first_ref = f32[64,128]{1,0:T(8,128)S(1)} collective-permute-done((f32[64,128]{1,0:T(8,128)S(1)}, f32[64,128]{1,0:T(8,128)S(1)}, u32[]{:S(2)}, u32[]{:S(2)}) %collective-permute-start.81) | collective-permute-done | bytes 32800 | tf_op jit(solution)/shard_map/ppermute | solution.py:447
  19.3 0.1 turn.1
  19.4 9.3 %conditional.1 = (f32[2,216,128]{2,1,0:T(8,128)S(1)}, f32[2,216,128]{2,1,0:T(8,128)S(1)}, f32[2,216,128]{2,1,0:T(8,128)S(1)}, f32[2,9,216,128]{3,2,1,0:T(8,128)S...) conditional(s32[]{:T(128)} %bitcast, (f32[3,160,128]{2,1,0:T(8,128)S(1)}, ...), branch_computations={%region_0.0_spmd, %region_1.0_spmd, %region_2.0_spmd, %region_3.0_... | conditional | flops 4008192 | bytes 491688 | solution.py:491
  19.4 6.1 %collective-permute-start.70 = (f32[64,128]{1,0:T(8,128)S(1)}, f32[64,128]{1,0:T(8,128)S(1)}, u32[]{:S(2)}, u32[]{:S(2)}) collective-permute-start(f32[64,128]{1,0:T(8,128)S(1)} %get-tuple-element.681), channel_id=1, source_target_pairs={{32,64},{33,65},{34,66},{35,67},{36,68},{37,69},{38,70},{39,71},{4... | collective-permute-start | bytes 98312 | tf_op jit(solution)/shard_map/cond/branch_28_fun/ppermute | solution.py:467
  25.5 1.9 %collective-permute-start.71 = (f32[64,128]{1,0:T(8,128)S(1)}, f32[64,128]{1,0:T(8,128)S(1)}, u32[]{:S(2)}, u32[]{:S(2)}) collective-permute-start(f32[64,128]{1,0:T(8,128)S(1)} %get-tuple-element.682), channel_id=1, source_target_pairs={{0,32},{64,96},{128,160},{192,224},{256,288},{320,352},{384,416},{... | collective-permute-start | bytes 98312 | tf_op jit(solution)/shard_map/cond/branch_28_fun/ppermute | solution.py:475
  27.4 1.2 %prepare.60 = (f32[2,216,128]{2,1,0:T(8,128)S(1)}, f32[2,216,128]{2,1,0:T(8,128)S(1)}, f32[2,216,128]{2,1,0:T(8,128)S(1)}, f32[2,9,216,128]{3,2,1,0:T(8,128)S(1)}) custom-call(f32[3,160,128]{2,1,0:T(8,128)S(1)} %get-tuple-element.674.x_ref, f32[64,128]{1,0:T(8,128)S(1)} %get-tuple-element.675.second_ref, f32[64,128]{1,0:T(8,128)S(1)} %get-tuple-element.676.first_ref), custom_call_target="tpu_custom_call" | custom-call | flops 4000000 | tf_op jit(solution)/shard_map/cond/branch_28_fun/prepare/pallas_call | solution.py:476
  28.6 0.0 collective-permute-done.70.two_ref
  28.6 0.0 collective-permute-done.71.one_ref
  28.7 2.7 %basis.1 = (f32[17,216,128]{2,1,0:T(8,128)S(1)}, f32[16,128]{1,0:T(8,128)S(1)}, f32[2,216,128]{2,1,0:T(8,128)S(1)}, f32[2,216,128]{2,1,0:T(8,128)S(1)}, f32[2,9,216,128]{3,2,1,0:T(8,128)S(1)}) custom-call(f32[3,160,128]{2,1,0:T(8,128)S(1)} %get-tuple-element.738.x_ref, ...), custom_call_target="tpu_custom_call", output_to_operand_aliasing={{2}: (2, {}), {3}: (3, {}), {4}: (4, {})} | custom-call | tf_op jit(solution)/shard_map/basis/pallas_call | solution.py:495
  31.4 14.1 %all_to_all.22 = f32[16,1,128]{2,1,0:T(1,128)S(1)} all-to-all(f32[16,1,128]{2,1,0:T(1,128)S(1)} %bitcast.12), channel_id=1, replica_groups=mesh['lat'=16,'lon_0'=8,'lon_1'=4] {'lat'}, dimensions={0} | all-to-all | bytes 16384 | tf_op jit(solution)/shard_map/all_to_all | solution.py:506
  45.5 13.0 %all_to_all.23 = f32[32,1,128]{2,1,0:T(1,128)S(1)} all-to-all(f32[32,1,128]{2,1,0:T(1,128)S(1)} %bitcast.9), channel_id=1, replica_groups=mesh['lat'=16,'lon_0'=8,'lon_1'=4] {'lon_0','lon_1'}, dimensions={0} | all-to-all | bytes 32768 | tf_op jit(solution)/shard_map/all_to_all | solution.py:508
  58.5 1.3 %final.1 = (f32[160,128]{1,0:T(8,128)}, f32[160,128]{1,0:T(8,128)}) custom-call(f32[32,128]{1,0:T(8,128)S(1)} %bitcast.10, f32[17,216,128]{2,1,0:T(8,128)S(1)} %get-tuple-element.753.basis_ref), custom_call_target="tpu_custom_call" | custom-call | tf_op jit(solution)/shard_map/final/pallas_call | solution.py:509
  (2 shorter events, 0.0 us)
Async XLA Ops:
  1.8 16.2 %collective-permute-start.80 = (f32[64,128]{1,0:T(8,128)S(1)}, f32[64,128]{1,0:T(8,128)S(1)}, u32[]{:S(2)}, u32[]{:S(2)}) collective-permute-start(f32[64,128]{1,0:T(8,128)S(1)} %get-tuple-element.740), channel_id=1, source_target_pairs={{1,2},{2,1},{3,4},{4,3},{5,6},{6,5},{7,8},{8,7},{9,10},{10,9},{11,... | collective-permute-start | bytes 98312 | tf_op jit(solution)/shard_map/ppermute | solution.py:446
  5.8 13.5 %collective-permute-start.81 = (f32[64,128]{1,0:T(8,128)S(1)}, f32[64,128]{1,0:T(8,128)S(1)}, u32[]{:S(2)}, u32[]{:S(2)}) collective-permute-start(f32[64,128]{1,0:T(8,128)S(1)} %get-tuple-element.741), channel_id=1, source_target_pairs={{0,1},{1,0},{2,3},{3,2},{4,5},{5,4},{6,7},{7,6},{8,9},{9,8},{10,11... | collective-permute-start | bytes 98312 | tf_op jit(solution)/shard_map/ppermute | solution.py:447
  19.4 9.3 %collective-permute-start.70 = (f32[64,128]{1,0:T(8,128)S(1)}, f32[64,128]{1,0:T(8,128)S(1)}, u32[]{:S(2)}, u32[]{:S(2)}) collective-permute-start(f32[64,128]{1,0:T(8,128)S(1)} %get-tuple-element.681), channel_id=1, source_target_pairs={{32,64},{33,65},{34,66},{35,67},{36,68},{37,69},{38,70},{39,71},{4... | collective-permute-start | bytes 98312 | tf_op jit(solution)/shard_map/cond/branch_28_fun/ppermute | solution.py:467
  25.5 3.2 %collective-permute-start.71 = (f32[64,128]{1,0:T(8,128)S(1)}, f32[64,128]{1,0:T(8,128)S(1)}, u32[]{:S(2)}, u32[]{:S(2)}) collective-permute-start(f32[64,128]{1,0:T(8,128)S(1)} %get-tuple-element.682), channel_id=1, source_target_pairs={{0,32},{64,96},{128,160},{192,224},{256,288},{320,352},{384,416},{... | collective-permute-start | bytes 98312 | tf_op jit(solution)/shard_map/cond/branch_28_fun/ppermute | solution.py:475

commit v11 on v10

--- a/solution.py
+++ b/solution.py
@@ -294,17 +294,19 @@
     def weights_at(at):
         return [[None if i == 1 else coef[t, i, pl.ds(at, 8), :] for i in range(9)] for t in range(2)]
 
-    def step(k, first, last):
+    def step(k, first, last, trim=False):
         total = [zero] * 6
         tiles = 1 if last else 2
         for g in range(1, GROUPS - 1) if last else range(GROUPS):
             at = 8 + 8 * g
             w = weights_at(at)
             now, new = [], []
-            for base in ((0,) if last else (0, STEPS + 1)):
-                out, here = twice_applied(base + k, at, tiles, w)
+            inner = 1 <= g <= ROWS // 8
+            for base in ((0,) if last or (trim and not inner) else (0, STEPS + 1)):
+                count = 1 if trim and base else tiles
+                out, here = twice_applied(base + k, at, count, w)
                 now.append(here)
-                for t in range(tiles):
+                for t in range(count):
                     ref = basis_ref if t == 0 else side
                     value = 0.5 * out[t] if first else out[t] - ref[base + k - 1, pl.ds(at, 8), :]
                     ref[base + k + 1, pl.ds(at, 8), :] = value
@@ -312,7 +314,7 @@
                         new.append(value)
             if last:
                 now.append(basis_ref[STEPS + 1 + k, pl.ds(at, 8), :])
-            if 1 <= g <= ROWS // 8:
+            if inner:
                 p, r = now
                 total[0] += p * p
                 total[1] += p * new[0]
@@ -329,7 +331,8 @@
         step(k, False, False)
         return carry
 
-    lax.fori_loop(1, STEPS - 1, middle, 0, unroll=2)
+    lax.fori_loop(1, STEPS - 2, middle, 0, unroll=5)
+    step(STEPS - 2, False, False, True)
     step(STEPS - 1, False, True)
 
     flat = jnp.sum(acc[...], axis=1)

time: 59.7 us -> 59.5 us (level)
  no operation moved by 1% of the time
where the time goes in v11:
time: 59.5 us; the launch traced here: 59.6 us
  blocking collectives  27.1 us (46%)
  starting transfers between devices  24.2 us (41%)
  Pallas kernels  5.96 us (10%)
  waiting for transfers between devices  1.28 us (2%)
  between operations  0.84 us (1%)
    all_to_all x1, blocking collectives, per_device(): sums = lax.all_to_all(sums, 'lat', split_axis=0, concat_axis=0, tiled=True)  14.1 us
    all_to_all x1, blocking collectives, per_device(): sums = lax.all_to_all(sums, LON, split_axis=0, concat_axis=0, tiled=True)  13 us
    ppermute x1, starting transfers between devices, per_device(): first = lax.ppermute(first, ('lat',) + LON, lon_round(0))  12.2 us
    ppermute x1, starting transfers between devices, second_round(): return lax.ppermute(value, ('lat',) + LON, others + fold)  6.1 us
    ppermute x1, starting transfers between devices, per_device(): second = lax.ppermute(second, ('lat',) + LON, lon_round(1))  3.94 us
    pallas_call x1, Pallas kernels, per_device(): call(basis_kernel, name='basis', out_shape=(shape(VECTORS, PITCH, LANES),...  2.17 us
    ppermute x1, starting transfers between devices, exchange(): one = lax.ppermute(one, 'lat', pairs)  1.92 us
    ppermute x1, waiting for transfers between devices, per_device(): first = lax.ppermute(first, ('lat',) + LON, lon_round(0))  1.27 us
  transfers between devices with their start and end apart: 4, of which 1 were waited for; matrix products, arithmetic and copies ran while one was open for 0% of the time, Pallas kernels for 2%

profile of v11, /device:TPU:1, one launch (start us, length us, event | category | flops | bytes accessed | tf_op | source)
XLA Modules:
  0.0 59.6 jit_solution(5421681436084250937)
XLA Ops:
  0.6 1.2 %pack.1 = (f32[3,160,128]{2,1,0:T(8,128)S(1)}, f32[64,128]{1,0:T(8,128)S(1)}, f32[64,128]{1,0:T(8,128)S(1)}, s32[1]{0:T(128)S(4)}, s32[1]{0:T(128)S(4)}) custom-call(f32[160,128]{1,0:T(8,128)} %f_hbm.1, f32[160,128]{1,0:T(8,128)} %p_hbm.1, f32[160,128]{1,0:T(8,128)} %d_hbm.1, s32[160,128]{1,0:T(8,128)} %m_hbm.1, s32[4096]{0:T(1024)} %map_hbm.1), custom_call_target="tpu_custom_call" | custom-call | tf_op jit(solution)/shard_map/pack/pallas_call | solution.py:430
  1.8 3.9 %collective-permute-start.80 = (f32[64,128]{1,0:T(8,128)S(1)}, f32[64,128]{1,0:T(8,128)S(1)}, u32[]{:S(2)}, u32[]{:S(2)}) collective-permute-start(f32[64,128]{1,0:T(8,128)S(1)} %get-tuple-element.740), channel_id=1, source_target_pairs={{1,2},{2,1},{3,4},{4,3},{5,6},{6,5},{7,8},{8,7},{9,10},{10,9},{11,... | collective-permute-start | bytes 98312 | tf_op jit(solution)/shard_map/ppermute | solution.py:449
  5.8 12.2 %collective-permute-start.81 = (f32[64,128]{1,0:T(8,128)S(1)}, f32[64,128]{1,0:T(8,128)S(1)}, u32[]{:S(2)}, u32[]{:S(2)}) collective-permute-start(f32[64,128]{1,0:T(8,128)S(1)} %get-tuple-element.741), channel_id=1, source_target_pairs={{0,1},{1,0},{2,3},{3,2},{4,5},{5,4},{6,7},{7,6},{8,9},{9,8},{10,11... | collective-permute-start | bytes 98312 | tf_op jit(solution)/shard_map/ppermute | solution.py:450
  18.0 0.0 collective-permute-done.80.second_ref
  18.0 1.3 %collective-permute-done.81.first_ref = f32[64,128]{1,0:T(8,128)S(1)} collective-permute-done((f32[64,128]{1,0:T(8,128)S(1)}, f32[64,128]{1,0:T(8,128)S(1)}, u32[]{:S(2)}, u32[]{:S(2)}) %collective-permute-start.81) | collective-permute-done | bytes 32800 | tf_op jit(solution)/shard_map/ppermute | solution.py:450
  19.3 0.1 turn.1
  19.4 9.5 %conditional.1 = (f32[2,216,128]{2,1,0:T(8,128)S(1)}, f32[2,216,128]{2,1,0:T(8,128)S(1)}, f32[2,216,128]{2,1,0:T(8,128)S(1)}, f32[2,9,216,128]{3,2,1,0:T(8,128)S...) conditional(s32[]{:T(128)} %bitcast, (f32[3,160,128]{2,1,0:T(8,128)S(1)}, ...), branch_computations={%region_0.0_spmd, %region_1.0_spmd, %region_2.0_spmd, %region_3.0_... | conditional | flops 4008192 | bytes 491688 | solution.py:494
  19.4 6.1 %collective-permute-start.50 = (f32[64,128]{1,0:T(8,128)S(1)}, f32[64,128]{1,0:T(8,128)S(1)}, u32[]{:S(2)}, u32[]{:S(2)}) collective-permute-start(f32[64,128]{1,0:T(8,128)S(1)} %get-tuple-element.589), channel_id=1, source_target_pairs={{32,64},{33,65},{34,66},{35,67},{36,68},{37,69},{38,70},{39,71},{4... | collective-permute-start | bytes 98312 | tf_op jit(solution)/shard_map/cond/branch_20_fun/ppermute | solution.py:470
  25.5 1.9 %collective-permute-start.51 = (f32[64,128]{1,0:T(8,128)S(1)}, f32[64,128]{1,0:T(8,128)S(1)}, u32[]{:S(2)}, u32[]{:S(2)}) collective-permute-start(f32[64,128]{1,0:T(8,128)S(1)} %get-tuple-element.590), channel_id=1, source_target_pairs={{0,32},{64,96},{128,160},{192,224},{256,288},{320,352},{384,416},{... | collective-permute-start | bytes 98312 | tf_op jit(solution)/shard_map/cond/branch_20_fun/ppermute | solution.py:478
  27.4 1.2 %prepare.52 = (f32[2,216,128]{2,1,0:T(8,128)S(1)}, f32[2,216,128]{2,1,0:T(8,128)S(1)}, f32[2,216,128]{2,1,0:T(8,128)S(1)}, f32[2,9,216,128]{3,2,1,0:T(8,128)S(1)}) custom-call(f32[3,160,128]{2,1,0:T(8,128)S(1)} %get-tuple-element.582.x_ref, f32[64,128]{1,0:T(8,128)S(1)} %get-tuple-element.583.second_ref, f32[64,128]{1,0:T(8,128)S(1)} %get-tuple-element.584.first_ref), custom_call_target="tpu_custom_call" | custom-call | flops 4000000 | tf_op jit(solution)/shard_map/cond/branch_20_fun/prepare/pallas_call | solution.py:479
  28.6 0.0 collective-permute-done.50.two_ref
  28.6 0.0 collective-permute-done.51.one_ref
  28.9 2.2 %basis.1 = (f32[17,216,128]{2,1,0:T(8,128)S(1)}, f32[16,128]{1,0:T(8,128)S(1)}, f32[2,216,128]{2,1,0:T(8,128)S(1)}, f32[2,216,128]{2,1,0:T(8,128)S(1)}, f32[2,9,216,128]{3,2,1,0:T(8,128)S(1)}) custom-call(f32[3,160,128]{2,1,0:T(8,128)S(1)} %get-tuple-element.738.x_ref, ...), custom_call_target="tpu_custom_call", output_to_operand_aliasing={{2}: (2, {}), {3}: (3, {}), {4}: (4, {})} | custom-call | tf_op jit(solution)/shard_map/basis/pallas_call | solution.py:498
  31.0 14.1 %all_to_all.22 = f32[16,1,128]{2,1,0:T(1,128)S(1)} all-to-all(f32[16,1,128]{2,1,0:T(1,128)S(1)} %bitcast.12), channel_id=1, replica_groups=mesh['lat'=16,'lon_0'=8,'lon_1'=4] {'lat'}, dimensions={0} | all-to-all | bytes 16384 | tf_op jit(solution)/shard_map/all_to_all | solution.py:509
  45.2 13.0 %all_to_all.23 = f32[32,1,128]{2,1,0:T(1,128)S(1)} all-to-all(f32[32,1,128]{2,1,0:T(1,128)S(1)} %bitcast.9), channel_id=1, replica_groups=mesh['lat'=16,'lon_0'=8,'lon_1'=4] {'lon_0','lon_1'}, dimensions={0} | all-to-all | bytes 32768 | tf_op jit(solution)/shard_map/all_to_all | solution.py:511
  58.2 1.3 %final.1 = (f32[160,128]{1,0:T(8,128)}, f32[160,128]{1,0:T(8,128)}) custom-call(f32[32,128]{1,0:T(8,128)S(1)} %bitcast.10, f32[17,216,128]{2,1,0:T(8,128)S(1)} %get-tuple-element.753.basis_ref), custom_call_target="tpu_custom_call" | custom-call | tf_op jit(solution)/shard_map/final/pallas_call | solution.py:512
  (2 shorter events, 0.0 us)
Async XLA Ops:
  1.8 16.2 %collective-permute-start.80 = (f32[64,128]{1,0:T(8,128)S(1)}, f32[64,128]{1,0:T(8,128)S(1)}, u32[]{:S(2)}, u32[]{:S(2)}) collective-permute-start(f32[64,128]{1,0:T(8,128)S(1)} %get-tuple-element.740), channel_id=1, source_target_pairs={{1,2},{2,1},{3,4},{4,3},{5,6},{6,5},{7,8},{8,7},{9,10},{10,9},{11,... | collective-permute-start | bytes 98312 | tf_op jit(solution)/shard_map/ppermute | solution.py:449
  5.8 13.5 %collective-permute-start.81 = (f32[64,128]{1,0:T(8,128)S(1)}, f32[64,128]{1,0:T(8,128)S(1)}, u32[]{:S(2)}, u32[]{:S(2)}) collective-permute-start(f32[64,128]{1,0:T(8,128)S(1)} %get-tuple-element.741), channel_id=1, source_target_pairs={{0,1},{1,0},{2,3},{3,2},{4,5},{5,4},{6,7},{7,6},{8,9},{9,8},{10,11... | collective-permute-start | bytes 98312 | tf_op jit(solution)/shard_map/ppermute | solution.py:450
  19.4 9.3 %collective-permute-start.50 = (f32[64,128]{1,0:T(8,128)S(1)}, f32[64,128]{1,0:T(8,128)S(1)}, u32[]{:S(2)}, u32[]{:S(2)}) collective-permute-start(f32[64,128]{1,0:T(8,128)S(1)} %get-tuple-element.589), channel_id=1, source_target_pairs={{32,64},{33,65},{34,66},{35,67},{36,68},{37,69},{38,70},{39,71},{4... | collective-permute-start | bytes 98312 | tf_op jit(solution)/shard_map/cond/branch_20_fun/ppermute | solution.py:470
  25.5 3.2 %collective-permute-start.51 = (f32[64,128]{1,0:T(8,128)S(1)}, f32[64,128]{1,0:T(8,128)S(1)}, u32[]{:S(2)}, u32[]{:S(2)}) collective-permute-start(f32[64,128]{1,0:T(8,128)S(1)} %get-tuple-element.590), channel_id=1, source_target_pairs={{0,32},{64,96},{128,160},{192,224},{256,288},{320,352},{384,416},{... | collective-permute-start | bytes 98312 | tf_op jit(solution)/shard_map/cond/branch_20_fun/ppermute | solution.py:478
